TPU v7x, 512 devices: a whole 4x8x8 slice. The times are simulated.
512 devices in a mesh: rep: 16 (over z_lo, x, core), shard: 32 (over y, z_hi).
Axes of the slice: x: 4, y: 8, z: 8 (z_hi: 4, z_lo: 2; z = z_hi * 2 + z_lo), core: 2. Of those that a mesh axis runs over, the one named last changes fastest.
Arguments:
- features: bfloat16 [1, 16, 4096, 8192], P(None, 'rep', 'shard'), may hold values from -6 to 6
- out_grads: bfloat16 [1, 16, 4096, 1024], P(None, 'rep', 'shard'), may hold values from -6 to 6
- doc_ids: int32 [1, 16, 4096], P(None, 'rep', 'shard'), may hold values from 0 to 15, never falling along the last dimension, each value on 1 to 512 neighbouring positions
- offsets: int32 [1, 16, 128], P(None, None, 'shard'), may hold values from 0 to 15
- momentum: bfloat16 [16, 1024, 8192], P('rep', None, 'shard'), may hold values from -6 to 6
Outputs:
- residual_momentum: bfloat16 [16, 1024, 8192], P('rep', None, 'shard')
- update: bfloat16 [1, 1024, 8192], P(None, None, 'shard')
Inputs may be any that keep to these rules, and one draw needn't show every extreme that they name: `doc_ids`: along each step's and group's tokens the document number never falls; every number from 0 to 15 occurs, none more than 512 times.
All inputs are finite; a program needn't handle non-finite values.
Results may differ from a plain program's by a relative error of at most 0.012.
Values may be sent and summed in bfloat16 or wider, within the bound.
No kernel may reach another device: no remote copies, remote signals or barrier semaphores. Data moves between devices by JAX's collectives and lax.ppermute only.
A program may use at most 64 MiB of HBM per device.

v0:
```python
import functools
import math

import jax
import jax.numpy as jnp
import numpy as np
from jax import lax
from jax.experimental import pallas as pl
from jax.experimental.pallas import tpu as pltpu
from jax.sharding import PartitionSpec as P


BLOCK = 64
STRIDE = 16
DOCS = 16
LINES = 8
BETA = 0.9
CLIP = 2.0
EPS = 1e-06


TILE = 256
GRANT = 16 << 20
FULL = 60 << 20


def dct_parts():
    freq = np.arange(BLOCK, dtype=np.float64)[:, None]
    place = np.arange(BLOCK, dtype=np.float64)[None, :]
    table = np.cos(math.pi * (2.0 * place + 1.0) * freq / (2.0 * BLOCK)) * math.sqrt(2.0 / BLOCK)
    table[0] /= math.sqrt(2.0)
    whole = np.kron(np.eye(TILE // BLOCK), table)
    high = whole.astype(jnp.bfloat16)
    low = (whole - high.astype(np.float64)).astype(jnp.bfloat16)
    return jnp.asarray(high), jnp.asarray(low)


def dot(a, b, dims):
    return lax.dot_general(a, b, (dims, ((), ())), preferred_element_type=jnp.float32)


def split(x):
    high = x.astype(jnp.bfloat16)
    return high, (x - high.astype(jnp.float32)).astype(jnp.bfloat16)


def left(table, x, dim):
    (th, tl), (xh, xl) = table, split(x)
    dims = ((dim,), (0,))
    return dot(th, xh, dims) + (dot(th, xl, dims) + dot(tl, xh, dims))


def right(x, table, dim):
    (th, tl), (xh, xl) = table, split(x)
    dims = ((1,), (dim,))
    return dot(xh, th, dims) + (dot(xl, th, dims) + dot(xh, tl, dims))


def selected(offsets):
    count, width = offsets.shape
    shape = (count, BLOCK, width)
    both = lax.broadcasted_iota(jnp.int32, shape, 1) + lax.broadcasted_iota(jnp.int32, shape, 2)
    return ((both & (STRIDE - 1)) == offsets[:, None, :]).reshape(count * BLOCK, width)


def gathered(exchanged, start, size):
    deep = exchanged.shape[0]
    z = lax.axis_index("shard") % deep
    return jnp.concatenate([exchanged[(z - k + deep) % deep, :, start : start + size] for k in range(deep)], axis=0)


def joined(parts, start, size):
    return jnp.concatenate([part[:, start : start + size] for part in parts], axis=0)


def fetch(rows, deep, width, moves, sem):
    me = lax.axis_index("shard")
    line = me // deep
    copies = []
    for i, (owner, z, target) in enumerate(moves):
        block = (line + owner + LINES) % LINES * deep + z
        column = pl.multiple_of(block * width, width)
        copies.append(pltpu.make_async_copy(rows.at[:, pl.ds(column, width)], target, sem.at[i]))
    for copy in copies:
        copy.start()
    return copies


def early_kernel(rows, grads, out, sem):
    deep = out.shape[0]
    panel = grads.shape[1]
    width = out.shape[2] - panel
    moves = [(4, z, out.at[z, :, pl.ds(panel, width)]) for z in range(deep)]
    copies = fetch(rows, deep, width, moves, sem)
    for z in range(deep):
        out[z, :, :panel] = grads[...]
    for copy in copies:
        copy.wait()


def late_kernel(rows, extra, *rest):
    deep = 4
    third, second, last, sem = rest[:deep], rest[deep : 2 * deep], rest[2 * deep], rest[2 * deep + 1]
    width = last.shape[2] // 3
    me = lax.axis_index("shard") % deep
    moves = []
    for k in range(deep):
        z = (me + k) % deep
        for j, owner in enumerate((3, -3)):
            moves.append((owner, z, third[k].at[:, pl.ds(j * width, width)]))
    for k in range(deep):
        z = (me + k) % deep
        for j, owner in enumerate((2, -2)):
            moves.append((owner, z, second[k].at[:, pl.ds(j * width, width)]))
    for z in range(deep):
        for j, owner in enumerate((1, -1, 0)):
            moves.append((owner, z, last.at[z, :, pl.ds(j * width, width)]))
    copies = fetch(rows, deep, width, moves, sem)
    for k in range(deep):
        third[k][:, 2 * width :] = extra[...]
    for copy in copies:
        copy.wait()


def scale_kernel(exchanged, *rest):
    notes, out = rest[:-1], rest[-1]
    deep, tokens = exchanged.shape[0], exchanged.shape[1]
    width = notes[0].shape[1] - 128
    panel = exchanged.shape[2] - width // 2
    z = lax.axis_index("shard") % deep
    marks = [note[:, width:].astype(jnp.float32) for note in notes]
    heads = marks[0][:8]
    for mark in marks[1:]:
        heads = heads + mark[:8]
    lengths = pltpu.roll(heads, 112, 1) + pltpu.roll(heads, 96, 1) + pltpu.roll(heads, 80, 1)
    share = 1.0 / jnp.maximum(lengths[:1], 1.0)
    lane = lax.broadcasted_iota(jnp.int32, (tokens, 128), 1)
    for k in range(deep):
        weight = jnp.sum(jnp.where(lane < DOCS, marks[k] * share, 0.0), axis=1, keepdims=True)
        block = exchanged[(z - k + deep) % deep, :, :panel].astype(jnp.float32)
        out[:, k * tokens : (k + 1) * tokens] = (block * weight).T.astype(jnp.bfloat16)


def far_kernel(weights, exchanged, up, down):
    half = up.shape[0]
    columns = gathered(exchanged, exchanged.shape[2] - up.shape[1], up.shape[1])
    dims = ((1,), (0,))
    up[...] = dot(weights[:half], columns, dims).astype(jnp.bfloat16)
    down[...] = dot(weights[half:], columns, dims).astype(jnp.bfloat16)


def near_kernel(start, top, pieces, weights, received, *rest):
    parts, out = rest[:-1], rest[-1]
    width = out.shape[1]
    columns = joined(parts, start, width) if pieces else gathered(parts[0], start, width)
    total = dot(weights[...], columns, ((1,), (0,)))
    rows = received.shape[0]
    if rows == out.shape[0]:
        out[...] = (total + received[...].astype(jnp.float32)).astype(jnp.bfloat16)
    else:
        here, other = (slice(0, rows), slice(rows, None)) if top else (slice(rows, None), slice(0, rows))
        out[here] = (total[here] + received[...].astype(jnp.float32)).astype(jnp.bfloat16)
        out[other] = total[other].astype(jnp.bfloat16)


def forward_kernel(weights, exchanged, up, down, momentum, offsets, high, low, ones, summed, decoded, sent, packed):
    table = (high[...], low[...])
    per = TILE // BLOCK
    rows = TILE // STRIDE
    width = summed.shape[1]
    columns = gathered(exchanged, 2 * width, width)
    for i in range(summed.shape[0] // TILE):
        here = slice(i * TILE, (i + 1) * TILE)
        total = dot(weights[here], columns, ((1,), (0,)))
        total = total + up[here].astype(jnp.float32) + down[here].astype(jnp.float32)
        gradient = total.astype(jnp.bfloat16)
        summed[here] = gradient
        value = BETA * momentum[here].astype(jnp.float32) + gradient.astype(jnp.float32)
        spectrum = right(left(table, value, 1), table, 1)
        kept = jnp.where(selected(offsets[i * per : (i + 1) * per]), spectrum, 0.0)
        packed[i * rows : (i + 1) * rows] = jnp.sum(kept.reshape(rows, STRIDE, TILE), axis=1)
    values = packed[...]
    group = BLOCK // STRIDE
    squares = jnp.sum((values * values).reshape(-1, group, TILE), axis=1)
    first = squares.astype(jnp.bfloat16)
    rest = squares - first.astype(jnp.float32)
    second, third = split(rest)
    dims = ((1,), (0,))
    total = dot(first, ones[...], dims) + (dot(second, ones[...], dims) + dot(third, ones[...], dims))
    mean = total * (1.0 / (BLOCK * group))
    scale = (CLIP * jnp.sqrt(mean + EPS)).astype(jnp.bfloat16).astype(jnp.float32)
    spread = jnp.broadcast_to(scale[:, None, :], (scale.shape[0], group, TILE)).reshape(values.shape)
    quantized = jnp.clip(values / spread, -1.0, 1.0).astype(jnp.bfloat16)
    result = quantized.astype(jnp.float32) * spread
    decoded[...] = result
    rounded = result.astype(jnp.bfloat16)
    for k in range(sent.shape[0]):
        sent[k] = rounded


def spread_tile(values, offsets):
    rows, width = values.shape
    wide = jnp.broadcast_to(values[:, None, :], (rows, STRIDE, width)).reshape(rows * STRIDE, width)
    return jnp.where(selected(offsets), wide, 0.0)


def inverse_tile(values, offsets, table):
    return right(left(table, spread_tile(values, offsets), 0), table, 0)


def residual_kernel(momentum, summed, decoded, offsets, high, low, out):
    table = (high[...], low[...])
    per = TILE // BLOCK
    rows = TILE // STRIDE
    for i in range(out.shape[0] // TILE):
        here = slice(i * TILE, (i + 1) * TILE)
        value = BETA * momentum[here].astype(jnp.float32) + summed[here].astype(jnp.float32)
        back = inverse_tile(decoded[i * rows : (i + 1) * rows], offsets[i * per : (i + 1) * per], table)
        out[here] = (value - back).astype(jnp.bfloat16)


def update_kernel(parts, offsets, high, low, out):
    table = (high[...], low[...])
    per = TILE // BLOCK
    rows = TILE // STRIDE
    count = parts.shape[0]
    for i in range(out.shape[0] // TILE):
        here = slice(i * rows, (i + 1) * rows)
        total = parts[0, here].astype(jnp.float32)
        for k in range(1, count):
            total += parts[k, here].astype(jnp.float32)
        back = inverse_tile(total * (1.0 / count), offsets[i * per : (i + 1) * per], table)
        out[i * TILE : (i + 1) * TILE] = back.astype(jnp.bfloat16)


def call(kernel, out_shape, flops, scratch=(), in_specs=None, grant=GRANT):
    extra = {} if in_specs is None else {"in_specs": in_specs}
    return pl.pallas_call(
        kernel,
        out_shape=out_shape,
        scratch_shapes=scratch,
        compiler_params=pltpu.CompilerParams(vmem_limit_bytes=grant),
        cost_estimate=pl.CostEstimate(flops=flops, bytes_accessed=2 << 20, transcendentals=0),
        **extra,
    )


def shaped(*shape, dtype=jnp.bfloat16):
    return jax.ShapeDtypeStruct(shape, dtype)


def step(features, out_grads, doc_ids, offsets, momentum):
    shards = lax.axis_size("shard")
    deep = shards // LINES
    groups = lax.axis_size("rep")

    def along_line(x, k):
        pairs = [(y * deep + z, y * deep + (z + k) % deep) for y in range(LINES) for z in range(deep)]
        return lax.ppermute(x, "shard", pairs)

    def across(x, k):
        pairs = [(y * deep + z, (y + k) % LINES * deep + z) for y in range(LINES) for z in range(deep)]
        return lax.ppermute(x, "shard", pairs)

    def exchange(x):
        lines = [[y * deep + z for z in range(deep)] for y in range(LINES)]
        return lax.all_to_all(x, "shard", 0, 0, axis_index_groups=lines, tiled=True)

    rows = features[0, 0]
    grads = out_grads[0, 0]
    tokens, panel = grads.shape
    width = rows.shape[1] // shards
    whole = pl.BlockSpec(memory_space=pltpu.VMEM)
    apart = pl.BlockSpec(memory_space=pltpu.HBM)
    work = 2 * panel * deep * tokens * width

    early = call(
        early_kernel,
        shaped(deep, tokens, panel + width),
        work,
        (pltpu.SemaphoreType.DMA((deep,)),),
        [apart, whole],
        FULL,
    )(rows, grads)
    early = exchange(early)

    onehot = (doc_ids[0, 0][:, None] == jnp.arange(128, dtype=jnp.int32)[None, :]).astype(jnp.float32)
    counts = jnp.broadcast_to(jnp.sum(onehot, axis=0, keepdims=True), (8, 128))
    before = across(counts, 1)
    after = across(counts, -1)
    lanes = jnp.concatenate([counts[:1, :16], before[:1, :16], after[:1, :16]], axis=1)
    extra = jnp.concatenate(
        [onehot[:, :16], jnp.broadcast_to(lanes, (tokens, 48)), jnp.zeros((tokens, 64), jnp.float32)], axis=1
    ).astype(jnp.bfloat16)

    outs = call(
        late_kernel,
        [shaped(tokens, 2 * width + 128)] * deep + [shaped(tokens, 2 * width)] * deep + [shaped(deep, tokens, 3 * width)],
        work,
        (pltpu.SemaphoreType.DMA((7 * deep,)),),
        [apart, whole],
        FULL,
    )(rows, extra)
    third, second, last = list(outs[:deep]), list(outs[deep : 2 * deep]), outs[2 * deep]
    for k in (2, 1, 3):
        third[k] = along_line(third[k], k)
    for k in (2, 1, 3):
        second[k] = along_line(second[k], k)
    last = exchange(last)

    weights = call(scale_kernel, shaped(panel, deep * tokens), work)(early, *third)
    half = panel // 2
    up, down = call(far_kernel, [shaped(half, width)] * 2, work)(weights, early)

    def ring(up, down):
        up = across(up, 1)
        down = across(down, -1)
        return up, down

    def near(start, top, received, parts):
        kernel = functools.partial(near_kernel, start, top, len(parts) > 1)
        return call(kernel, shaped(panel, width), work)(weights, received, *parts)

    up, down = ring(up, down)
    up, down = ring(near(0, True, up, third), near(width, False, down, third))
    up, down = ring(near(0, True, up, second), near(width, False, down, second))
    up, down = ring(near(0, True, up, [last]), near(width, False, down, [last]))

    high, low = dct_parts()
    ones = jnp.asarray(np.kron(np.eye(TILE // BLOCK), np.ones((BLOCK, BLOCK))), jnp.bfloat16)
    wide = jnp.repeat(offsets[0], BLOCK, axis=1)
    kept = panel // STRIDE
    flops = 6 * 2 * 2 * panel * TILE * TILE
    summed, decoded, sent = call(
        forward_kernel,
        (
            shaped(panel, width),
            shaped(kept, width, dtype=jnp.float32),
            shaped(groups, kept, width),
        ),
        flops,
        (pltpu.VMEM((kept, width), jnp.float32),),
    )(weights, last, up, down, momentum[0], wide, high, low, ones)
    parts = lax.all_to_all(sent, "rep", 0, 0, tiled=True)
    residual = call(residual_kernel, shaped(panel, width), flops)(momentum[0], summed, decoded, wide, high, low)
    update = call(update_kernel, shaped(panel, width), flops)(parts, wide, high, low)
    return residual[None], update[None]


def solution(mesh):
    return jax.shard_map(
        step,
        mesh=mesh,
        in_specs=(
            P(None, "rep", "shard", None),
            P(None, "rep", "shard", None),
            P(None, "rep", "shard"),
            P(None, None, "shard"),
            P("rep", None, "shard"),
        ),
        out_specs=(P("rep", None, "shard"), P(None, None, "shard")),
        check_vma=False,
    )
```

profile of v0, /device:TPU:1, one launch (start us, length us, event | category | flops | bytes accessed | tf_op | source)
XLA Modules:
  0.0 172.1 jit_solution(11265768951299398688)
XLA Ops:
  0.6 3.0 %shard_map.95 = bf16[4,128,1280]{2,1,0:T(8,128)(2,1)} custom-call(bf16[128,8192]{1,0:T(8,128)(2,1)} %bitcast.14, bf16[128,1024]{1,0:T(8,128)(2,1)} %bitcast.16), custom_call_target="tpu_custom_call" | custom-call | flops 268435456 | bytes 2097152 | tf_op jit(solution)/shard_map/pallas_call | solution.py:277
  3.7 10.8 %all-to-all-start = ((bf16[4,128,1280]{2,1,0:T(8,128)(2,1)}), bf16[4,128,1280]{2,1,0:T(8,128)(2,1)S(1)}, u32[]{:S(2)}, u32[]{:S(2)}) async-start(bf16[4,128,1280]{2,1,0:T(8,128)(2,1)} %shard_map.95), calls=%async_computation | async-start | bytes 2621440 | tf_op jit(solution)/shard_map/all_to_all | solution.py:267
  14.6 3.2 %collective-permute-start = (bf16[8,128]{1,0:T(8,128)(2,1)S(1)}, bf16[8,128]{1,0:T(8,128)(2,1)S(1)}, u32[]{:S(2)}, u32[]{:S(2)}) collective-permute-start(bf16[8,128]{1,0:T(8,128)(2,1)S(1)} %broadcast_in_dim.29), channel_id=1, source_target_pairs={{0,4},{1,5},{2,6},{3,7},{4,8},{5,9},{6,10},{7,11},{8,12},{9,13},{1... | collective-permute-start | bytes 6152 | tf_op jit(solution)/shard_map/ppermute | solution.py:263
  17.8 3.8 %collective-permute-start.1 = (bf16[8,128]{1,0:T(8,128)(2,1)S(1)}, bf16[8,128]{1,0:T(8,128)(2,1)S(1)}, u32[]{:S(2)}, u32[]{:S(2)}) collective-permute-start(bf16[8,128]{1,0:T(8,128)(2,1)S(1)} %broadcast_in_dim.29), channel_id=1, source_target_pairs={{0,28},{1,29},{2,30},{3,31},{4,0},{5,1},{6,2},{7,3},{8,4},{9,5},{1... | collective-permute-start | bytes 6152 | tf_op jit(solution)/shard_map/ppermute | solution.py:263
  21.8 0.6 collective-permute-done.1
  22.6 0.6 maximum_maximum_fusion.extra
  23.2 3.8 %shard_map.96 = (bf16[128,640]{1,0:T(8,128)(2,1)}, bf16[128,640]{1,0:T(8,128)(2,1)}, bf16[128,640]{1,0:T(8,128)(2,1)}, bf16[128,640]{1,0:T(8,128)(2,1)}, bf16[12...) custom-call(bf16[128,8192]{1,0:T(8,128)(2,1)} %bitcast.15, ...), custom_call_target="tpu_custom_call" | custom-call | flops 268435456 | bytes 2097152 | tf_op jit(solution)/shard_map/pallas_call | solution.py:296
  27.0 4.3 %collective-permute-start.2 = (bf16[128,640]{1,0:T(8,128)(2,1)}, bf16[128,640]{1,0:T(8,128)(2,1)S(1)}, u32[]{:S(2)}, u32[]{:S(2)}) collective-permute-start(bf16[128,640]{1,0:T(8,128)(2,1)} %get-tuple-element.17), channel_id=1, source_target_pairs={{0,1},{1,2},{2,3},{3,0},{4,5},{5,6},{6,7},{7,4},{8,9},{9,10},{10,1... | collective-permute-start | bytes 491528 | tf_op jit(solution)/shard_map/ppermute | solution.py:259
  31.3 5.2 %collective-permute-start.3 = (bf16[128,640]{1,0:T(8,128)(2,1)}, bf16[128,640]{1,0:T(8,128)(2,1)S(1)}, u32[]{:S(2)}, u32[]{:S(2)}) collective-permute-start(bf16[128,640]{1,0:T(8,128)(2,1)} %get-tuple-element.18), channel_id=1, source_target_pairs={{0,2},{1,3},{2,0},{3,1},{4,6},{5,7},{6,4},{7,5},{8,10},{9,11},{10,... | collective-permute-start | bytes 491528 | tf_op jit(solution)/shard_map/ppermute | solution.py:259
  36.5 5.2 %collective-permute-start.4 = (bf16[128,640]{1,0:T(8,128)(2,1)}, bf16[128,640]{1,0:T(8,128)(2,1)S(1)}, u32[]{:S(2)}, u32[]{:S(2)}) collective-permute-start(bf16[128,640]{1,0:T(8,128)(2,1)} %get-tuple-element.19), channel_id=1, source_target_pairs={{0,3},{1,0},{2,1},{3,2},{4,7},{5,4},{6,5},{7,6},{8,11},{9,8},{10,9... | collective-permute-start | bytes 491528 | tf_op jit(solution)/shard_map/ppermute | solution.py:259
  41.7 1.0 collective-permute-done.2.rest_1_
  42.7 6.7 %collective-permute-done.3.rest_2_ = bf16[128,640]{1,0:T(8,128)(2,1)S(1)} collective-permute-done((bf16[128,640]{1,0:T(8,128)(2,1)}, bf16[128,640]{1,0:T(8,128)(2,1)S(1)}, u32[]{:S(2)}, u32[]{:S(2)}) %collective-permute-start.3) | collective-permute-done | bytes 163872 | tf_op jit(solution)/shard_map/ppermute | solution.py:259
  49.4 12.1 %collective-permute-done.4.rest_3_ = bf16[128,640]{1,0:T(8,128)(2,1)S(1)} collective-permute-done((bf16[128,640]{1,0:T(8,128)(2,1)}, bf16[128,640]{1,0:T(8,128)(2,1)S(1)}, u32[]{:S(2)}, u32[]{:S(2)}) %collective-permute-start.4) | collective-permute-done | bytes 163872 | tf_op jit(solution)/shard_map/ppermute | solution.py:259
  61.5 0.9 copy-done
  62.4 0.6 shard_map.97.weights
  63.0 1.2 shard_map.98
  64.1 5.2 %collective-permute-start.12 = (bf16[512,256]{1,0:T(8,128)(2,1)}, bf16[512,256]{1,0:T(8,128)(2,1)S(1)}, u32[]{:S(2)}, u32[]{:S(2)}) collective-permute-start(bf16[512,256]{1,0:T(8,128)(2,1)} %get-tuple-element.26), channel_id=1, source_target_pairs={{0,28},{1,29},{2,30},{3,31},{4,0},{5,1},{6,2},{7,3},{8,4},{9,5},{1... | collective-permute-start | bytes 786440 | tf_op jit(solution)/shard_map/ppermute | solution.py:263
  69.3 1.9 %collective-permute-start.5 = (bf16[512,256]{1,0:T(8,128)(2,1)S(1)}, bf16[512,256]{1,0:T(8,128)(2,1)S(1)}, u32[]{:S(2)}, u32[]{:S(2)}) collective-permute-start(bf16[512,256]{1,0:T(8,128)(2,1)S(1)} %get-tuple-element.21), channel_id=1, source_target_pairs={{0,4},{1,5},{2,6},{3,7},{4,8},{5,9},{6,10},{7,11},{8,12},{9,13},{1... | collective-permute-start | bytes 786440 | tf_op jit(solution)/shard_map/ppermute | solution.py:263
  71.3 3.6 %all-to-all-start.1 = ((bf16[4,128,768]{2,1,0:T(8,128)(2,1)}), bf16[4,128,768]{2,1,0:T(8,128)(2,1)S(1)}, u32[]{:S(2)}, u32[]{:S(2)}) async-start(bf16[4,128,768]{2,1,0:T(8,128)(2,1)} %get-tuple-element.20), calls=%async_computation.1 | async-start | bytes 1572864 | tf_op jit(solution)/shard_map/all_to_all | solution.py:267
  74.9 0.4 shard_map.102
  75.3 5.3 %collective-permute-start.13 = (bf16[1024,256]{1,0:T(8,128)(2,1)S(1)}, bf16[1024,256]{1,0:T(8,128)(2,1)S(1)}, u32[]{:S(2)}, u32[]{:S(2)}) collective-permute-start(bf16[1024,256]{1,0:T(8,128)(2,1)S(1)} %shard_map.102), channel_id=1, source_target_pairs={{0,28},{1,29},{2,30},{3,31},{4,0},{5,1},{6,2},{7,3},{8,4},{9,5},{1... | collective-permute-start | bytes 1572872 | tf_op jit(solution)/shard_map/ppermute | solution.py:263
  80.6 0.4 shard_map.99
  81.1 1.9 %collective-permute-start.6 = (bf16[1024,256]{1,0:T(8,128)(2,1)S(1)}, bf16[1024,256]{1,0:T(8,128)(2,1)S(1)}, u32[]{:S(2)}, u32[]{:S(2)}) collective-permute-start(bf16[1024,256]{1,0:T(8,128)(2,1)S(1)} %shard_map.99), channel_id=1, source_target_pairs={{0,4},{1,5},{2,6},{3,7},{4,8},{5,9},{6,10},{7,11},{8,12},{9,13},{1... | collective-permute-start | bytes 1572872 | tf_op jit(solution)/shard_map/ppermute | solution.py:263
  83.0 4.1 %collective-permute-start.7 = (bf16[128,512]{1,0:T(8,128)(2,1)S(1)}, bf16[128,512]{1,0:T(8,128)(2,1)S(1)}, u32[]{:S(2)}, u32[]{:S(2)}) collective-permute-start(bf16[128,512]{1,0:T(8,128)(2,1)S(1)} %copy-done.12), channel_id=1, source_target_pairs={{0,1},{1,2},{2,3},{3,0},{4,5},{5,6},{6,7},{7,4},{8,9},{9,10},{10,1... | collective-permute-start | bytes 393224 | tf_op jit(solution)/shard_map/ppermute | solution.py:259
  87.1 4.8 %collective-permute-start.8 = (bf16[128,512]{1,0:T(8,128)(2,1)S(1)}, bf16[128,512]{1,0:T(8,128)(2,1)S(1)}, u32[]{:S(2)}, u32[]{:S(2)}) collective-permute-start(bf16[128,512]{1,0:T(8,128)(2,1)S(1)} %copy-done.11), channel_id=1, source_target_pairs={{0,2},{1,3},{2,0},{3,1},{4,6},{5,7},{6,4},{7,5},{8,10},{9,11},{10,... | collective-permute-start | bytes 393224 | tf_op jit(solution)/shard_map/ppermute | solution.py:259
  91.9 5.2 %collective-permute-start.9 = (bf16[128,512]{1,0:T(8,128)(2,1)S(1)}, bf16[128,512]{1,0:T(8,128)(2,1)S(1)}, u32[]{:S(2)}, u32[]{:S(2)}) collective-permute-start(bf16[128,512]{1,0:T(8,128)(2,1)S(1)} %copy-done.10), channel_id=1, source_target_pairs={{0,3},{1,0},{2,1},{3,2},{4,7},{5,4},{6,5},{7,6},{8,11},{9,8},{10,9... | collective-permute-start | bytes 393224 | tf_op jit(solution)/shard_map/ppermute | solution.py:259
  97.2 7.8 %collective-permute-done.8.rest_2_ = bf16[128,512]{1,0:T(8,128)(2,1)S(1)} collective-permute-done((bf16[128,512]{1,0:T(8,128)(2,1)S(1)}, bf16[128,512]{1,0:T(8,128)(2,1)S(1)}, u32[]{:S(2)}, u32[]{:S(2)}) %collective-permute-start.8) | collective-permute-done | bytes 131104 | tf_op jit(solution)/shard_map/ppermute | solution.py:259
  104.9 2.9 %collective-permute-done.9.rest_3_ = bf16[128,512]{1,0:T(8,128)(2,1)S(1)} collective-permute-done((bf16[128,512]{1,0:T(8,128)(2,1)S(1)}, bf16[128,512]{1,0:T(8,128)(2,1)S(1)}, u32[]{:S(2)}, u32[]{:S(2)}) %collective-permute-start.9) | collective-permute-done | bytes 131104 | tf_op jit(solution)/shard_map/ppermute | solution.py:259
  107.8 0.4 shard_map.103
  108.2 4.8 %collective-permute-start.14 = (bf16[1024,256]{1,0:T(8,128)(2,1)S(1)}, bf16[1024,256]{1,0:T(8,128)(2,1)S(1)}, u32[]{:S(2)}, u32[]{:S(2)}) collective-permute-start(bf16[1024,256]{1,0:T(8,128)(2,1)S(1)} %shard_map.103), channel_id=1, source_target_pairs={{0,28},{1,29},{2,30},{3,31},{4,0},{5,1},{6,2},{7,3},{8,4},{9,5},{1... | collective-permute-start | bytes 1572872 | tf_op jit(solution)/shard_map/ppermute | solution.py:263
  113.1 0.4 shard_map.100
  113.5 1.9 %collective-permute-start.10 = (bf16[1024,256]{1,0:T(8,128)(2,1)S(1)}, bf16[1024,256]{1,0:T(8,128)(2,1)}, u32[]{:S(2)}, u32[]{:S(2)}) collective-permute-start(bf16[1024,256]{1,0:T(8,128)(2,1)S(1)} %shard_map.100), channel_id=1, source_target_pairs={{0,4},{1,5},{2,6},{3,7},{4,8},{5,9},{6,10},{7,11},{8,12},{9,13},{1... | collective-permute-start | bytes 1572872 | tf_op jit(solution)/shard_map/ppermute | solution.py:263
  115.4 8.4 %collective-permute-done.14.received = bf16[1024,256]{1,0:T(8,128)(2,1)S(1)} collective-permute-done((bf16[1024,256]{1,0:T(8,128)(2,1)S(1)}, bf16[1024,256]{1,0:T(8,128)(2,1)S(1)}, u32[]{:S(2)}, u32[]{:S(2)}) %collective-permute-start.14) | collective-permute-done | bytes 524320 | tf_op jit(solution)/shard_map/ppermute | solution.py:263
  123.8 0.4 shard_map.104
  124.3 5.5 %collective-permute-start.15 = (bf16[1024,256]{1,0:T(8,128)(2,1)S(1)}, bf16[1024,256]{1,0:T(8,128)(2,1)}, u32[]{:S(2)}, u32[]{:S(2)}) collective-permute-start(bf16[1024,256]{1,0:T(8,128)(2,1)S(1)} %shard_map.104), channel_id=1, source_target_pairs={{0,28},{1,29},{2,30},{3,31},{4,0},{5,1},{6,2},{7,3},{8,4},{9,5},{1... | collective-permute-start | bytes 1572872 | tf_op jit(solution)/shard_map/ppermute | solution.py:263
  129.8 1.5 shard_map.101
  131.2 1.9 %collective-permute-start.11 = (bf16[1024,256]{1,0:T(8,128)(2,1)S(1)}, bf16[1024,256]{1,0:T(8,128)(2,1)}, u32[]{:S(2)}, u32[]{:S(2)}) collective-permute-start(bf16[1024,256]{1,0:T(8,128)(2,1)S(1)} %shard_map.101), channel_id=1, source_target_pairs={{0,4},{1,5},{2,6},{3,7},{4,8},{5,9},{6,10},{7,11},{8,12},{9,13},{1... | collective-permute-start | bytes 1572872 | tf_op jit(solution)/shard_map/ppermute | solution.py:263
  133.3 0.7 broadcast_in_dim.33
  134.0 0.8 reshape.11.offsets
  134.8 4.8 %collective-permute-done.15.down = bf16[1024,256]{1,0:T(8,128)(2,1)} collective-permute-done((bf16[1024,256]{1,0:T(8,128)(2,1)S(1)}, bf16[1024,256]{1,0:T(8,128)(2,1)}, u32[]{:S(2)}, u32[]{:S(2)}) %collective-permute-start.15) | collective-permute-done | bytes 524320 | tf_op jit(solution)/shard_map/ppermute | solution.py:263
  139.7 6.6 %collective-permute-done.11.up = bf16[1024,256]{1,0:T(8,128)(2,1)} collective-permute-done((bf16[1024,256]{1,0:T(8,128)(2,1)S(1)}, bf16[1024,256]{1,0:T(8,128)(2,1)}, u32[]{:S(2)}, u32[]{:S(2)}) %collective-permute-start.11) | collective-permute-done | bytes 524320 | tf_op jit(solution)/shard_map/ppermute | solution.py:263
  146.3 0.9 copy-done.5
  147.2 0.9 copy-done.7
  148.1 4.6 %shard_map.105 = (bf16[1024,256]{1,0:T(8,128)(2,1)S(1)}, f32[64,256]{1,0:T(8,128)S(1)}, bf16[16,64,256]{2,1,0:T(8,128)(2,1)}) custom-call(bf16[1024,512]{1,0:T(8,128)(2,1)S(1)} %shard_map.97.weights, bf16[4,128,768]{2,1,0:T(8,128)(2,1)S(1)} %all-to-all-done.1.rest_0_.exchanged, bf16[1024,256]{1,0:T(8,128)(2,1)} %collective-permute-done.11.up, ...), custom_call_target="tpu_custom_call" | custom-call | flops 1610612736 | bytes 2097152 | tf_op jit(solution)/shard_map/pallas_call | solution.py:334
  152.7 7.6 %all-to-all-start.2 = ((bf16[16,64,256]{2,1,0:T(8,128)(2,1)}), bf16[16,64,256]{2,1,0:T(8,128)(2,1)S(1)}, u32[]{:S(2)}, u32[]{:S(2)}) async-start(bf16[16,64,256]{2,1,0:T(8,128)(2,1)} %get-tuple-element.29), calls=%async_computation.2 | async-start | bytes 1048576 | tf_op jit(solution)/shard_map/all_to_all | solution.py:344
  160.3 2.1 %shard_map.106 = bf16[1024,256]{1,0:T(8,128)(2,1)} custom-call(bf16[1024,256]{1,0:T(8,128)(2,1)S(1)} %bitcast.13, bf16[1024,256]{1,0:T(8,128)(2,1)S(1)} %get-tuple-element.27.summed, f32[64,256]{1,0:T(8,128)S(1)} %get-tuple-element.28.decoded, s32[16,256]{1,0:T(8,128)S(1)} %reshape.11.offsets, bf16[256,256]{1,0:T(8,128)(2,1)S(1)} %copy-done.4, ...), custom_call_target="tpu_custom_call" | custom-call | flops 1610612736 | bytes 2097152 | tf_op jit(solution)/shard_map/pallas_call | solution.py:345
  162.4 7.6 %all-to-all-done.2.parts = bf16[16,64,256]{2,1,0:T(8,128)(2,1)S(1)} async-done(((bf16[16,64,256]{2,1,0:T(8,128)(2,1)}), bf16[16,64,256]{2,1,0:T(8,128)(2,1)S(1)}, u32[]{:S(2)}, u32[]{:S(2)}) %all-to-all-start.2) | async-done | bytes 524320 | tf_op jit(solution)/shard_map/all_to_all | solution.py:344
  170.0 2.1 %shard_map.107 = bf16[1024,256]{1,0:T(8,128)(2,1)} custom-call(bf16[16,64,256]{2,1,0:T(8,128)(2,1)S(1)} %all-to-all-done.2.parts, s32[16,256]{1,0:T(8,128)S(1)} %reshape.11.offsets, bf16[256,256]{1,0:T(8,128)(2,1)S(1)} %copy-done.4, bf16[256,256]{1,0:T(8,128)(2,1)S(1)} %copy-done.6), custom_call_target="tpu_custom_call" | custom-call | flops 1610612736 | bytes 2097152 | tf_op jit(solution)/shard_map/pallas_call | solution.py:346
  (43 shorter events, 0.6 us)
Async XLA Ops:
  3.6 10.9 %copy-start.9 = (s32[1,1,128]{2,1,0:T(1,128)S(1)}, s32[1,1,128]{2,1,0:T(1,128)}, u32[]{:S(2)}) copy-start(s32[1,1,128]{2,1,0:T(1,128)} %param.10) | copy-start | bytes 1540
  3.7 57.8 %all-to-all-start = ((bf16[4,128,1280]{2,1,0:T(8,128)(2,1)}), bf16[4,128,1280]{2,1,0:T(8,128)(2,1)S(1)}, u32[]{:S(2)}, u32[]{:S(2)}) async-start(bf16[4,128,1280]{2,1,0:T(8,128)(2,1)} %shard_map.95), calls=%async_computation | async-start | bytes 2621440 | tf_op jit(solution)/shard_map/all_to_all | solution.py:267
  14.6 7.2 %collective-permute-start = (bf16[8,128]{1,0:T(8,128)(2,1)S(1)}, bf16[8,128]{1,0:T(8,128)(2,1)S(1)}, u32[]{:S(2)}, u32[]{:S(2)}) collective-permute-start(bf16[8,128]{1,0:T(8,128)(2,1)S(1)} %broadcast_in_dim.29), channel_id=1, source_target_pairs={{0,4},{1,5},{2,6},{3,7},{4,8},{5,9},{6,10},{7,11},{8,12},{9,13},{1... | collective-permute-start | bytes 6152 | tf_op jit(solution)/shard_map/ppermute | solution.py:263
  17.8 4.6 %collective-permute-start.1 = (bf16[8,128]{1,0:T(8,128)(2,1)S(1)}, bf16[8,128]{1,0:T(8,128)(2,1)S(1)}, u32[]{:S(2)}, u32[]{:S(2)}) collective-permute-start(bf16[8,128]{1,0:T(8,128)(2,1)S(1)} %broadcast_in_dim.29), channel_id=1, source_target_pairs={{0,28},{1,29},{2,30},{3,31},{4,0},{5,1},{6,2},{7,3},{8,4},{9,5},{1... | collective-permute-start | bytes 6152 | tf_op jit(solution)/shard_map/ppermute | solution.py:263
  27.0 15.7 %collective-permute-start.2 = (bf16[128,640]{1,0:T(8,128)(2,1)}, bf16[128,640]{1,0:T(8,128)(2,1)S(1)}, u32[]{:S(2)}, u32[]{:S(2)}) collective-permute-start(bf16[128,640]{1,0:T(8,128)(2,1)} %get-tuple-element.17), channel_id=1, source_target_pairs={{0,1},{1,2},{2,3},{3,0},{4,5},{5,6},{6,7},{7,4},{8,9},{9,10},{10,1... | collective-permute-start | bytes 491528 | tf_op jit(solution)/shard_map/ppermute | solution.py:259
  31.3 18.1 %collective-permute-start.3 = (bf16[128,640]{1,0:T(8,128)(2,1)}, bf16[128,640]{1,0:T(8,128)(2,1)S(1)}, u32[]{:S(2)}, u32[]{:S(2)}) collective-permute-start(bf16[128,640]{1,0:T(8,128)(2,1)} %get-tuple-element.18), channel_id=1, source_target_pairs={{0,2},{1,3},{2,0},{3,1},{4,6},{5,7},{6,4},{7,5},{8,10},{9,11},{10,... | collective-permute-start | bytes 491528 | tf_op jit(solution)/shard_map/ppermute | solution.py:259
  36.5 25.0 %collective-permute-start.4 = (bf16[128,640]{1,0:T(8,128)(2,1)}, bf16[128,640]{1,0:T(8,128)(2,1)S(1)}, u32[]{:S(2)}, u32[]{:S(2)}) collective-permute-start(bf16[128,640]{1,0:T(8,128)(2,1)} %get-tuple-element.19), channel_id=1, source_target_pairs={{0,3},{1,0},{2,1},{3,2},{4,7},{5,4},{6,5},{7,6},{8,11},{9,8},{10,9... | collective-permute-start | bytes 491528 | tf_op jit(solution)/shard_map/ppermute | solution.py:259
  61.5 0.9 copy-start
  64.1 10.7 %copy-start.1 = (bf16[128,640]{1,0:T(8,128)(2,1)S(1)}, bf16[128,640]{1,0:T(8,128)(2,1)}, u32[]{:S(2)}) copy-start(bf16[128,640]{1,0:T(8,128)(2,1)} %get-tuple-element.16.rest_0_) | copy-start | bytes 491524
  64.1 10.7 %collective-permute-start.12 = (bf16[512,256]{1,0:T(8,128)(2,1)}, bf16[512,256]{1,0:T(8,128)(2,1)S(1)}, u32[]{:S(2)}, u32[]{:S(2)}) collective-permute-start(bf16[512,256]{1,0:T(8,128)(2,1)} %get-tuple-element.26), channel_id=1, source_target_pairs={{0,28},{1,29},{2,30},{3,31},{4,0},{5,1},{6,2},{7,3},{8,4},{9,5},{1... | collective-permute-start | bytes 786440 | tf_op jit(solution)/shard_map/ppermute | solution.py:263
  69.3 11.3 %collective-permute-start.5 = (bf16[512,256]{1,0:T(8,128)(2,1)S(1)}, bf16[512,256]{1,0:T(8,128)(2,1)S(1)}, u32[]{:S(2)}, u32[]{:S(2)}) collective-permute-start(bf16[512,256]{1,0:T(8,128)(2,1)S(1)} %get-tuple-element.21), channel_id=1, source_target_pairs={{0,4},{1,5},{2,6},{3,7},{4,8},{5,9},{6,10},{7,11},{8,12},{9,13},{1... | collective-permute-start | bytes 786440 | tf_op jit(solution)/shard_map/ppermute | solution.py:263
  71.3 44.2 %all-to-all-start.1 = ((bf16[4,128,768]{2,1,0:T(8,128)(2,1)}), bf16[4,128,768]{2,1,0:T(8,128)(2,1)S(1)}, u32[]{:S(2)}, u32[]{:S(2)}) async-start(bf16[4,128,768]{2,1,0:T(8,128)(2,1)} %get-tuple-element.20), calls=%async_computation.1 | async-start | bytes 1572864 | tf_op jit(solution)/shard_map/all_to_all | solution.py:267
  75.3 7.7 %copy-start.12 = (bf16[128,512]{1,0:T(8,128)(2,1)S(1)}, bf16[128,512]{1,0:T(8,128)(2,1)}, u32[]{:S(2)}) copy-start(bf16[128,512]{1,0:T(8,128)(2,1)} %get-tuple-element.23) | copy-start | bytes 393220
  75.3 11.8 %copy-start.11 = (bf16[128,512]{1,0:T(8,128)(2,1)S(1)}, bf16[128,512]{1,0:T(8,128)(2,1)}, u32[]{:S(2)}) copy-start(bf16[128,512]{1,0:T(8,128)(2,1)} %get-tuple-element.24) | copy-start | bytes 393220
  75.3 16.6 %copy-start.10 = (bf16[128,512]{1,0:T(8,128)(2,1)S(1)}, bf16[128,512]{1,0:T(8,128)(2,1)}, u32[]{:S(2)}) copy-start(bf16[128,512]{1,0:T(8,128)(2,1)} %get-tuple-element.25) | copy-start | bytes 393220
  75.3 32.5 %copy-start.2 = (bf16[128,512]{1,0:T(8,128)(2,1)S(1)}, bf16[128,512]{1,0:T(8,128)(2,1)}, u32[]{:S(2)}) copy-start(bf16[128,512]{1,0:T(8,128)(2,1)} %get-tuple-element.22.rest_0_) | copy-start | bytes 393220
  75.3 32.5 %collective-permute-start.13 = (bf16[1024,256]{1,0:T(8,128)(2,1)S(1)}, bf16[1024,256]{1,0:T(8,128)(2,1)S(1)}, u32[]{:S(2)}, u32[]{:S(2)}) collective-permute-start(bf16[1024,256]{1,0:T(8,128)(2,1)S(1)} %shard_map.102), channel_id=1, source_target_pairs={{0,28},{1,29},{2,30},{3,31},{4,0},{5,1},{6,2},{7,3},{8,4},{9,5},{1... | collective-permute-start | bytes 1572872 | tf_op jit(solution)/shard_map/ppermute | solution.py:263
  81.1 32.0 %collective-permute-start.6 = (bf16[1024,256]{1,0:T(8,128)(2,1)S(1)}, bf16[1024,256]{1,0:T(8,128)(2,1)S(1)}, u32[]{:S(2)}, u32[]{:S(2)}) collective-permute-start(bf16[1024,256]{1,0:T(8,128)(2,1)S(1)} %shard_map.99), channel_id=1, source_target_pairs={{0,4},{1,5},{2,6},{3,7},{4,8},{5,9},{6,10},{7,11},{8,12},{9,13},{1... | collective-permute-start | bytes 1572872 | tf_op jit(solution)/shard_map/ppermute | solution.py:263
  83.0 14.1 %collective-permute-start.7 = (bf16[128,512]{1,0:T(8,128)(2,1)S(1)}, bf16[128,512]{1,0:T(8,128)(2,1)S(1)}, u32[]{:S(2)}, u32[]{:S(2)}) collective-permute-start(bf16[128,512]{1,0:T(8,128)(2,1)S(1)} %copy-done.12), channel_id=1, source_target_pairs={{0,1},{1,2},{2,3},{3,0},{4,5},{5,6},{6,7},{7,4},{8,9},{9,10},{10,1... | collective-permute-start | bytes 393224 | tf_op jit(solution)/shard_map/ppermute | solution.py:259
  87.1 17.8 %collective-permute-start.8 = (bf16[128,512]{1,0:T(8,128)(2,1)S(1)}, bf16[128,512]{1,0:T(8,128)(2,1)S(1)}, u32[]{:S(2)}, u32[]{:S(2)}) collective-permute-start(bf16[128,512]{1,0:T(8,128)(2,1)S(1)} %copy-done.11), channel_id=1, source_target_pairs={{0,2},{1,3},{2,0},{3,1},{4,6},{5,7},{6,4},{7,5},{8,10},{9,11},{10,... | collective-permute-start | bytes 393224 | tf_op jit(solution)/shard_map/ppermute | solution.py:259
  91.9 15.9 %collective-permute-start.9 = (bf16[128,512]{1,0:T(8,128)(2,1)S(1)}, bf16[128,512]{1,0:T(8,128)(2,1)S(1)}, u32[]{:S(2)}, u32[]{:S(2)}) collective-permute-start(bf16[128,512]{1,0:T(8,128)(2,1)S(1)} %copy-done.10), channel_id=1, source_target_pairs={{0,3},{1,0},{2,1},{3,2},{4,7},{5,4},{6,5},{7,6},{8,11},{9,8},{10,9... | collective-permute-start | bytes 393224 | tf_op jit(solution)/shard_map/ppermute | solution.py:259
  108.2 15.6 %collective-permute-start.14 = (bf16[1024,256]{1,0:T(8,128)(2,1)S(1)}, bf16[1024,256]{1,0:T(8,128)(2,1)S(1)}, u32[]{:S(2)}, u32[]{:S(2)}) collective-permute-start(bf16[1024,256]{1,0:T(8,128)(2,1)S(1)} %shard_map.103), channel_id=1, source_target_pairs={{0,28},{1,29},{2,30},{3,31},{4,0},{5,1},{6,2},{7,3},{8,4},{9,5},{1... | collective-permute-start | bytes 1572872 | tf_op jit(solution)/shard_map/ppermute | solution.py:263
  113.5 16.3 %collective-permute-start.10 = (bf16[1024,256]{1,0:T(8,128)(2,1)S(1)}, bf16[1024,256]{1,0:T(8,128)(2,1)}, u32[]{:S(2)}, u32[]{:S(2)}) collective-permute-start(bf16[1024,256]{1,0:T(8,128)(2,1)S(1)} %shard_map.100), channel_id=1, source_target_pairs={{0,4},{1,5},{2,6},{3,7},{4,8},{5,9},{6,10},{7,11},{8,12},{9,13},{1... | collective-permute-start | bytes 1572872 | tf_op jit(solution)/shard_map/ppermute | solution.py:263
  124.3 8.9 %copy-start.8 = (s32[1,16,4]{1,2,0:T(4,128)S(1)}, s32[1,16,4]{1,2,0:T(4,128)}, u32[]{:S(2)}) copy-start(s32[1,16,4]{1,2,0:T(4,128)} %param.11) | copy-start | bytes 772
  124.3 22.0 %copy-start.3 = (bf16[1,1024,256]{2,1,0:T(8,128)(2,1)S(1)}, bf16[1,1024,256]{2,1,0:T(8,128)(2,1)}, u32[]{:S(2)}) copy-start(bf16[1,1024,256]{2,1,0:T(8,128)(2,1)} %param.12) | copy-start | bytes 1572868
  124.3 22.0 %copy-start.4 = (bf16[256,256]{1,0:T(8,128)(2,1)S(1)}, bf16[256,256]{1,0:T(8,128)(2,1)}, u32[]{:S(2)}) copy-start(bf16[256,256]{1,0:T(8,128)(2,1)} %constant.11.clone.high) | copy-start | bytes 393220
  124.3 15.4 %collective-permute-start.15 = (bf16[1024,256]{1,0:T(8,128)(2,1)S(1)}, bf16[1024,256]{1,0:T(8,128)(2,1)}, u32[]{:S(2)}, u32[]{:S(2)}) collective-permute-start(bf16[1024,256]{1,0:T(8,128)(2,1)S(1)} %shard_map.104), channel_id=1, source_target_pairs={{0,28},{1,29},{2,30},{3,31},{4,0},{5,1},{6,2},{7,3},{8,4},{9,5},{1... | collective-permute-start | bytes 1572872 | tf_op jit(solution)/shard_map/ppermute | solution.py:263
  131.2 15.1 %collective-permute-start.11 = (bf16[1024,256]{1,0:T(8,128)(2,1)S(1)}, bf16[1024,256]{1,0:T(8,128)(2,1)}, u32[]{:S(2)}, u32[]{:S(2)}) collective-permute-start(bf16[1024,256]{1,0:T(8,128)(2,1)S(1)} %shard_map.101), channel_id=1, source_target_pairs={{0,4},{1,5},{2,6},{3,7},{4,8},{5,9},{6,10},{7,11},{8,12},{9,13},{1... | collective-permute-start | bytes 1572872 | tf_op jit(solution)/shard_map/ppermute | solution.py:263
  146.3 0.9 copy-start.5
  147.2 0.9 copy-start.7
  148.1 12.2 %copy-start.6 = (bf16[256,256]{1,0:T(8,128)(2,1)S(1)}, bf16[256,256]{1,0:T(8,128)(2,1)}, u32[]{:S(2)}) copy-start(bf16[256,256]{1,0:T(8,128)(2,1)} %constant.12.clone.low) | copy-start | bytes 393220
  152.7 17.2 %all-to-all-start.2 = ((bf16[16,64,256]{2,1,0:T(8,128)(2,1)}), bf16[16,64,256]{2,1,0:T(8,128)(2,1)S(1)}, u32[]{:S(2)}, u32[]{:S(2)}) async-start(bf16[16,64,256]{2,1,0:T(8,128)(2,1)} %get-tuple-element.29), calls=%async_computation.2 | async-start | bytes 1048576 | tf_op jit(solution)/shard_map/all_to_all | solution.py:344
where the time goes:
time: 173 us; the launch traced here: 172 us
  starting transfers between devices  86.2 us (50%)
  waiting for transfers between devices  58.5 us (34%)
  Pallas kernels  20.9 us (12%)
  local copies, waits for them, and re-layouts  4.57 us (3%)
    ppermute x10, starting transfers between devices, across(): return lax.ppermute(x, 'shard', pairs)  35.5 us
    ppermute x6, waiting for transfers between devices, along_line(): return lax.ppermute(x, 'shard', pairs)  30.4 us
    ppermute x6, starting transfers between devices, along_line(): return lax.ppermute(x, 'shard', pairs)  28.8 us
    ppermute x10, waiting for transfers between devices, across(): return lax.ppermute(x, 'shard', pairs)  20.5 us
    all_to_all x2, starting transfers between devices, exchange(): return lax.all_to_all(x, 'shard', 0, 0, axis_index_groups=lines, tiled=True)  14.4 us
    all_to_all x1, waiting for transfers between devices, step(): parts = lax.all_to_all(sent, 'rep', 0, 0, tiled=True)  7.59 us
    all_to_all x1, starting transfers between devices, step(): parts = lax.all_to_all(sent, 'rep', 0, 0, tiled=True)  7.56 us
    pallas_call x1, Pallas kernels, step(): call(forward_kernel, (shaped(panel, width), shaped(kept, width, dtype=jnp...  4.62 us
  transfers between devices with their start and end apart: 19, of which 10 were waited for; matrix products, arithmetic and copies ran while one was open for 2% of the time, Pallas kernels for 6%

commit v1 on v0

--- a/solution.py
+++ b/solution.py
@@ -98,9 +98,9 @@
         copy.wait()
 
 
-def late_kernel(rows, extra, *rest):
-    deep = 4
-    third, second, last, sem = rest[:deep], rest[deep : 2 * deep], rest[2 * deep], rest[2 * deep + 1]
+def late_kernel(rows, *rest):
+    third, (second, last, sem) = rest[:-3], rest[-3:]
+    deep = len(third)
     width = last.shape[2] // 3
     me = lax.axis_index("shard") % deep
     moves = []
@@ -108,27 +108,20 @@
         z = (me + k) % deep
         for j, owner in enumerate((3, -3)):
             moves.append((owner, z, third[k].at[:, pl.ds(j * width, width)]))
-    for k in range(deep):
-        z = (me + k) % deep
-        for j, owner in enumerate((2, -2)):
-            moves.append((owner, z, second[k].at[:, pl.ds(j * width, width)]))
-    for z in range(deep):
-        for j, owner in enumerate((1, -1, 0)):
-            moves.append((owner, z, last.at[z, :, pl.ds(j * width, width)]))
-    copies = fetch(rows, deep, width, moves, sem)
-    for k in range(deep):
-        third[k][:, 2 * width :] = extra[...]
-    for copy in copies:
+    for target, owners in ((second, (2, -2)), (last, (1, -1, 0))):
+        for z in range(deep):
+            for j, owner in enumerate(owners):
+                moves.append((owner, z, target.at[z, :, pl.ds(j * width, width)]))
+    for copy in fetch(rows, deep, width, moves, sem):
         copy.wait()
 
 
 def scale_kernel(exchanged, *rest):
     notes, out = rest[:-1], rest[-1]
     deep, tokens = exchanged.shape[0], exchanged.shape[1]
-    width = notes[0].shape[1] - 128
-    panel = exchanged.shape[2] - width // 2
+    panel = out.shape[0]
     z = lax.axis_index("shard") % deep
-    marks = [note[:, width:].astype(jnp.float32) for note in notes]
+    marks = [note[...].astype(jnp.float32) for note in notes]
     heads = marks[0][:8]
     for mark in marks[1:]:
         heads = heads + mark[:8]
@@ -293,22 +286,26 @@
         [onehot[:, :16], jnp.broadcast_to(lanes, (tokens, 48)), jnp.zeros((tokens, 64), jnp.float32)], axis=1
     ).astype(jnp.bfloat16)
 
+    notes = [extra]
+    for k in (2, 1, 3):
+        notes.append(along_line(extra, k))
+    notes = [notes[0], notes[2], notes[1], notes[3]]
+
     outs = call(
         late_kernel,
-        [shaped(tokens, 2 * width + 128)] * deep + [shaped(tokens, 2 * width)] * deep + [shaped(deep, tokens, 3 * width)],
+        [shaped(tokens, 2 * width)] * deep + [shaped(deep, tokens, 2 * width), shaped(deep, tokens, 3 * width)],
         work,
         (pltpu.SemaphoreType.DMA((7 * deep,)),),
-        [apart, whole],
+        [apart],
         FULL,
-    )(rows, extra)
-    third, second, last = list(outs[:deep]), list(outs[deep : 2 * deep]), outs[2 * deep]
+    )(rows)
+    third, second, last = list(outs[:deep]), outs[deep], outs[deep + 1]
     for k in (2, 1, 3):
         third[k] = along_line(third[k], k)
-    for k in (2, 1, 3):
-        second[k] = along_line(second[k], k)
+    second = exchange(second)
     last = exchange(last)
 
-    weights = call(scale_kernel, shaped(panel, deep * tokens), work)(early, *third)
+    weights = call(scale_kernel, shaped(panel, deep * tokens), work)(early, *notes)
     half = panel // 2
     up, down = call(far_kernel, [shaped(half, width)] * 2, work)(weights, early)
 
@@ -323,7 +320,7 @@
 
     up, down = ring(up, down)
     up, down = ring(near(0, True, up, third), near(width, False, down, third))
-    up, down = ring(near(0, True, up, second), near(width, False, down, second))
+    up, down = ring(near(0, True, up, [second]), near(width, False, down, [second]))
     up, down = ring(near(0, True, up, [last]), near(width, False, down, [last]))
 
     high, low = dct_parts()

time: 173 us -> 179 us (1.035)
  the two profiles are of different devices: /device:TPU:1 before, /device:TPU:408 now
where the time goes in v1:
time: 179 us; the launch traced here: 177 us
  starting transfers between devices  90.4 us (51%)
  waiting for transfers between devices  62.3 us (35%)
  Pallas kernels  20.3 us (11%)
  local copies, waits for them, and re-layouts  3.31 us (2%)
    ppermute x10, starting transfers between devices, across(): return lax.ppermute(x, 'shard', pairs)  36.9 us
    ppermute x6, starting transfers between devices, along_line(): return lax.ppermute(x, 'shard', pairs)  25.9 us
    ppermute x10, waiting for transfers between devices, across(): return lax.ppermute(x, 'shard', pairs)  25.5 us
    all_to_all x3, waiting for transfers between devices, exchange(): return lax.all_to_all(x, 'shard', 0, 0, axis_index_groups=lines, tiled=True)  20.5 us
    all_to_all x3, starting transfers between devices, exchange(): return lax.all_to_all(x, 'shard', 0, 0, axis_index_groups=lines, tiled=True)  18.4 us
    all_to_all x1, starting transfers between devices, step(): parts = lax.all_to_all(sent, 'rep', 0, 0, tiled=True)  9.19 us
    all_to_all x1, waiting for transfers between devices, step(): parts = lax.all_to_all(sent, 'rep', 0, 0, tiled=True)  8.75 us
    ppermute x6, waiting for transfers between devices, along_line(): return lax.ppermute(x, 'shard', pairs)  7.55 us
  transfers between devices with their start and end apart: 20, of which 10 were waited for; matrix products, arithmetic and copies ran while one was open for 0% of the time, Pallas kernels for 6%

profile of v1, /device:TPU:408, one launch (start us, length us, event | category | flops | bytes accessed | tf_op | source)
XLA Modules:
  0.0 177.5 jit_solution(4000408028349769450)
XLA Ops:
  0.6 3.0 %shard_map.95 = bf16[4,128,1280]{2,1,0:T(8,128)(2,1)} custom-call(bf16[128,8192]{1,0:T(8,128)(2,1)} %bitcast.14, bf16[128,1024]{1,0:T(8,128)(2,1)} %bitcast.16), custom_call_target="tpu_custom_call" | custom-call | flops 268435456 | bytes 2097152 | tf_op jit(solution)/shard_map/pallas_call | solution.py:270
  3.7 5.4 %all-to-all-start = ((bf16[4,128,1280]{2,1,0:T(8,128)(2,1)}), bf16[4,128,1280]{2,1,0:T(8,128)(2,1)S(1)}, u32[]{:S(2)}, u32[]{:S(2)}) async-start(bf16[4,128,1280]{2,1,0:T(8,128)(2,1)} %shard_map.95), calls=%async_computation | async-start | bytes 2621440 | tf_op jit(solution)/shard_map/all_to_all | solution.py:260
  9.1 0.1 fusion.1
  9.2 2.4 %collective-permute-start.1 = (bf16[8,128]{1,0:T(8,128)(2,1)S(1)}, bf16[8,128]{1,0:T(8,128)(2,1)S(1)}, u32[]{:S(2)}, u32[]{:S(2)}) collective-permute-start(bf16[8,128]{1,0:T(8,128)(2,1)S(1)} %broadcast_in_dim.29), channel_id=1, source_target_pairs={{0,28},{1,29},{2,30},{3,31},{4,0},{5,1},{6,2},{7,3},{8,4},{9,5},{1... | collective-permute-start | bytes 6152 | tf_op jit(solution)/shard_map/ppermute | solution.py:256
  11.6 4.7 %collective-permute-start = (bf16[8,128]{1,0:T(8,128)(2,1)S(1)}, bf16[8,128]{1,0:T(8,128)(2,1)S(1)}, u32[]{:S(2)}, u32[]{:S(2)}) collective-permute-start(bf16[8,128]{1,0:T(8,128)(2,1)S(1)} %broadcast_in_dim.29), channel_id=1, source_target_pairs={{0,4},{1,5},{2,6},{3,7},{4,8},{5,9},{6,10},{7,11},{8,12},{9,13},{1... | collective-permute-start | bytes 6152 | tf_op jit(solution)/shard_map/ppermute | solution.py:256
  16.3 3.0 %shard_map.97 = (bf16[128,512]{1,0:T(8,128)(2,1)}, bf16[128,512]{1,0:T(8,128)(2,1)}, bf16[128,512]{1,0:T(8,128)(2,1)}, bf16[128,512]{1,0:T(8,128)(2,1)}, bf16[4,...) custom-call(bf16[128,8192]{1,0:T(8,128)(2,1)} %bitcast.15), custom_call_target="tpu_custom_call" | custom-call | flops 268435456 | bytes 2097152 | tf_op jit(solution)/shard_map/pallas_call | solution.py:294
  19.4 20.5 %all-to-all-done.exchanged = bf16[4,128,1280]{2,1,0:T(8,128)(2,1)S(1)} async-done(((bf16[4,128,1280]{2,1,0:T(8,128)(2,1)}), bf16[4,128,1280]{2,1,0:T(8,128)(2,1)S(1)}, u32[]{:S(2)}, u32[]{:S(2)}) %all-to-all-start) | async-done | bytes 1310752 | tf_op jit(solution)/shard_map/all_to_all | solution.py:260
  39.8 5.4 %all-to-all-start.2 = ((bf16[4,128,512]{2,1,0:T(8,128)(2,1)}), bf16[4,128,512]{2,1,0:T(8,128)(2,1)S(1)}, u32[]{:S(2)}, u32[]{:S(2)}) async-start(bf16[4,128,512]{2,1,0:T(8,128)(2,1)} %get-tuple-element.19), calls=%async_computation.2 | async-start | bytes 1048576 | tf_op jit(solution)/shard_map/all_to_all | solution.py:260
  45.5 4.3 %collective-permute-start.4 = (bf16[128,128]{1,0:T(8,128)(2,1)S(1)}, bf16[128,128]{1,0:T(8,128)(2,1)S(1)}, u32[]{:S(2)}, u32[]{:S(2)}) collective-permute-start(bf16[128,128]{1,0:T(8,128)(2,1)S(1)} %maximum_maximum_fusion.rest_0_), channel_id=1, source_target_pairs={{0,3},{1,0},{2,1},{3,2},{4,7},{5,4},{6,5},{7,6},{8,11},{9,8},{10,9... | collective-permute-start | bytes 98312 | tf_op jit(solution)/shard_map/ppermute | solution.py:252
  49.8 1.9 %collective-permute-start.3 = (bf16[128,128]{1,0:T(8,128)(2,1)S(1)}, bf16[128,128]{1,0:T(8,128)(2,1)S(1)}, u32[]{:S(2)}, u32[]{:S(2)}) collective-permute-start(bf16[128,128]{1,0:T(8,128)(2,1)S(1)} %maximum_maximum_fusion.rest_0_), channel_id=1, source_target_pairs={{0,2},{1,3},{2,0},{3,1},{4,6},{5,7},{6,4},{7,5},{8,10},{9,11},{10,... | collective-permute-start | bytes 98312 | tf_op jit(solution)/shard_map/ppermute | solution.py:252
  51.7 6.0 %collective-permute-start.2 = (bf16[128,128]{1,0:T(8,128)(2,1)S(1)}, bf16[128,128]{1,0:T(8,128)(2,1)S(1)}, u32[]{:S(2)}, u32[]{:S(2)}) collective-permute-start(bf16[128,128]{1,0:T(8,128)(2,1)S(1)} %maximum_maximum_fusion.rest_0_), channel_id=1, source_target_pairs={{0,1},{1,2},{2,3},{3,0},{4,5},{5,6},{6,7},{7,4},{8,9},{9,10},{10,1... | collective-permute-start | bytes 98312 | tf_op jit(solution)/shard_map/ppermute | solution.py:252
  57.8 1.9 %collective-permute-done.4.rest_3_ = bf16[128,128]{1,0:T(8,128)(2,1)S(1)} collective-permute-done((bf16[128,128]{1,0:T(8,128)(2,1)S(1)}, bf16[128,128]{1,0:T(8,128)(2,1)S(1)}, u32[]{:S(2)}, u32[]{:S(2)}) %collective-permute-start.4) | collective-permute-done | bytes 32800 | tf_op jit(solution)/shard_map/ppermute | solution.py:252
  59.7 0.2 collective-permute-done.2.rest_1_
  59.9 0.6 shard_map.96.weights
  60.5 1.2 shard_map.98
  61.8 4.8 %collective-permute-start.5 = (bf16[512,256]{1,0:T(8,128)(2,1)}, bf16[512,256]{1,0:T(8,128)(2,1)S(1)}, u32[]{:S(2)}, u32[]{:S(2)}) collective-permute-start(bf16[512,256]{1,0:T(8,128)(2,1)} %get-tuple-element.14), channel_id=1, source_target_pairs={{0,4},{1,5},{2,6},{3,7},{4,8},{5,9},{6,10},{7,11},{8,12},{9,13},{1... | collective-permute-start | bytes 786440 | tf_op jit(solution)/shard_map/ppermute | solution.py:256
  66.6 1.9 %collective-permute-start.12 = (bf16[512,256]{1,0:T(8,128)(2,1)}, bf16[512,256]{1,0:T(8,128)(2,1)S(1)}, u32[]{:S(2)}, u32[]{:S(2)}) collective-permute-start(bf16[512,256]{1,0:T(8,128)(2,1)} %get-tuple-element.20), channel_id=1, source_target_pairs={{0,28},{1,29},{2,30},{3,31},{4,0},{5,1},{6,2},{7,3},{8,4},{9,5},{1... | collective-permute-start | bytes 786440 | tf_op jit(solution)/shard_map/ppermute | solution.py:256
  68.5 6.1 %collective-permute-start.6 = (bf16[128,512]{1,0:T(8,128)(2,1)}, bf16[128,512]{1,0:T(8,128)(2,1)S(1)}, u32[]{:S(2)}, u32[]{:S(2)}) collective-permute-start(bf16[128,512]{1,0:T(8,128)(2,1)} %get-tuple-element.16), channel_id=1, source_target_pairs={{0,1},{1,2},{2,3},{3,0},{4,5},{5,6},{6,7},{7,4},{8,9},{9,10},{10,1... | collective-permute-start | bytes 393224 | tf_op jit(solution)/shard_map/ppermute | solution.py:252
  74.6 5.1 %collective-permute-start.7 = (bf16[128,512]{1,0:T(8,128)(2,1)}, bf16[128,512]{1,0:T(8,128)(2,1)S(1)}, u32[]{:S(2)}, u32[]{:S(2)}) collective-permute-start(bf16[128,512]{1,0:T(8,128)(2,1)} %get-tuple-element.17), channel_id=1, source_target_pairs={{0,2},{1,3},{2,0},{3,1},{4,6},{5,7},{6,4},{7,5},{8,10},{9,11},{10,... | collective-permute-start | bytes 393224 | tf_op jit(solution)/shard_map/ppermute | solution.py:252
  79.7 2.5 %collective-permute-start.8 = (bf16[128,512]{1,0:T(8,128)(2,1)S(1)}, bf16[128,512]{1,0:T(8,128)(2,1)S(1)}, u32[]{:S(2)}, u32[]{:S(2)}) collective-permute-start(bf16[128,512]{1,0:T(8,128)(2,1)S(1)} %copy-done.8), channel_id=1, source_target_pairs={{0,3},{1,0},{2,1},{3,2},{4,7},{5,4},{6,5},{7,6},{8,11},{9,8},{10,9... | collective-permute-start | bytes 393224 | tf_op jit(solution)/shard_map/ppermute | solution.py:252
  82.2 7.6 %all-to-all-start.1 = ((bf16[4,128,768]{2,1,0:T(8,128)(2,1)}), bf16[4,128,768]{2,1,0:T(8,128)(2,1)S(1)}, u32[]{:S(2)}, u32[]{:S(2)}) async-start(bf16[4,128,768]{2,1,0:T(8,128)(2,1)} %get-tuple-element.13), calls=%async_computation.1 | async-start | bytes 1572864 | tf_op jit(solution)/shard_map/all_to_all | solution.py:260
  89.8 5.4 %collective-permute-done.8.rest_3_ = bf16[128,512]{1,0:T(8,128)(2,1)S(1)} collective-permute-done((bf16[128,512]{1,0:T(8,128)(2,1)S(1)}, bf16[128,512]{1,0:T(8,128)(2,1)S(1)}, u32[]{:S(2)}, u32[]{:S(2)}) %collective-permute-start.8) | collective-permute-done | bytes 131104 | tf_op jit(solution)/shard_map/ppermute | solution.py:252
  95.2 0.4 shard_map.99
  95.7 5.9 %collective-permute-start.9 = (bf16[1024,256]{1,0:T(8,128)(2,1)S(1)}, bf16[1024,256]{1,0:T(8,128)(2,1)S(1)}, u32[]{:S(2)}, u32[]{:S(2)}) collective-permute-start(bf16[1024,256]{1,0:T(8,128)(2,1)S(1)} %shard_map.99), channel_id=1, source_target_pairs={{0,4},{1,5},{2,6},{3,7},{4,8},{5,9},{6,10},{7,11},{8,12},{9,13},{1... | collective-permute-start | bytes 1572872 | tf_op jit(solution)/shard_map/ppermute | solution.py:256
  101.6 0.4 shard_map.102
  102.0 1.9 %collective-permute-start.13 = (bf16[1024,256]{1,0:T(8,128)(2,1)S(1)}, bf16[1024,256]{1,0:T(8,128)(2,1)S(1)}, u32[]{:S(2)}, u32[]{:S(2)}) collective-permute-start(bf16[1024,256]{1,0:T(8,128)(2,1)S(1)} %shard_map.102), channel_id=1, source_target_pairs={{0,28},{1,29},{2,30},{3,31},{4,0},{5,1},{6,2},{7,3},{8,4},{9,5},{1... | collective-permute-start | bytes 1572872 | tf_op jit(solution)/shard_map/ppermute | solution.py:256
  104.0 7.7 %collective-permute-done.9.received = bf16[1024,256]{1,0:T(8,128)(2,1)S(1)} collective-permute-done((bf16[1024,256]{1,0:T(8,128)(2,1)S(1)}, bf16[1024,256]{1,0:T(8,128)(2,1)S(1)}, u32[]{:S(2)}, u32[]{:S(2)}) %collective-permute-start.9) | collective-permute-done | bytes 524320 | tf_op jit(solution)/shard_map/ppermute | solution.py:256
  111.7 0.4 shard_map.100
  112.1 5.6 %collective-permute-start.10 = (bf16[1024,256]{1,0:T(8,128)(2,1)S(1)}, bf16[1024,256]{1,0:T(8,128)(2,1)}, u32[]{:S(2)}, u32[]{:S(2)}) collective-permute-start(bf16[1024,256]{1,0:T(8,128)(2,1)S(1)} %shard_map.100), channel_id=1, source_target_pairs={{0,4},{1,5},{2,6},{3,7},{4,8},{5,9},{6,10},{7,11},{8,12},{9,13},{1... | collective-permute-start | bytes 1572872 | tf_op jit(solution)/shard_map/ppermute | solution.py:256
  117.7 0.3 collective-permute-done.13.received
  118.0 0.4 shard_map.103
  118.5 1.9 %collective-permute-start.14 = (bf16[1024,256]{1,0:T(8,128)(2,1)S(1)}, bf16[1024,256]{1,0:T(8,128)(2,1)S(1)}, u32[]{:S(2)}, u32[]{:S(2)}) collective-permute-start(bf16[1024,256]{1,0:T(8,128)(2,1)S(1)} %shard_map.103), channel_id=1, source_target_pairs={{0,28},{1,29},{2,30},{3,31},{4,0},{5,1},{6,2},{7,3},{8,4},{9,5},{1... | collective-permute-start | bytes 1572872 | tf_op jit(solution)/shard_map/ppermute | solution.py:256
  120.4 7.3 %collective-permute-done.10.received = bf16[1024,256]{1,0:T(8,128)(2,1)} collective-permute-done((bf16[1024,256]{1,0:T(8,128)(2,1)S(1)}, bf16[1024,256]{1,0:T(8,128)(2,1)}, u32[]{:S(2)}, u32[]{:S(2)}) %collective-permute-start.10) | collective-permute-done | bytes 524320 | tf_op jit(solution)/shard_map/ppermute | solution.py:256
  127.7 1.5 shard_map.101
  129.2 5.8 %collective-permute-start.11 = (bf16[1024,256]{1,0:T(8,128)(2,1)S(1)}, bf16[1024,256]{1,0:T(8,128)(2,1)}, u32[]{:S(2)}, u32[]{:S(2)}) collective-permute-start(bf16[1024,256]{1,0:T(8,128)(2,1)S(1)} %shard_map.101), channel_id=1, source_target_pairs={{0,4},{1,5},{2,6},{3,7},{4,8},{5,9},{6,10},{7,11},{8,12},{9,13},{1... | collective-permute-start | bytes 1572872 | tf_op jit(solution)/shard_map/ppermute | solution.py:256
  135.0 0.5 shard_map.104
  135.5 1.9 %collective-permute-start.15 = (bf16[1024,256]{1,0:T(8,128)(2,1)S(1)}, bf16[1024,256]{1,0:T(8,128)(2,1)}, u32[]{:S(2)}, u32[]{:S(2)}) collective-permute-start(bf16[1024,256]{1,0:T(8,128)(2,1)S(1)} %shard_map.104), channel_id=1, source_target_pairs={{0,28},{1,29},{2,30},{3,31},{4,0},{5,1},{6,2},{7,3},{8,4},{9,5},{1... | collective-permute-start | bytes 1572872 | tf_op jit(solution)/shard_map/ppermute | solution.py:256
  137.6 0.1 reshape.11.offsets
  137.7 4.0 %collective-permute-done.11.up = bf16[1024,256]{1,0:T(8,128)(2,1)} collective-permute-done((bf16[1024,256]{1,0:T(8,128)(2,1)S(1)}, bf16[1024,256]{1,0:T(8,128)(2,1)}, u32[]{:S(2)}, u32[]{:S(2)}) %collective-permute-start.11) | collective-permute-done | bytes 524320 | tf_op jit(solution)/shard_map/ppermute | solution.py:256
  141.7 6.2 %collective-permute-done.15.down = bf16[1024,256]{1,0:T(8,128)(2,1)} collective-permute-done((bf16[1024,256]{1,0:T(8,128)(2,1)S(1)}, bf16[1024,256]{1,0:T(8,128)(2,1)}, u32[]{:S(2)}, u32[]{:S(2)}) %collective-permute-start.15) | collective-permute-done | bytes 524320 | tf_op jit(solution)/shard_map/ppermute | solution.py:256
  147.9 1.0 copy-done.1
  148.9 0.9 copy-done.3
  149.8 0.9 copy-done.5
  150.8 4.6 %shard_map.105 = (bf16[1024,256]{1,0:T(8,128)(2,1)S(1)}, f32[64,256]{1,0:T(8,128)S(1)}, bf16[16,64,256]{2,1,0:T(8,128)(2,1)}) custom-call(bf16[1024,512]{1,0:T(8,128)(2,1)S(1)} %shard_map.96.weights, bf16[4,128,768]{2,1,0:T(8,128)(2,1)S(1)} %all-to-all-done.1.rest_0_.exchanged, bf16[1024,256]{1,0:T(8,128)(2,1)} %collective-permute-done.11.up, ...), custom_call_target="tpu_custom_call" | custom-call | flops 1610612736 | bytes 2097152 | tf_op jit(solution)/shard_map/pallas_call | solution.py:331
  155.4 9.2 %all-to-all-start.3 = ((bf16[16,64,256]{2,1,0:T(8,128)(2,1)}), bf16[16,64,256]{2,1,0:T(8,128)(2,1)S(1)}, u32[]{:S(2)}, u32[]{:S(2)}) async-start(bf16[16,64,256]{2,1,0:T(8,128)(2,1)} %get-tuple-element.23), calls=%async_computation.3 | async-start | bytes 1048576 | tf_op jit(solution)/shard_map/all_to_all | solution.py:341
  164.6 2.1 %shard_map.106 = bf16[1024,256]{1,0:T(8,128)(2,1)} custom-call(bf16[1024,256]{1,0:T(8,128)(2,1)S(1)} %bitcast.13, bf16[1024,256]{1,0:T(8,128)(2,1)S(1)} %get-tuple-element.21.summed, f32[64,256]{1,0:T(8,128)S(1)} %get-tuple-element.22.decoded, s32[16,256]{1,0:T(8,128)S(1)} %reshape.11.offsets, bf16[256,256]{1,0:T(8,128)(2,1)S(1)} %copy-done.4, ...), custom_call_target="tpu_custom_call" | custom-call | flops 1610612736 | bytes 2097152 | tf_op jit(solution)/shard_map/pallas_call | solution.py:342
  166.6 8.8 %all-to-all-done.3.parts = bf16[16,64,256]{2,1,0:T(8,128)(2,1)S(1)} async-done(((bf16[16,64,256]{2,1,0:T(8,128)(2,1)}), bf16[16,64,256]{2,1,0:T(8,128)(2,1)S(1)}, u32[]{:S(2)}, u32[]{:S(2)}) %all-to-all-start.3) | async-done | bytes 524320 | tf_op jit(solution)/shard_map/all_to_all | solution.py:341
  175.4 2.1 %shard_map.107 = bf16[1024,256]{1,0:T(8,128)(2,1)} custom-call(bf16[16,64,256]{2,1,0:T(8,128)(2,1)S(1)} %all-to-all-done.3.parts, s32[16,256]{1,0:T(8,128)S(1)} %reshape.11.offsets, bf16[256,256]{1,0:T(8,128)(2,1)S(1)} %copy-done.4, bf16[256,256]{1,0:T(8,128)(2,1)S(1)} %copy-done.2), custom_call_target="tpu_custom_call" | custom-call | flops 1610612736 | bytes 2097152 | tf_op jit(solution)/shard_map/pallas_call | solution.py:343
  (37 shorter events, 0.6 us)
Async XLA Ops:
  3.6 5.4 %copy-start.7 = (s32[1,1,128]{2,1,0:T(1,128)S(1)}, s32[1,1,128]{2,1,0:T(1,128)}, u32[]{:S(2)}) copy-start(s32[1,1,128]{2,1,0:T(1,128)} %param.10) | copy-start | bytes 1540
  3.7 36.2 %all-to-all-start = ((bf16[4,128,1280]{2,1,0:T(8,128)(2,1)}), bf16[4,128,1280]{2,1,0:T(8,128)(2,1)S(1)}, u32[]{:S(2)}, u32[]{:S(2)}) async-start(bf16[4,128,1280]{2,1,0:T(8,128)(2,1)} %shard_map.95), calls=%async_computation | async-start | bytes 2621440 | tf_op jit(solution)/shard_map/all_to_all | solution.py:260
  9.2 36.1 %collective-permute-start.1 = (bf16[8,128]{1,0:T(8,128)(2,1)S(1)}, bf16[8,128]{1,0:T(8,128)(2,1)S(1)}, u32[]{:S(2)}, u32[]{:S(2)}) collective-permute-start(bf16[8,128]{1,0:T(8,128)(2,1)S(1)} %broadcast_in_dim.29), channel_id=1, source_target_pairs={{0,28},{1,29},{2,30},{3,31},{4,0},{5,1},{6,2},{7,3},{8,4},{9,5},{1... | collective-permute-start | bytes 6152 | tf_op jit(solution)/shard_map/ppermute | solution.py:256
  11.6 33.8 %collective-permute-start = (bf16[8,128]{1,0:T(8,128)(2,1)S(1)}, bf16[8,128]{1,0:T(8,128)(2,1)S(1)}, u32[]{:S(2)}, u32[]{:S(2)}) collective-permute-start(bf16[8,128]{1,0:T(8,128)(2,1)S(1)} %broadcast_in_dim.29), channel_id=1, source_target_pairs={{0,4},{1,5},{2,6},{3,7},{4,8},{5,9},{6,10},{7,11},{8,12},{9,13},{1... | collective-permute-start | bytes 6152 | tf_op jit(solution)/shard_map/ppermute | solution.py:256
  39.8 42.4 %all-to-all-start.2 = ((bf16[4,128,512]{2,1,0:T(8,128)(2,1)}), bf16[4,128,512]{2,1,0:T(8,128)(2,1)S(1)}, u32[]{:S(2)}, u32[]{:S(2)}) async-start(bf16[4,128,512]{2,1,0:T(8,128)(2,1)} %get-tuple-element.19), calls=%async_computation.2 | async-start | bytes 1048576 | tf_op jit(solution)/shard_map/all_to_all | solution.py:260
  45.5 14.2 %collective-permute-start.4 = (bf16[128,128]{1,0:T(8,128)(2,1)S(1)}, bf16[128,128]{1,0:T(8,128)(2,1)S(1)}, u32[]{:S(2)}, u32[]{:S(2)}) collective-permute-start(bf16[128,128]{1,0:T(8,128)(2,1)S(1)} %maximum_maximum_fusion.rest_0_), channel_id=1, source_target_pairs={{0,3},{1,0},{2,1},{3,2},{4,7},{5,4},{6,5},{7,6},{8,11},{9,8},{10,9... | collective-permute-start | bytes 98312 | tf_op jit(solution)/shard_map/ppermute | solution.py:252
  49.8 9.9 %collective-permute-start.3 = (bf16[128,128]{1,0:T(8,128)(2,1)S(1)}, bf16[128,128]{1,0:T(8,128)(2,1)S(1)}, u32[]{:S(2)}, u32[]{:S(2)}) collective-permute-start(bf16[128,128]{1,0:T(8,128)(2,1)S(1)} %maximum_maximum_fusion.rest_0_), channel_id=1, source_target_pairs={{0,2},{1,3},{2,0},{3,1},{4,6},{5,7},{6,4},{7,5},{8,10},{9,11},{10,... | collective-permute-start | bytes 98312 | tf_op jit(solution)/shard_map/ppermute | solution.py:252
  51.7 8.2 %collective-permute-start.2 = (bf16[128,128]{1,0:T(8,128)(2,1)S(1)}, bf16[128,128]{1,0:T(8,128)(2,1)S(1)}, u32[]{:S(2)}, u32[]{:S(2)}) collective-permute-start(bf16[128,128]{1,0:T(8,128)(2,1)S(1)} %maximum_maximum_fusion.rest_0_), channel_id=1, source_target_pairs={{0,1},{1,2},{2,3},{3,0},{4,5},{5,6},{6,7},{7,4},{8,9},{9,10},{10,1... | collective-permute-start | bytes 98312 | tf_op jit(solution)/shard_map/ppermute | solution.py:252
  60.5 19.2 %copy-start.8 = (bf16[128,512]{1,0:T(8,128)(2,1)S(1)}, bf16[128,512]{1,0:T(8,128)(2,1)}, u32[]{:S(2)}) copy-start(bf16[128,512]{1,0:T(8,128)(2,1)} %get-tuple-element.18) | copy-start | bytes 393220
  61.8 33.5 %copy-start = (bf16[128,512]{1,0:T(8,128)(2,1)S(1)}, bf16[128,512]{1,0:T(8,128)(2,1)}, u32[]{:S(2)}) copy-start(bf16[128,512]{1,0:T(8,128)(2,1)} %get-tuple-element.15.rest_0_) | copy-start | bytes 393220
  61.8 33.5 %collective-permute-start.5 = (bf16[512,256]{1,0:T(8,128)(2,1)}, bf16[512,256]{1,0:T(8,128)(2,1)S(1)}, u32[]{:S(2)}, u32[]{:S(2)}) collective-permute-start(bf16[512,256]{1,0:T(8,128)(2,1)} %get-tuple-element.14), channel_id=1, source_target_pairs={{0,4},{1,5},{2,6},{3,7},{4,8},{5,9},{6,10},{7,11},{8,12},{9,13},{1... | collective-permute-start | bytes 786440 | tf_op jit(solution)/shard_map/ppermute | solution.py:256
  66.6 35.0 %collective-permute-start.12 = (bf16[512,256]{1,0:T(8,128)(2,1)}, bf16[512,256]{1,0:T(8,128)(2,1)S(1)}, u32[]{:S(2)}, u32[]{:S(2)}) collective-permute-start(bf16[512,256]{1,0:T(8,128)(2,1)} %get-tuple-element.20), channel_id=1, source_target_pairs={{0,28},{1,29},{2,30},{3,31},{4,0},{5,1},{6,2},{7,3},{8,4},{9,5},{1... | collective-permute-start | bytes 786440 | tf_op jit(solution)/shard_map/ppermute | solution.py:256
  68.5 21.3 %collective-permute-start.6 = (bf16[128,512]{1,0:T(8,128)(2,1)}, bf16[128,512]{1,0:T(8,128)(2,1)S(1)}, u32[]{:S(2)}, u32[]{:S(2)}) collective-permute-start(bf16[128,512]{1,0:T(8,128)(2,1)} %get-tuple-element.16), channel_id=1, source_target_pairs={{0,1},{1,2},{2,3},{3,0},{4,5},{5,6},{6,7},{7,4},{8,9},{9,10},{10,1... | collective-permute-start | bytes 393224 | tf_op jit(solution)/shard_map/ppermute | solution.py:252
  74.6 15.2 %collective-permute-start.7 = (bf16[128,512]{1,0:T(8,128)(2,1)}, bf16[128,512]{1,0:T(8,128)(2,1)S(1)}, u32[]{:S(2)}, u32[]{:S(2)}) collective-permute-start(bf16[128,512]{1,0:T(8,128)(2,1)} %get-tuple-element.17), channel_id=1, source_target_pairs={{0,2},{1,3},{2,0},{3,1},{4,6},{5,7},{6,4},{7,5},{8,10},{9,11},{10,... | collective-permute-start | bytes 393224 | tf_op jit(solution)/shard_map/ppermute | solution.py:252
  79.7 15.5 %collective-permute-start.8 = (bf16[128,512]{1,0:T(8,128)(2,1)S(1)}, bf16[128,512]{1,0:T(8,128)(2,1)S(1)}, u32[]{:S(2)}, u32[]{:S(2)}) collective-permute-start(bf16[128,512]{1,0:T(8,128)(2,1)S(1)} %copy-done.8), channel_id=1, source_target_pairs={{0,3},{1,0},{2,1},{3,2},{4,7},{5,4},{6,5},{7,6},{8,11},{9,8},{10,9... | collective-permute-start | bytes 393224 | tf_op jit(solution)/shard_map/ppermute | solution.py:252
  82.2 38.2 %all-to-all-start.1 = ((bf16[4,128,768]{2,1,0:T(8,128)(2,1)}), bf16[4,128,768]{2,1,0:T(8,128)(2,1)S(1)}, u32[]{:S(2)}, u32[]{:S(2)}) async-start(bf16[4,128,768]{2,1,0:T(8,128)(2,1)} %get-tuple-element.13), calls=%async_computation.1 | async-start | bytes 1572864 | tf_op jit(solution)/shard_map/all_to_all | solution.py:260
  95.7 16.0 %collective-permute-start.9 = (bf16[1024,256]{1,0:T(8,128)(2,1)S(1)}, bf16[1024,256]{1,0:T(8,128)(2,1)S(1)}, u32[]{:S(2)}, u32[]{:S(2)}) collective-permute-start(bf16[1024,256]{1,0:T(8,128)(2,1)S(1)} %shard_map.99), channel_id=1, source_target_pairs={{0,4},{1,5},{2,6},{3,7},{4,8},{5,9},{6,10},{7,11},{8,12},{9,13},{1... | collective-permute-start | bytes 1572872 | tf_op jit(solution)/shard_map/ppermute | solution.py:256
  102.0 16.0 %collective-permute-start.13 = (bf16[1024,256]{1,0:T(8,128)(2,1)S(1)}, bf16[1024,256]{1,0:T(8,128)(2,1)S(1)}, u32[]{:S(2)}, u32[]{:S(2)}) collective-permute-start(bf16[1024,256]{1,0:T(8,128)(2,1)S(1)} %shard_map.102), channel_id=1, source_target_pairs={{0,28},{1,29},{2,30},{3,31},{4,0},{5,1},{6,2},{7,3},{8,4},{9,5},{1... | collective-permute-start | bytes 1572872 | tf_op jit(solution)/shard_map/ppermute | solution.py:256
  112.1 15.6 %collective-permute-start.10 = (bf16[1024,256]{1,0:T(8,128)(2,1)S(1)}, bf16[1024,256]{1,0:T(8,128)(2,1)}, u32[]{:S(2)}, u32[]{:S(2)}) collective-permute-start(bf16[1024,256]{1,0:T(8,128)(2,1)S(1)} %shard_map.100), channel_id=1, source_target_pairs={{0,4},{1,5},{2,6},{3,7},{4,8},{5,9},{6,10},{7,11},{8,12},{9,13},{1... | collective-permute-start | bytes 1572872 | tf_op jit(solution)/shard_map/ppermute | solution.py:256
  118.5 16.6 %collective-permute-start.14 = (bf16[1024,256]{1,0:T(8,128)(2,1)S(1)}, bf16[1024,256]{1,0:T(8,128)(2,1)S(1)}, u32[]{:S(2)}, u32[]{:S(2)}) collective-permute-start(bf16[1024,256]{1,0:T(8,128)(2,1)S(1)} %shard_map.103), channel_id=1, source_target_pairs={{0,28},{1,29},{2,30},{3,31},{4,0},{5,1},{6,2},{7,3},{8,4},{9,5},{1... | collective-permute-start | bytes 1572872 | tf_op jit(solution)/shard_map/ppermute | solution.py:256
  129.2 8.3 %copy-start.6 = (s32[1,16,4]{1,2,0:T(4,128)S(1)}, s32[1,16,4]{1,2,0:T(4,128)}, u32[]{:S(2)}) copy-start(s32[1,16,4]{1,2,0:T(4,128)} %param.11) | copy-start | bytes 772
  129.2 18.7 %copy-start.2 = (bf16[256,256]{1,0:T(8,128)(2,1)S(1)}, bf16[256,256]{1,0:T(8,128)(2,1)}, u32[]{:S(2)}) copy-start(bf16[256,256]{1,0:T(8,128)(2,1)} %constant.12.clone.low) | copy-start | bytes 393220
  129.2 12.5 %collective-permute-start.11 = (bf16[1024,256]{1,0:T(8,128)(2,1)S(1)}, bf16[1024,256]{1,0:T(8,128)(2,1)}, u32[]{:S(2)}, u32[]{:S(2)}) collective-permute-start(bf16[1024,256]{1,0:T(8,128)(2,1)S(1)} %shard_map.101), channel_id=1, source_target_pairs={{0,4},{1,5},{2,6},{3,7},{4,8},{5,9},{6,10},{7,11},{8,12},{9,13},{1... | collective-permute-start | bytes 1572872 | tf_op jit(solution)/shard_map/ppermute | solution.py:256
  135.5 12.4 %collective-permute-start.15 = (bf16[1024,256]{1,0:T(8,128)(2,1)S(1)}, bf16[1024,256]{1,0:T(8,128)(2,1)}, u32[]{:S(2)}, u32[]{:S(2)}) collective-permute-start(bf16[1024,256]{1,0:T(8,128)(2,1)S(1)} %shard_map.104), channel_id=1, source_target_pairs={{0,28},{1,29},{2,30},{3,31},{4,0},{5,1},{6,2},{7,3},{8,4},{9,5},{1... | collective-permute-start | bytes 1572872 | tf_op jit(solution)/shard_map/ppermute | solution.py:256
  147.9 1.0 copy-start.1
  148.9 0.9 copy-start.3
  149.8 0.9 copy-start.5
  150.8 13.8 %copy-start.4 = (bf16[256,256]{1,0:T(8,128)(2,1)S(1)}, bf16[256,256]{1,0:T(8,128)(2,1)}, u32[]{:S(2)}) copy-start(bf16[256,256]{1,0:T(8,128)(2,1)} %constant.11.clone.high) | copy-start | bytes 393220
  155.4 20.0 %all-to-all-start.3 = ((bf16[16,64,256]{2,1,0:T(8,128)(2,1)}), bf16[16,64,256]{2,1,0:T(8,128)(2,1)S(1)}, u32[]{:S(2)}, u32[]{:S(2)}) async-start(bf16[16,64,256]{2,1,0:T(8,128)(2,1)} %get-tuple-element.23), calls=%async_computation.3 | async-start | bytes 1048576 | tf_op jit(solution)/shard_map/all_to_all | solution.py:341

commit v2 on v1

--- a/solution.py
+++ b/solution.py
@@ -67,10 +67,6 @@
     deep = exchanged.shape[0]
     z = lax.axis_index("shard") % deep
     return jnp.concatenate([exchanged[(z - k + deep) % deep, :, start : start + size] for k in range(deep)], axis=0)
-
-
-def joined(parts, start, size):
-    return jnp.concatenate([part[:, start : start + size] for part in parts], axis=0)
 
 
 def fetch(rows, deep, width, moves, sem):
@@ -98,17 +94,11 @@
         copy.wait()
 
 
-def late_kernel(rows, *rest):
-    third, (second, last, sem) = rest[:-3], rest[-3:]
-    deep = len(third)
-    width = last.shape[2] // 3
-    me = lax.axis_index("shard") % deep
+def late_kernel(rows, third, second, first, own, sem):
+    deep = own.shape[0]
+    width = own.shape[2]
     moves = []
-    for k in range(deep):
-        z = (me + k) % deep
-        for j, owner in enumerate((3, -3)):
-            moves.append((owner, z, third[k].at[:, pl.ds(j * width, width)]))
-    for target, owners in ((second, (2, -2)), (last, (1, -1, 0))):
+    for target, owners in ((third, (3, -3)), (second, (2, -2)), (first, (1, -1)), (own, (0,))):
         for z in range(deep):
             for j, owner in enumerate(owners):
                 moves.append((owner, z, target.at[z, :, pl.ds(j * width, width)]))
@@ -142,11 +132,9 @@
     down[...] = dot(weights[half:], columns, dims).astype(jnp.bfloat16)
 
 
-def near_kernel(start, top, pieces, weights, received, *rest):
-    parts, out = rest[:-1], rest[-1]
+def near_kernel(start, top, weights, received, exchanged, out):
     width = out.shape[1]
-    columns = joined(parts, start, width) if pieces else gathered(parts[0], start, width)
-    total = dot(weights[...], columns, ((1,), (0,)))
+    total = dot(weights[...], gathered(exchanged, start, width), ((1,), (0,)))
     rows = received.shape[0]
     if rows == out.shape[0]:
         out[...] = (total + received[...].astype(jnp.float32)).astype(jnp.bfloat16)
@@ -156,18 +144,27 @@
         out[other] = total[other].astype(jnp.bfloat16)
 
 
-def forward_kernel(weights, exchanged, up, down, momentum, offsets, high, low, ones, summed, decoded, sent, packed):
+def base_kernel(weights, exchanged, momentum, offsets, *rest):
+    tables, (product, kept, offsets_out, *tables_out) = rest[: len(rest) // 2 - 1], rest[len(rest) // 2 - 1 :]
+    product[...] = dot(weights[...], gathered(exchanged, 0, product.shape[1]), ((1,), (0,)))
+    kept[...] = momentum[...]
+    offsets_out[...] = offsets[...]
+    for table, out in zip(tables, tables_out):
+        out[...] = table[...]
+
+
+def forward_kernel(product, up, down, momentum, offsets, high, low, ones, summed, decoded, sent, packed, held, sem):
     table = (high[...], low[...])
     per = TILE // BLOCK
     rows = TILE // STRIDE
-    width = summed.shape[1]
-    columns = gathered(exchanged, 2 * width, width)
-    for i in range(summed.shape[0] // TILE):
+    copies = []
+    for i in range(product.shape[0] // TILE):
         here = slice(i * TILE, (i + 1) * TILE)
-        total = dot(weights[here], columns, ((1,), (0,)))
-        total = total + up[here].astype(jnp.float32) + down[here].astype(jnp.float32)
+        total = product[here] + up[here].astype(jnp.float32) + down[here].astype(jnp.float32)
         gradient = total.astype(jnp.bfloat16)
-        summed[here] = gradient
+        held[here] = gradient
+        copies.append(pltpu.make_async_copy(held.at[pl.ds(i * TILE, TILE)], summed.at[pl.ds(i * TILE, TILE)], sem.at[i]))
+        copies[-1].start()
         value = BETA * momentum[here].astype(jnp.float32) + gradient.astype(jnp.float32)
         spectrum = right(left(table, value, 1), table, 1)
         kept = jnp.where(selected(offsets[i * per : (i + 1) * per]), spectrum, 0.0)
@@ -189,6 +186,8 @@
     rounded = result.astype(jnp.bfloat16)
     for k in range(sent.shape[0]):
         sent[k] = rounded
+    for copy in copies:
+        copy.wait()
 
 
 def spread_tile(values, offsets):
@@ -291,19 +290,18 @@
         notes.append(along_line(extra, k))
     notes = [notes[0], notes[2], notes[1], notes[3]]
 
-    outs = call(
+    third, second, first, own = call(
         late_kernel,
-        [shaped(tokens, 2 * width)] * deep + [shaped(deep, tokens, 2 * width), shaped(deep, tokens, 3 * width)],
+        [shaped(deep, tokens, 2 * width)] * 3 + [shaped(deep, tokens, width)],
         work,
         (pltpu.SemaphoreType.DMA((7 * deep,)),),
         [apart],
         FULL,
     )(rows)
-    third, second, last = list(outs[:deep]), outs[deep], outs[deep + 1]
-    for k in (2, 1, 3):
-        third[k] = along_line(third[k], k)
+    third = exchange(third)
     second = exchange(second)
-    last = exchange(last)
+    first = exchange(first)
+    own = exchange(own)
 
     weights = call(scale_kernel, shaped(panel, deep * tokens), work)(early, *notes)
     half = panel // 2
@@ -314,30 +312,42 @@
         down = across(down, -1)
         return up, down
 
-    def near(start, top, received, parts):
-        kernel = functools.partial(near_kernel, start, top, len(parts) > 1)
-        return call(kernel, shaped(panel, width), work)(weights, received, *parts)
+    def near(start, top, received, exchanged):
+        kernel = functools.partial(near_kernel, start, top)
+        return call(kernel, shaped(panel, width), work)(weights, received, exchanged)
+
+    def both(up, down, exchanged):
+        return near(0, True, up, exchanged), near(width, False, down, exchanged)
 
     up, down = ring(up, down)
-    up, down = ring(near(0, True, up, third), near(width, False, down, third))
-    up, down = ring(near(0, True, up, [second]), near(width, False, down, [second]))
-    up, down = ring(near(0, True, up, [last]), near(width, False, down, [last]))
+    up, down = ring(*both(up, down, third))
+    up, down = ring(*both(up, down, second))
+    up, down = ring(*both(up, down, first))
 
     high, low = dct_parts()
     ones = jnp.asarray(np.kron(np.eye(TILE // BLOCK), np.ones((BLOCK, BLOCK))), jnp.bfloat16)
     wide = jnp.repeat(offsets[0], BLOCK, axis=1)
     kept = panel // STRIDE
     flops = 6 * 2 * 2 * panel * TILE * TILE
-    summed, decoded, sent = call(
+    tables = (high, low, ones)
+    product, momentum_near, wide_near, *tables_near = call(
+        base_kernel,
+        [shaped(panel, width, dtype=jnp.float32), shaped(panel, width), shaped(*wide.shape, dtype=jnp.int32)]
+        + [shaped(*table.shape) for table in tables],
+        work,
+    )(weights, own, momentum[0], wide, *tables)
+    summed, decoded, sent = pl.pallas_call(
         forward_kernel,
-        (
-            shaped(panel, width),
-            shaped(kept, width, dtype=jnp.float32),
-            shaped(groups, kept, width),
+        out_shape=(shaped(panel, width), shaped(kept, width, dtype=jnp.float32), shaped(groups, kept, width)),
+        out_specs=(apart, whole, whole),
+        scratch_shapes=(
+            pltpu.VMEM((kept, width), jnp.float32),
+            pltpu.VMEM((panel, width), jnp.bfloat16),
+            pltpu.SemaphoreType.DMA((panel // TILE,)),
         ),
-        flops,
-        (pltpu.VMEM((kept, width), jnp.float32),),
-    )(weights, last, up, down, momentum[0], wide, high, low, ones)
+        compiler_params=pltpu.CompilerParams(vmem_limit_bytes=GRANT),
+        cost_estimate=pl.CostEstimate(flops=flops, bytes_accessed=2 << 20, transcendentals=0),
+    )(product, up, down, momentum_near, wide_near, *tables_near)
     parts = lax.all_to_all(sent, "rep", 0, 0, tiled=True)
     residual = call(residual_kernel, shaped(panel, width), flops)(momentum[0], summed, decoded, wide, high, low)
     update = call(update_kernel, shaped(panel, width), flops)(parts, wide, high, low)

time: 179 us -> 184 us (1.028)
  the two profiles are of different devices: /device:TPU:408 before, /device:TPU:1 now
where the time goes in v2:
time: 184 us; the launch traced here: 183 us
  starting transfers between devices  108 us (59%)
  waiting for transfers between devices  48.9 us (27%)
  Pallas kernels  23.1 us (13%)
  local copies, waits for them, and re-layouts  2.28 us (1%)
    ppermute x10, starting transfers between devices, across(): return lax.ppermute(x, 'shard', pairs)  34.9 us
    all_to_all x5, starting transfers between devices, exchange(): return lax.all_to_all(x, 'shard', 0, 0, axis_index_groups=lines, tiled=True)  33.4 us
    all_to_all x1, starting transfers between devices, step(): parts = lax.all_to_all(sent, 'rep', 0, 0, tiled=True)  25.8 us
    all_to_all x5, waiting for transfers between devices, exchange(): return lax.all_to_all(x, 'shard', 0, 0, axis_index_groups=lines, tiled=True)  25.2 us
    ppermute x3, starting transfers between devices, along_line(): return lax.ppermute(x, 'shard', pairs)  13.5 us
    ppermute x10, waiting for transfers between devices, across(): return lax.ppermute(x, 'shard', pairs)  13.3 us
    all_to_all x1, waiting for transfers between devices, step(): parts = lax.all_to_all(sent, 'rep', 0, 0, tiled=True)  7.6 us
    pallas_call x6, Pallas kernels, near(): call(kernel, shaped(panel, width), work)(weights, received, exchanged)  5.84 us
  transfers between devices with their start and end apart: 19, of which 11 were waited for; matrix products, arithmetic and copies ran while one was open for 0% of the time, Pallas kernels for 7%

profile of v2, /device:TPU:1, one launch (start us, length us, event | category | flops | bytes accessed | tf_op | source)
XLA Modules:
  0.0 183.0 jit_solution(12498150094430544191)
XLA Ops:
  0.6 3.0 %shard_map.97 = (bf16[4,128,512]{2,1,0:T(8,128)(2,1)}, bf16[4,128,512]{2,1,0:T(8,128)(2,1)}, bf16[4,128,512]{2,1,0:T(8,128)(2,1)}, bf16[4,128,256]{2,1,0:T(8,128)(2,1)}) custom-call(bf16[128,8192]{1,0:T(8,128)(2,1)} %bitcast.14), custom_call_target="tpu_custom_call" | custom-call | flops 268435456 | bytes 2097152 | tf_op jit(solution)/shard_map/pallas_call | solution.py:293
  3.6 10.8 %all-to-all-start.2 = ((bf16[4,128,512]{2,1,0:T(8,128)(2,1)}), bf16[4,128,512]{2,1,0:T(8,128)(2,1)S(1)}, u32[]{:S(2)}, u32[]{:S(2)}) async-start(bf16[4,128,512]{2,1,0:T(8,128)(2,1)} %get-tuple-element.20), calls=%async_computation.2 | async-start | bytes 1048576 | tf_op jit(solution)/shard_map/all_to_all | solution.py:259
  14.5 3.0 %shard_map.95 = bf16[4,128,1280]{2,1,0:T(8,128)(2,1)} custom-call(bf16[128,8192]{1,0:T(8,128)(2,1)} %bitcast.15, bf16[128,1024]{1,0:T(8,128)(2,1)} %bitcast.16), custom_call_target="tpu_custom_call" | custom-call | flops 268435456 | bytes 2097152 | tf_op jit(solution)/shard_map/pallas_call | solution.py:269
  17.5 8.9 %all-to-all-done.2.exchanged = bf16[4,128,512]{2,1,0:T(8,128)(2,1)S(1)} async-done(((bf16[4,128,512]{2,1,0:T(8,128)(2,1)}), bf16[4,128,512]{2,1,0:T(8,128)(2,1)S(1)}, u32[]{:S(2)}, u32[]{:S(2)}) %all-to-all-start.2) | async-done | bytes 524320 | tf_op jit(solution)/shard_map/all_to_all | solution.py:259
  26.4 4.9 %all-to-all-start = ((bf16[4,128,1280]{2,1,0:T(8,128)(2,1)}), bf16[4,128,1280]{2,1,0:T(8,128)(2,1)S(1)}, u32[]{:S(2)}, u32[]{:S(2)}) async-start(bf16[4,128,1280]{2,1,0:T(8,128)(2,1)} %shard_map.95), calls=%async_computation | async-start | bytes 2621440 | tf_op jit(solution)/shard_map/all_to_all | solution.py:259
  31.3 0.1 fusion.1
  31.4 5.1 %collective-permute-start.1 = (bf16[8,128]{1,0:T(8,128)(2,1)S(1)}, bf16[8,128]{1,0:T(8,128)(2,1)S(1)}, u32[]{:S(2)}, u32[]{:S(2)}) collective-permute-start(bf16[8,128]{1,0:T(8,128)(2,1)S(1)} %broadcast_in_dim.29), channel_id=1, source_target_pairs={{0,28},{1,29},{2,30},{3,31},{4,0},{5,1},{6,2},{7,3},{8,4},{9,5},{1... | collective-permute-start | bytes 6152 | tf_op jit(solution)/shard_map/ppermute | solution.py:255
  36.5 1.9 %collective-permute-start = (bf16[8,128]{1,0:T(8,128)(2,1)S(1)}, bf16[8,128]{1,0:T(8,128)(2,1)S(1)}, u32[]{:S(2)}, u32[]{:S(2)}) collective-permute-start(bf16[8,128]{1,0:T(8,128)(2,1)S(1)} %broadcast_in_dim.29), channel_id=1, source_target_pairs={{0,4},{1,5},{2,6},{3,7},{4,8},{5,9},{6,10},{7,11},{8,12},{9,13},{1... | collective-permute-start | bytes 6152 | tf_op jit(solution)/shard_map/ppermute | solution.py:255
  38.7 3.7 %collective-permute-done = bf16[8,128]{1,0:T(8,128)(2,1)S(1)} collective-permute-done((bf16[8,128]{1,0:T(8,128)(2,1)S(1)}, bf16[8,128]{1,0:T(8,128)(2,1)S(1)}, u32[]{:S(2)}, u32[]{:S(2)}) %collective-permute-start) | collective-permute-done | bytes 2080 | tf_op jit(solution)/shard_map/ppermute | solution.py:255
  42.5 8.6 %all-to-all-done.exchanged = bf16[4,128,1280]{2,1,0:T(8,128)(2,1)S(1)} async-done(((bf16[4,128,1280]{2,1,0:T(8,128)(2,1)}), bf16[4,128,1280]{2,1,0:T(8,128)(2,1)S(1)}, u32[]{:S(2)}, u32[]{:S(2)}) %all-to-all-start) | async-done | bytes 1310752 | tf_op jit(solution)/shard_map/all_to_all | solution.py:259
  51.2 5.8 %all-to-all-start.3 = ((bf16[4,128,512]{2,1,0:T(8,128)(2,1)}), bf16[4,128,512]{2,1,0:T(8,128)(2,1)S(1)}, u32[]{:S(2)}, u32[]{:S(2)}) async-start(bf16[4,128,512]{2,1,0:T(8,128)(2,1)} %get-tuple-element.21), calls=%async_computation.3 | async-start | bytes 1048576 | tf_op jit(solution)/shard_map/all_to_all | solution.py:259
  57.0 5.5 %collective-permute-start.4 = (bf16[128,128]{1,0:T(8,128)(2,1)S(1)}, bf16[128,128]{1,0:T(8,128)(2,1)S(1)}, u32[]{:S(2)}, u32[]{:S(2)}) collective-permute-start(bf16[128,128]{1,0:T(8,128)(2,1)S(1)} %maximum_maximum_fusion.rest_0_), channel_id=1, source_target_pairs={{0,3},{1,0},{2,1},{3,2},{4,7},{5,4},{6,5},{7,6},{8,11},{9,8},{10,9... | collective-permute-start | bytes 98312 | tf_op jit(solution)/shard_map/ppermute | solution.py:251
  62.5 4.0 %collective-permute-start.3 = (bf16[128,128]{1,0:T(8,128)(2,1)S(1)}, bf16[128,128]{1,0:T(8,128)(2,1)S(1)}, u32[]{:S(2)}, u32[]{:S(2)}) collective-permute-start(bf16[128,128]{1,0:T(8,128)(2,1)S(1)} %maximum_maximum_fusion.rest_0_), channel_id=1, source_target_pairs={{0,2},{1,3},{2,0},{3,1},{4,6},{5,7},{6,4},{7,5},{8,10},{9,11},{10,... | collective-permute-start | bytes 98312 | tf_op jit(solution)/shard_map/ppermute | solution.py:251
  66.5 4.0 %collective-permute-start.2 = (bf16[128,128]{1,0:T(8,128)(2,1)S(1)}, bf16[128,128]{1,0:T(8,128)(2,1)S(1)}, u32[]{:S(2)}, u32[]{:S(2)}) collective-permute-start(bf16[128,128]{1,0:T(8,128)(2,1)S(1)} %maximum_maximum_fusion.rest_0_), channel_id=1, source_target_pairs={{0,1},{1,2},{2,3},{3,0},{4,5},{5,6},{6,7},{7,4},{8,9},{9,10},{10,1... | collective-permute-start | bytes 98312 | tf_op jit(solution)/shard_map/ppermute | solution.py:251
  70.5 0.6 collective-permute-done.3.rest_2_
  71.1 2.2 %collective-permute-done.2.rest_1_ = bf16[128,128]{1,0:T(8,128)(2,1)S(1)} collective-permute-done((bf16[128,128]{1,0:T(8,128)(2,1)S(1)}, bf16[128,128]{1,0:T(8,128)(2,1)S(1)}, u32[]{:S(2)}, u32[]{:S(2)}) %collective-permute-start.2) | collective-permute-done | bytes 32800 | tf_op jit(solution)/shard_map/ppermute | solution.py:251
  73.3 0.6 shard_map.96.weights
  73.8 0.5 shard_map.99
  74.3 3.2 %collective-permute-start.5 = (bf16[512,256]{1,0:T(8,128)(2,1)S(1)}, bf16[512,256]{1,0:T(8,128)(2,1)S(1)}, u32[]{:S(2)}, u32[]{:S(2)}) collective-permute-start(bf16[512,256]{1,0:T(8,128)(2,1)S(1)} %get-tuple-element.19), channel_id=1, source_target_pairs={{0,4},{1,5},{2,6},{3,7},{4,8},{5,9},{6,10},{7,11},{8,12},{9,13},{1... | collective-permute-start | bytes 786440 | tf_op jit(solution)/shard_map/ppermute | solution.py:255
  77.5 3.8 %collective-permute-start.9 = (bf16[512,256]{1,0:T(8,128)(2,1)S(1)}, bf16[512,256]{1,0:T(8,128)(2,1)S(1)}, u32[]{:S(2)}, u32[]{:S(2)}) collective-permute-start(bf16[512,256]{1,0:T(8,128)(2,1)S(1)} %get-tuple-element.23), channel_id=1, source_target_pairs={{0,28},{1,29},{2,30},{3,31},{4,0},{5,1},{6,2},{7,3},{8,4},{9,5},{1... | collective-permute-start | bytes 786440 | tf_op jit(solution)/shard_map/ppermute | solution.py:255
  81.3 2.1 %collective-permute-done.5.received = bf16[512,256]{1,0:T(8,128)(2,1)S(1)} collective-permute-done((bf16[512,256]{1,0:T(8,128)(2,1)S(1)}, bf16[512,256]{1,0:T(8,128)(2,1)S(1)}, u32[]{:S(2)}, u32[]{:S(2)}) %collective-permute-start.5) | collective-permute-done | bytes 262176 | tf_op jit(solution)/shard_map/ppermute | solution.py:255
  83.4 1.2 shard_map.100
  84.7 1.9 %collective-permute-start.6 = (bf16[1024,256]{1,0:T(8,128)(2,1)}, bf16[1024,256]{1,0:T(8,128)(2,1)S(1)}, u32[]{:S(2)}, u32[]{:S(2)}) collective-permute-start(bf16[1024,256]{1,0:T(8,128)(2,1)} %shard_map.100), channel_id=1, source_target_pairs={{0,4},{1,5},{2,6},{3,7},{4,8},{5,9},{6,10},{7,11},{8,12},{9,13},{1... | collective-permute-start | bytes 1572872 | tf_op jit(solution)/shard_map/ppermute | solution.py:255
  86.6 1.3 shard_map.103
  87.9 4.6 %collective-permute-start.10 = (bf16[1024,256]{1,0:T(8,128)(2,1)}, bf16[1024,256]{1,0:T(8,128)(2,1)S(1)}, u32[]{:S(2)}, u32[]{:S(2)}) collective-permute-start(bf16[1024,256]{1,0:T(8,128)(2,1)} %shard_map.103), channel_id=1, source_target_pairs={{0,28},{1,29},{2,30},{3,31},{4,0},{5,1},{6,2},{7,3},{8,4},{9,5},{1... | collective-permute-start | bytes 1572872 | tf_op jit(solution)/shard_map/ppermute | solution.py:255
  92.4 5.0 %all-to-all-start.4 = ((bf16[4,128,512]{2,1,0:T(8,128)(2,1)}), bf16[4,128,512]{2,1,0:T(8,128)(2,1)S(1)}, u32[]{:S(2)}, u32[]{:S(2)}) async-start(bf16[4,128,512]{2,1,0:T(8,128)(2,1)} %get-tuple-element.22), calls=%async_computation.4 | async-start | bytes 1048576 | tf_op jit(solution)/shard_map/all_to_all | solution.py:259
  97.4 1.2 shard_map.101
  98.7 1.9 %collective-permute-start.7 = (bf16[1024,256]{1,0:T(8,128)(2,1)}, bf16[1024,256]{1,0:T(8,128)(2,1)S(1)}, u32[]{:S(2)}, u32[]{:S(2)}) collective-permute-start(bf16[1024,256]{1,0:T(8,128)(2,1)} %shard_map.101), channel_id=1, source_target_pairs={{0,4},{1,5},{2,6},{3,7},{4,8},{5,9},{6,10},{7,11},{8,12},{9,13},{1... | collective-permute-start | bytes 1572872 | tf_op jit(solution)/shard_map/ppermute | solution.py:255
  100.6 0.1 collective-permute-done.10.received
  100.7 1.2 shard_map.104
  101.9 5.2 %collective-permute-start.11 = (bf16[1024,256]{1,0:T(8,128)(2,1)}, bf16[1024,256]{1,0:T(8,128)(2,1)S(1)}, u32[]{:S(2)}, u32[]{:S(2)}) collective-permute-start(bf16[1024,256]{1,0:T(8,128)(2,1)} %shard_map.104), channel_id=1, source_target_pairs={{0,28},{1,29},{2,30},{3,31},{4,0},{5,1},{6,2},{7,3},{8,4},{9,5},{1... | collective-permute-start | bytes 1572872 | tf_op jit(solution)/shard_map/ppermute | solution.py:255
  107.1 6.2 %collective-permute-done.7.received = bf16[1024,256]{1,0:T(8,128)(2,1)S(1)} collective-permute-done((bf16[1024,256]{1,0:T(8,128)(2,1)}, bf16[1024,256]{1,0:T(8,128)(2,1)S(1)}, u32[]{:S(2)}, u32[]{:S(2)}) %collective-permute-start.7) | collective-permute-done | bytes 524320 | tf_op jit(solution)/shard_map/ppermute | solution.py:255
  113.4 0.5 shard_map.102
  113.8 2.1 %collective-permute-start.8 = (bf16[1024,256]{1,0:T(8,128)(2,1)S(1)}, bf16[1024,256]{1,0:T(8,128)(2,1)}, u32[]{:S(2)}, u32[]{:S(2)}) collective-permute-start(bf16[1024,256]{1,0:T(8,128)(2,1)S(1)} %shard_map.102), channel_id=1, source_target_pairs={{0,4},{1,5},{2,6},{3,7},{4,8},{5,9},{6,10},{7,11},{8,12},{9,13},{1... | collective-permute-start | bytes 1572872 | tf_op jit(solution)/shard_map/ppermute | solution.py:255
  115.9 1.2 collective-permute-done.11.received
  117.0 0.8 copy-done.1
  117.8 1.0 copy-done.2
  118.9 0.4 shard_map.105
  119.3 5.2 %collective-permute-start.12 = (bf16[1024,256]{1,0:T(8,128)(2,1)S(1)}, bf16[1024,256]{1,0:T(8,128)(2,1)}, u32[]{:S(2)}, u32[]{:S(2)}) collective-permute-start(bf16[1024,256]{1,0:T(8,128)(2,1)S(1)} %shard_map.105), channel_id=1, source_target_pairs={{0,28},{1,29},{2,30},{3,31},{4,0},{5,1},{6,2},{7,3},{8,4},{9,5},{1... | collective-permute-start | bytes 1572872 | tf_op jit(solution)/shard_map/ppermute | solution.py:255
  124.5 6.9 %all-to-all-start.1 = ((bf16[4,128,256]{2,1,0:T(8,128)(2,1)}), bf16[4,128,256]{2,1,0:T(8,128)(2,1)S(1)}, u32[]{:S(2)}, u32[]{:S(2)}) async-start(bf16[4,128,256]{2,1,0:T(8,128)(2,1)} %get-tuple-element.17), calls=%async_computation.1 | async-start | bytes 524288 | tf_op jit(solution)/shard_map/all_to_all | solution.py:259
  131.6 0.1 reshape.11.offsets
  131.7 7.7 %all-to-all-done.1.exchanged = bf16[4,128,256]{2,1,0:T(8,128)(2,1)S(1)} async-done(((bf16[4,128,256]{2,1,0:T(8,128)(2,1)}), bf16[4,128,256]{2,1,0:T(8,128)(2,1)S(1)}, u32[]{:S(2)}, u32[]{:S(2)}) %all-to-all-start.1) | async-done | bytes 262176 | tf_op jit(solution)/shard_map/all_to_all | solution.py:259
  139.4 0.5 shard_map.98
  139.9 5.6 %shard_map.106 = (bf16[1024,256]{1,0:T(8,128)(2,1)S(1)}, f32[64,256]{1,0:T(8,128)S(1)}, bf16[16,64,256]{2,1,0:T(8,128)(2,1)}) custom-call(f32[1024,256]{1,0:T(8,128)S(1)} %get-tuple-element.18.product, bf16[1024,256]{1,0:T(8,128)(2,1)} %collective-permute-done.8.up, bf16[1024,256]{1,0:T(8,128)(2,1)} %collective-permute-done.12.down, ...), custom_call_target="tpu_custom_call" | custom-call | flops 1610612736 | bytes 2097152 | tf_op jit(solution)/shard_map/pallas_call | solution.py:339
  145.5 25.8 %all-to-all-start.5 = ((bf16[16,64,256]{2,1,0:T(8,128)(2,1)}), bf16[16,64,256]{2,1,0:T(8,128)(2,1)S(1)}, u32[]{:S(2)}, u32[]{:S(2)}) async-start(bf16[16,64,256]{2,1,0:T(8,128)(2,1)} %get-tuple-element.31), calls=%async_computation.5 | async-start | bytes 1048576 | tf_op jit(solution)/shard_map/all_to_all | solution.py:351
  171.2 2.1 %shard_map.107 = bf16[1024,256]{1,0:T(8,128)(2,1)} custom-call(bf16[1024,256]{1,0:T(8,128)(2,1)S(1)} %bitcast.13, bf16[1024,256]{1,0:T(8,128)(2,1)S(1)} %get-tuple-element.29.summed, f32[64,256]{1,0:T(8,128)S(1)} %get-tuple-element.30.decoded, s32[16,256]{1,0:T(8,128)S(1)} %reshape.11.offsets, bf16[256,256]{1,0:T(8,128)(2,1)S(1)} %copy-done.4, ...), custom_call_target="tpu_custom_call" | custom-call | flops 1610612736 | bytes 2097152 | tf_op jit(solution)/shard_map/pallas_call | solution.py:352
  173.3 7.6 %all-to-all-done.5.parts = bf16[16,64,256]{2,1,0:T(8,128)(2,1)S(1)} async-done(((bf16[16,64,256]{2,1,0:T(8,128)(2,1)}), bf16[16,64,256]{2,1,0:T(8,128)(2,1)S(1)}, u32[]{:S(2)}, u32[]{:S(2)}) %all-to-all-start.5) | async-done | bytes 524320 | tf_op jit(solution)/shard_map/all_to_all | solution.py:351
  180.9 2.1 %shard_map.108 = bf16[1024,256]{1,0:T(8,128)(2,1)} custom-call(bf16[16,64,256]{2,1,0:T(8,128)(2,1)S(1)} %all-to-all-done.5.parts, s32[16,256]{1,0:T(8,128)S(1)} %reshape.11.offsets, bf16[256,256]{1,0:T(8,128)(2,1)S(1)} %copy-done.4, bf16[256,256]{1,0:T(8,128)(2,1)S(1)} %copy-done.3), custom_call_target="tpu_custom_call" | custom-call | flops 1610612736 | bytes 2097152 | tf_op jit(solution)/shard_map/pallas_call | solution.py:353
  (34 shorter events, 0.6 us)
Async XLA Ops:
  3.6 22.8 %all-to-all-start.2 = ((bf16[4,128,512]{2,1,0:T(8,128)(2,1)}), bf16[4,128,512]{2,1,0:T(8,128)(2,1)S(1)}, u32[]{:S(2)}, u32[]{:S(2)}) async-start(bf16[4,128,512]{2,1,0:T(8,128)(2,1)} %get-tuple-element.20), calls=%async_computation.2 | async-start | bytes 1048576 | tf_op jit(solution)/shard_map/all_to_all | solution.py:259
  17.5 13.8 %copy-start.7 = (s32[1,1,128]{2,1,0:T(1,128)S(1)}, s32[1,1,128]{2,1,0:T(1,128)}, u32[]{:S(2)}) copy-start(s32[1,1,128]{2,1,0:T(1,128)} %param.10) | copy-start | bytes 1540
  26.4 24.8 %all-to-all-start = ((bf16[4,128,1280]{2,1,0:T(8,128)(2,1)}), bf16[4,128,1280]{2,1,0:T(8,128)(2,1)S(1)}, u32[]{:S(2)}, u32[]{:S(2)}) async-start(bf16[4,128,1280]{2,1,0:T(8,128)(2,1)} %shard_map.95), calls=%async_computation | async-start | bytes 2621440 | tf_op jit(solution)/shard_map/all_to_all | solution.py:259
  31.4 7.2 %collective-permute-start.1 = (bf16[8,128]{1,0:T(8,128)(2,1)S(1)}, bf16[8,128]{1,0:T(8,128)(2,1)S(1)}, u32[]{:S(2)}, u32[]{:S(2)}) collective-permute-start(bf16[8,128]{1,0:T(8,128)(2,1)S(1)} %broadcast_in_dim.29), channel_id=1, source_target_pairs={{0,28},{1,29},{2,30},{3,31},{4,0},{5,1},{6,2},{7,3},{8,4},{9,5},{1... | collective-permute-start | bytes 6152 | tf_op jit(solution)/shard_map/ppermute | solution.py:255
  36.5 5.8 %collective-permute-start = (bf16[8,128]{1,0:T(8,128)(2,1)S(1)}, bf16[8,128]{1,0:T(8,128)(2,1)S(1)}, u32[]{:S(2)}, u32[]{:S(2)}) collective-permute-start(bf16[8,128]{1,0:T(8,128)(2,1)S(1)} %broadcast_in_dim.29), channel_id=1, source_target_pairs={{0,4},{1,5},{2,6},{3,7},{4,8},{5,9},{6,10},{7,11},{8,12},{9,13},{1... | collective-permute-start | bytes 6152 | tf_op jit(solution)/shard_map/ppermute | solution.py:255
  51.2 41.3 %all-to-all-start.3 = ((bf16[4,128,512]{2,1,0:T(8,128)(2,1)}), bf16[4,128,512]{2,1,0:T(8,128)(2,1)S(1)}, u32[]{:S(2)}, u32[]{:S(2)}) async-start(bf16[4,128,512]{2,1,0:T(8,128)(2,1)} %get-tuple-element.21), calls=%async_computation.3 | async-start | bytes 1048576 | tf_op jit(solution)/shard_map/all_to_all | solution.py:259
  57.0 13.5 %collective-permute-start.4 = (bf16[128,128]{1,0:T(8,128)(2,1)S(1)}, bf16[128,128]{1,0:T(8,128)(2,1)S(1)}, u32[]{:S(2)}, u32[]{:S(2)}) collective-permute-start(bf16[128,128]{1,0:T(8,128)(2,1)S(1)} %maximum_maximum_fusion.rest_0_), channel_id=1, source_target_pairs={{0,3},{1,0},{2,1},{3,2},{4,7},{5,4},{6,5},{7,6},{8,11},{9,8},{10,9... | collective-permute-start | bytes 98312 | tf_op jit(solution)/shard_map/ppermute | solution.py:251
  62.5 8.6 %collective-permute-start.3 = (bf16[128,128]{1,0:T(8,128)(2,1)S(1)}, bf16[128,128]{1,0:T(8,128)(2,1)S(1)}, u32[]{:S(2)}, u32[]{:S(2)}) collective-permute-start(bf16[128,128]{1,0:T(8,128)(2,1)S(1)} %maximum_maximum_fusion.rest_0_), channel_id=1, source_target_pairs={{0,2},{1,3},{2,0},{3,1},{4,6},{5,7},{6,4},{7,5},{8,10},{9,11},{10,... | collective-permute-start | bytes 98312 | tf_op jit(solution)/shard_map/ppermute | solution.py:251
  66.5 6.8 %collective-permute-start.2 = (bf16[128,128]{1,0:T(8,128)(2,1)S(1)}, bf16[128,128]{1,0:T(8,128)(2,1)S(1)}, u32[]{:S(2)}, u32[]{:S(2)}) collective-permute-start(bf16[128,128]{1,0:T(8,128)(2,1)S(1)} %maximum_maximum_fusion.rest_0_), channel_id=1, source_target_pairs={{0,1},{1,2},{2,3},{3,0},{4,5},{5,6},{6,7},{7,4},{8,9},{9,10},{10,1... | collective-permute-start | bytes 98312 | tf_op jit(solution)/shard_map/ppermute | solution.py:251
  74.3 9.1 %collective-permute-start.5 = (bf16[512,256]{1,0:T(8,128)(2,1)S(1)}, bf16[512,256]{1,0:T(8,128)(2,1)S(1)}, u32[]{:S(2)}, u32[]{:S(2)}) collective-permute-start(bf16[512,256]{1,0:T(8,128)(2,1)S(1)} %get-tuple-element.19), channel_id=1, source_target_pairs={{0,4},{1,5},{2,6},{3,7},{4,8},{5,9},{6,10},{7,11},{8,12},{9,13},{1... | collective-permute-start | bytes 786440 | tf_op jit(solution)/shard_map/ppermute | solution.py:255
  77.5 9.1 %collective-permute-start.9 = (bf16[512,256]{1,0:T(8,128)(2,1)S(1)}, bf16[512,256]{1,0:T(8,128)(2,1)S(1)}, u32[]{:S(2)}, u32[]{:S(2)}) collective-permute-start(bf16[512,256]{1,0:T(8,128)(2,1)S(1)} %get-tuple-element.23), channel_id=1, source_target_pairs={{0,28},{1,29},{2,30},{3,31},{4,0},{5,1},{6,2},{7,3},{8,4},{9,5},{1... | collective-permute-start | bytes 786440 | tf_op jit(solution)/shard_map/ppermute | solution.py:255
  84.7 12.7 %collective-permute-start.6 = (bf16[1024,256]{1,0:T(8,128)(2,1)}, bf16[1024,256]{1,0:T(8,128)(2,1)S(1)}, u32[]{:S(2)}, u32[]{:S(2)}) collective-permute-start(bf16[1024,256]{1,0:T(8,128)(2,1)} %shard_map.100), channel_id=1, source_target_pairs={{0,4},{1,5},{2,6},{3,7},{4,8},{5,9},{6,10},{7,11},{8,12},{9,13},{1... | collective-permute-start | bytes 1572872 | tf_op jit(solution)/shard_map/ppermute | solution.py:255
  87.9 12.8 %collective-permute-start.10 = (bf16[1024,256]{1,0:T(8,128)(2,1)}, bf16[1024,256]{1,0:T(8,128)(2,1)S(1)}, u32[]{:S(2)}, u32[]{:S(2)}) collective-permute-start(bf16[1024,256]{1,0:T(8,128)(2,1)} %shard_map.103), channel_id=1, source_target_pairs={{0,28},{1,29},{2,30},{3,31},{4,0},{5,1},{6,2},{7,3},{8,4},{9,5},{1... | collective-permute-start | bytes 1572872 | tf_op jit(solution)/shard_map/ppermute | solution.py:255
  92.4 14.7 %all-to-all-start.4 = ((bf16[4,128,512]{2,1,0:T(8,128)(2,1)}), bf16[4,128,512]{2,1,0:T(8,128)(2,1)S(1)}, u32[]{:S(2)}, u32[]{:S(2)}) async-start(bf16[4,128,512]{2,1,0:T(8,128)(2,1)} %get-tuple-element.22), calls=%async_computation.4 | async-start | bytes 1048576 | tf_op jit(solution)/shard_map/all_to_all | solution.py:259
  98.7 14.7 %collective-permute-start.7 = (bf16[1024,256]{1,0:T(8,128)(2,1)}, bf16[1024,256]{1,0:T(8,128)(2,1)S(1)}, u32[]{:S(2)}, u32[]{:S(2)}) collective-permute-start(bf16[1024,256]{1,0:T(8,128)(2,1)} %shard_map.101), channel_id=1, source_target_pairs={{0,4},{1,5},{2,6},{3,7},{4,8},{5,9},{6,10},{7,11},{8,12},{9,13},{1... | collective-permute-start | bytes 1572872 | tf_op jit(solution)/shard_map/ppermute | solution.py:255
  101.9 15.1 %collective-permute-start.11 = (bf16[1024,256]{1,0:T(8,128)(2,1)}, bf16[1024,256]{1,0:T(8,128)(2,1)S(1)}, u32[]{:S(2)}, u32[]{:S(2)}) collective-permute-start(bf16[1024,256]{1,0:T(8,128)(2,1)} %shard_map.104), channel_id=1, source_target_pairs={{0,28},{1,29},{2,30},{3,31},{4,0},{5,1},{6,2},{7,3},{8,4},{9,5},{1... | collective-permute-start | bytes 1572872 | tf_op jit(solution)/shard_map/ppermute | solution.py:255
  113.3 18.1 %copy-start.6 = (s32[1,16,4]{1,2,0:T(4,128)S(1)}, s32[1,16,4]{1,2,0:T(4,128)}, u32[]{:S(2)}) copy-start(s32[1,16,4]{1,2,0:T(4,128)} %param.11) | copy-start | bytes 772
  113.3 26.0 %copy-start.3 = (bf16[256,256]{1,0:T(8,128)(2,1)S(1)}, bf16[256,256]{1,0:T(8,128)(2,1)}, u32[]{:S(2)}) copy-start(bf16[256,256]{1,0:T(8,128)(2,1)} %constant.12.clone.rest_1_.low) | copy-start | bytes 393220
  113.3 26.0 %copy-start.4 = (bf16[256,256]{1,0:T(8,128)(2,1)S(1)}, bf16[256,256]{1,0:T(8,128)(2,1)}, u32[]{:S(2)}) copy-start(bf16[256,256]{1,0:T(8,128)(2,1)} %constant.11.clone.rest_0_.high) | copy-start | bytes 393220
  113.3 26.0 %copy-start.5 = (bf16[256,256]{1,0:T(8,128)(2,1)S(1)}, bf16[256,256]{1,0:T(8,128)(2,1)}, u32[]{:S(2)}) copy-start(bf16[256,256]{1,0:T(8,128)(2,1)} %constant.13.clone.rest_2_) | copy-start | bytes 393220
  113.8 25.6 %copy-start = (bf16[1,1024,256]{2,1,0:T(8,128)(2,1)S(1)}, bf16[1,1024,256]{2,1,0:T(8,128)(2,1)}, u32[]{:S(2)}) copy-start(bf16[1,1024,256]{2,1,0:T(8,128)(2,1)} %param.12) | copy-start | bytes 1572868
  113.8 26.0 %collective-permute-start.8 = (bf16[1024,256]{1,0:T(8,128)(2,1)S(1)}, bf16[1024,256]{1,0:T(8,128)(2,1)}, u32[]{:S(2)}, u32[]{:S(2)}) collective-permute-start(bf16[1024,256]{1,0:T(8,128)(2,1)S(1)} %shard_map.102), channel_id=1, source_target_pairs={{0,4},{1,5},{2,6},{3,7},{4,8},{5,9},{6,10},{7,11},{8,12},{9,13},{1... | collective-permute-start | bytes 1572872 | tf_op jit(solution)/shard_map/ppermute | solution.py:255
  117.0 0.8 copy-start.1
  117.8 1.0 copy-start.2
  119.3 20.5 %collective-permute-start.12 = (bf16[1024,256]{1,0:T(8,128)(2,1)S(1)}, bf16[1024,256]{1,0:T(8,128)(2,1)}, u32[]{:S(2)}, u32[]{:S(2)}) collective-permute-start(bf16[1024,256]{1,0:T(8,128)(2,1)S(1)} %shard_map.105), channel_id=1, source_target_pairs={{0,28},{1,29},{2,30},{3,31},{4,0},{5,1},{6,2},{7,3},{8,4},{9,5},{1... | collective-permute-start | bytes 1572872 | tf_op jit(solution)/shard_map/ppermute | solution.py:255
  124.5 14.8 %all-to-all-start.1 = ((bf16[4,128,256]{2,1,0:T(8,128)(2,1)}), bf16[4,128,256]{2,1,0:T(8,128)(2,1)S(1)}, u32[]{:S(2)}, u32[]{:S(2)}) async-start(bf16[4,128,256]{2,1,0:T(8,128)(2,1)} %get-tuple-element.17), calls=%async_computation.1 | async-start | bytes 524288 | tf_op jit(solution)/shard_map/all_to_all | solution.py:259
  145.5 35.4 %all-to-all-start.5 = ((bf16[16,64,256]{2,1,0:T(8,128)(2,1)}), bf16[16,64,256]{2,1,0:T(8,128)(2,1)S(1)}, u32[]{:S(2)}, u32[]{:S(2)}) async-start(bf16[16,64,256]{2,1,0:T(8,128)(2,1)} %get-tuple-element.31), calls=%async_computation.5 | async-start | bytes 1048576 | tf_op jit(solution)/shard_map/all_to_all | solution.py:351

commit v3 on v2

--- a/solution.py
+++ b/solution.py
@@ -32,7 +32,10 @@
     whole = np.kron(np.eye(TILE // BLOCK), table)
     high = whole.astype(jnp.bfloat16)
     low = (whole - high.astype(np.float64)).astype(jnp.bfloat16)
-    return jnp.asarray(high), jnp.asarray(low)
+    some = slice(0, BLOCK)
+    ahead = np.concatenate([high[some, some], high[some, some], low[some, some]], axis=1)
+    back = np.concatenate([high[some, some].T, high[some, some].T, low[some, some].T], axis=1)
+    return tuple(jnp.asarray(part) for part in (high, low, ahead, back))
 
 
 def dot(a, b, dims):
@@ -44,10 +47,14 @@
     return high, (x - high.astype(jnp.float32)).astype(jnp.bfloat16)
 
 
-def left(table, x, dim):
-    (th, tl), (xh, xl) = table, split(x)
-    dims = ((dim,), (0,))
-    return dot(th, xh, dims) + (dot(th, xl, dims) + dot(tl, xh, dims))
+def left(table, x):
+    high, low = split(x)
+    dims = ((1,), (0,))
+    out = []
+    for i in range(x.shape[0] // BLOCK):
+        here = slice(i * BLOCK, (i + 1) * BLOCK)
+        out.append(dot(table, jnp.concatenate([high[here], low[here], high[here]], axis=0), dims))
+    return jnp.concatenate(out, axis=0)
 
 
 def right(x, table, dim):
@@ -82,23 +89,24 @@
     return copies
 
 
-def early_kernel(rows, grads, out, sem):
+def early_kernel(rows, grads, out, sem, given):
     deep = out.shape[0]
     panel = grads.shape[1]
     width = out.shape[2] - panel
     moves = [(4, z, out.at[z, :, pl.ds(panel, width)]) for z in range(deep)]
     copies = fetch(rows, deep, width, moves, sem)
     for z in range(deep):
-        out[z, :, :panel] = grads[...]
+        copies.append(pltpu.make_async_copy(grads, out.at[z, :, pl.ds(0, panel)], given.at[z]))
+        copies[-1].start()
     for copy in copies:
         copy.wait()
 
 
-def late_kernel(rows, third, second, first, own, sem):
-    deep = own.shape[0]
-    width = own.shape[2]
+def late_kernel(rows, third, second, first, sem):
+    deep = third.shape[0]
+    width = third.shape[2] // 2
     moves = []
-    for target, owners in ((third, (3, -3)), (second, (2, -2)), (first, (1, -1)), (own, (0,))):
+    for target, owners in ((third, (3, -3)), (second, (2, -2)), (first, (1, -1, 0))):
         for z in range(deep):
             for j, owner in enumerate(owners):
                 moves.append((owner, z, target.at[z, :, pl.ds(j * width, width)]))
@@ -112,16 +120,14 @@
     panel = out.shape[0]
     z = lax.axis_index("shard") % deep
     marks = [note[...].astype(jnp.float32) for note in notes]
-    heads = marks[0][:8]
+    heads = marks[0][DOCS:]
     for mark in marks[1:]:
-        heads = heads + mark[:8]
-    lengths = pltpu.roll(heads, 112, 1) + pltpu.roll(heads, 96, 1) + pltpu.roll(heads, 80, 1)
-    share = 1.0 / jnp.maximum(lengths[:1], 1.0)
-    lane = lax.broadcasted_iota(jnp.int32, (tokens, 128), 1)
+        heads = heads + mark[DOCS:]
+    share = 1.0 / jnp.maximum(jnp.sum(heads, axis=1, keepdims=True), 1.0)
     for k in range(deep):
-        weight = jnp.sum(jnp.where(lane < DOCS, marks[k] * share, 0.0), axis=1, keepdims=True)
+        weight = jnp.sum(marks[k][:DOCS] * share, axis=0, keepdims=True)
         block = exchanged[(z - k + deep) % deep, :, :panel].astype(jnp.float32)
-        out[:, k * tokens : (k + 1) * tokens] = (block * weight).T.astype(jnp.bfloat16)
+        out[:, k * tokens : (k + 1) * tokens] = (block.T * weight).astype(jnp.bfloat16)
 
 
 def far_kernel(weights, exchanged, up, down):
@@ -146,14 +152,14 @@
 
 def base_kernel(weights, exchanged, momentum, offsets, *rest):
     tables, (product, kept, offsets_out, *tables_out) = rest[: len(rest) // 2 - 1], rest[len(rest) // 2 - 1 :]
-    product[...] = dot(weights[...], gathered(exchanged, 0, product.shape[1]), ((1,), (0,)))
+    product[...] = dot(weights[...], gathered(exchanged, 2 * product.shape[1], product.shape[1]), ((1,), (0,)))
     kept[...] = momentum[...]
     offsets_out[...] = offsets[...]
     for table, out in zip(tables, tables_out):
         out[...] = table[...]
 
 
-def forward_kernel(product, up, down, momentum, offsets, high, low, ones, summed, decoded, sent, packed, held, sem):
+def forward_kernel(product, up, down, momentum, offsets, high, low, ahead, ones, summed, decoded, sent, packed, held, sem):
     table = (high[...], low[...])
     per = TILE // BLOCK
     rows = TILE // STRIDE
@@ -166,7 +172,7 @@
         copies.append(pltpu.make_async_copy(held.at[pl.ds(i * TILE, TILE)], summed.at[pl.ds(i * TILE, TILE)], sem.at[i]))
         copies[-1].start()
         value = BETA * momentum[here].astype(jnp.float32) + gradient.astype(jnp.float32)
-        spectrum = right(left(table, value, 1), table, 1)
+        spectrum = right(left(ahead[...], value), table, 1)
         kept = jnp.where(selected(offsets[i * per : (i + 1) * per]), spectrum, 0.0)
         packed[i * rows : (i + 1) * rows] = jnp.sum(kept.reshape(rows, STRIDE, TILE), axis=1)
     values = packed[...]
@@ -196,22 +202,22 @@
     return jnp.where(selected(offsets), wide, 0.0)
 
 
-def inverse_tile(values, offsets, table):
-    return right(left(table, spread_tile(values, offsets), 0), table, 0)
-
-
-def residual_kernel(momentum, summed, decoded, offsets, high, low, out):
+def inverse_tile(values, offsets, table, back):
+    return right(left(back, spread_tile(values, offsets)), table, 0)
+
+
+def residual_kernel(momentum, summed, decoded, offsets, high, low, back_table, out):
     table = (high[...], low[...])
     per = TILE // BLOCK
     rows = TILE // STRIDE
     for i in range(out.shape[0] // TILE):
         here = slice(i * TILE, (i + 1) * TILE)
         value = BETA * momentum[here].astype(jnp.float32) + summed[here].astype(jnp.float32)
-        back = inverse_tile(decoded[i * rows : (i + 1) * rows], offsets[i * per : (i + 1) * per], table)
+        back = inverse_tile(decoded[i * rows : (i + 1) * rows], offsets[i * per : (i + 1) * per], table, back_table[...])
         out[here] = (value - back).astype(jnp.bfloat16)
 
 
-def update_kernel(parts, offsets, high, low, out):
+def update_kernel(parts, offsets, high, low, back_table, out):
     table = (high[...], low[...])
     per = TILE // BLOCK
     rows = TILE // STRIDE
@@ -221,7 +227,7 @@
         total = parts[0, here].astype(jnp.float32)
         for k in range(1, count):
             total += parts[k, here].astype(jnp.float32)
-        back = inverse_tile(total * (1.0 / count), offsets[i * per : (i + 1) * per], table)
+        back = inverse_tile(total * (1.0 / count), offsets[i * per : (i + 1) * per], table, back_table[...])
         out[i * TILE : (i + 1) * TILE] = back.astype(jnp.bfloat16)
 
 
@@ -270,29 +276,29 @@
         early_kernel,
         shaped(deep, tokens, panel + width),
         work,
-        (pltpu.SemaphoreType.DMA((deep,)),),
-        [apart, whole],
+        (pltpu.SemaphoreType.DMA((deep,)), pltpu.SemaphoreType.DMA((deep,))),
+        [apart, apart],
         FULL,
     )(rows, grads)
     early = exchange(early)
 
-    onehot = (doc_ids[0, 0][:, None] == jnp.arange(128, dtype=jnp.int32)[None, :]).astype(jnp.float32)
-    counts = jnp.broadcast_to(jnp.sum(onehot, axis=0, keepdims=True), (8, 128))
+    documents = lax.broadcasted_iota(jnp.int32, (DOCS, tokens), 0)
+    onehot = (doc_ids[0] == documents).astype(jnp.float32)
+    counts = jnp.broadcast_to(jnp.sum(onehot, axis=1, keepdims=True), (DOCS, tokens))
     before = across(counts, 1)
     after = across(counts, -1)
-    lanes = jnp.concatenate([counts[:1, :16], before[:1, :16], after[:1, :16]], axis=1)
-    extra = jnp.concatenate(
-        [onehot[:, :16], jnp.broadcast_to(lanes, (tokens, 48)), jnp.zeros((tokens, 64), jnp.float32)], axis=1
-    ).astype(jnp.bfloat16)
+    lane = lax.broadcasted_iota(jnp.int32, (DOCS, tokens), 1)
+    heads = jnp.where(lane == 0, counts, jnp.where(lane == 1, before, jnp.where(lane == 2, after, 0.0)))
+    extra = jnp.concatenate([onehot, heads], axis=0).astype(jnp.bfloat16)
 
     notes = [extra]
     for k in (2, 1, 3):
         notes.append(along_line(extra, k))
     notes = [notes[0], notes[2], notes[1], notes[3]]
 
-    third, second, first, own = call(
+    third, second, first = call(
         late_kernel,
-        [shaped(deep, tokens, 2 * width)] * 3 + [shaped(deep, tokens, width)],
+        [shaped(deep, tokens, 2 * width)] * 2 + [shaped(deep, tokens, 3 * width)],
         work,
         (pltpu.SemaphoreType.DMA((7 * deep,)),),
         [apart],
@@ -301,7 +307,6 @@
     third = exchange(third)
     second = exchange(second)
     first = exchange(first)
-    own = exchange(own)
 
     weights = call(scale_kernel, shaped(panel, deep * tokens), work)(early, *notes)
     half = panel // 2
@@ -324,18 +329,18 @@
     up, down = ring(*both(up, down, second))
     up, down = ring(*both(up, down, first))
 
-    high, low = dct_parts()
+    high, low, ahead, back = dct_parts()
     ones = jnp.asarray(np.kron(np.eye(TILE // BLOCK), np.ones((BLOCK, BLOCK))), jnp.bfloat16)
     wide = jnp.repeat(offsets[0], BLOCK, axis=1)
     kept = panel // STRIDE
     flops = 6 * 2 * 2 * panel * TILE * TILE
-    tables = (high, low, ones)
+    tables = (high, low, ahead, ones)
     product, momentum_near, wide_near, *tables_near = call(
         base_kernel,
         [shaped(panel, width, dtype=jnp.float32), shaped(panel, width), shaped(*wide.shape, dtype=jnp.int32)]
         + [shaped(*table.shape) for table in tables],
         work,
-    )(weights, own, momentum[0], wide, *tables)
+    )(weights, first, momentum[0], wide, *tables)
     summed, decoded, sent = pl.pallas_call(
         forward_kernel,
         out_shape=(shaped(panel, width), shaped(kept, width, dtype=jnp.float32), shaped(groups, kept, width)),
@@ -349,8 +354,8 @@
         cost_estimate=pl.CostEstimate(flops=flops, bytes_accessed=2 << 20, transcendentals=0),
     )(product, up, down, momentum_near, wide_near, *tables_near)
     parts = lax.all_to_all(sent, "rep", 0, 0, tiled=True)
-    residual = call(residual_kernel, shaped(panel, width), flops)(momentum[0], summed, decoded, wide, high, low)
-    update = call(update_kernel, shaped(panel, width), flops)(parts, wide, high, low)
+    residual = call(residual_kernel, shaped(panel, width), flops)(momentum[0], summed, decoded, wide, high, low, back)
+    update = call(update_kernel, shaped(panel, width), flops)(parts, wide, high, low, back)
     return residual[None], update[None]
 
 

time: 184 us -> 179 us (0.973)
  the two profiles are of different devices: /device:TPU:1 before, /device:TPU:24 now
where the time goes in v3:
time: 179 us; the launch traced here: 178 us
  starting transfers between devices  87.2 us (49%)
  waiting for transfers between devices  61.5 us (34%)
  Pallas kernels  22 us (12%)
  local copies, waits for them, and re-layouts  5.95 us (3%)
    ppermute x10, starting transfers between devices, across(): return lax.ppermute(x, 'shard', pairs)  36.3 us
    all_to_all x4, starting transfers between devices, exchange(): return lax.all_to_all(x, 'shard', 0, 0, axis_index_groups=lines, tiled=True)  31.9 us
    all_to_all x4, waiting for transfers between devices, exchange(): return lax.all_to_all(x, 'shard', 0, 0, axis_index_groups=lines, tiled=True)  27.1 us
    ppermute x10, waiting for transfers between devices, across(): return lax.ppermute(x, 'shard', pairs)  21.9 us
    ppermute x3, starting transfers between devices, along_line(): return lax.ppermute(x, 'shard', pairs)  14.6 us
    all_to_all x1, waiting for transfers between devices, step(): parts = lax.all_to_all(sent, 'rep', 0, 0, tiled=True)  9.06 us
    pallas_call x6, Pallas kernels, near(): call(kernel, shaped(panel, width), work)(weights, received, exchanged)  5.64 us
    pallas_call x1, Pallas kernels, step(): pl.pallas_call(forward_kernel, out_shape=(shaped(panel, width), shaped(ke...  5.18 us
  transfers between devices with their start and end apart: 18, of which 10 were waited for; matrix products, arithmetic and copies ran while one was open for 1% of the time, Pallas kernels for 7%

profile of v3, /device:TPU:24, one launch (start us, length us, event | category | flops | bytes accessed | tf_op | source)
XLA Modules:
  0.0 177.8 jit_solution(15441930611738936685)
XLA Ops:
  0.6 3.0 %shard_map.115 = (bf16[4,128,512]{2,1,0:T(8,128)(2,1)}, bf16[4,128,512]{2,1,0:T(8,128)(2,1)}, bf16[4,128,768]{2,1,0:T(8,128)(2,1)}) custom-call(bf16[128,8192]{1,0:T(8,128)(2,1)} %bitcast.9), custom_call_target="tpu_custom_call" | custom-call | flops 268435456 | bytes 2097152 | tf_op jit(solution)/shard_map/pallas_call | solution.py:299
  3.6 10.3 %all-to-all-start.2 = ((bf16[4,128,512]{2,1,0:T(8,128)(2,1)}), bf16[4,128,512]{2,1,0:T(8,128)(2,1)S(1)}, u32[]{:S(2)}, u32[]{:S(2)}) async-start(bf16[4,128,512]{2,1,0:T(8,128)(2,1)} %get-tuple-element.20), calls=%async_computation.2 | async-start | bytes 1048576 | tf_op jit(solution)/shard_map/all_to_all | solution.py:265
  13.9 2.6 %shard_map.113 = bf16[4,128,1280]{2,1,0:T(8,128)(2,1)} custom-call(bf16[128,8192]{1,0:T(8,128)(2,1)} %bitcast.10, bf16[128,1024]{1,0:T(8,128)(2,1)} %bitcast.11), custom_call_target="tpu_custom_call" | custom-call | flops 268435456 | bytes 2097152 | tf_op jit(solution)/shard_map/pallas_call | solution.py:275
  16.6 11.9 %all-to-all-done.2.exchanged = bf16[4,128,512]{2,1,0:T(8,128)(2,1)S(1)} async-done(((bf16[4,128,512]{2,1,0:T(8,128)(2,1)}), bf16[4,128,512]{2,1,0:T(8,128)(2,1)S(1)}, u32[]{:S(2)}, u32[]{:S(2)}) %all-to-all-start.2) | async-done | bytes 524320 | tf_op jit(solution)/shard_map/all_to_all | solution.py:265
  28.4 4.8 %all-to-all-start = ((bf16[4,128,1280]{2,1,0:T(8,128)(2,1)}), bf16[4,128,1280]{2,1,0:T(8,128)(2,1)S(1)}, u32[]{:S(2)}, u32[]{:S(2)}) async-start(bf16[4,128,1280]{2,1,0:T(8,128)(2,1)} %shard_map.113), calls=%async_computation | async-start | bytes 2621440 | tf_op jit(solution)/shard_map/all_to_all | solution.py:265
  33.5 2.4 %collective-permute-start.1 = (bf16[16,128]{1,0:T(8,128)(2,1)S(1)}, bf16[16,128]{1,0:T(8,128)(2,1)S(1)}, u32[]{:S(2)}, u32[]{:S(2)}) collective-permute-start(bf16[16,128]{1,0:T(8,128)(2,1)S(1)} %broadcast_in_dim.19), channel_id=1, source_target_pairs={{0,28},{1,29},{2,30},{3,31},{4,0},{5,1},{6,2},{7,3},{8,4},{9,5},{1... | collective-permute-start | bytes 12296 | tf_op jit(solution)/shard_map/ppermute | solution.py:261
  35.8 4.7 %collective-permute-start = (bf16[16,128]{1,0:T(8,128)(2,1)S(1)}, bf16[16,128]{1,0:T(8,128)(2,1)S(1)}, u32[]{:S(2)}, u32[]{:S(2)}) collective-permute-start(bf16[16,128]{1,0:T(8,128)(2,1)S(1)} %broadcast_in_dim.19), channel_id=1, source_target_pairs={{0,4},{1,5},{2,6},{3,7},{4,8},{5,9},{6,10},{7,11},{8,12},{9,13},{1... | collective-permute-start | bytes 12296 | tf_op jit(solution)/shard_map/ppermute | solution.py:261
  40.5 15.3 %all-to-all-done.exchanged = bf16[4,128,1280]{2,1,0:T(8,128)(2,1)S(1)} async-done(((bf16[4,128,1280]{2,1,0:T(8,128)(2,1)}), bf16[4,128,1280]{2,1,0:T(8,128)(2,1)S(1)}, u32[]{:S(2)}, u32[]{:S(2)}) %all-to-all-start) | async-done | bytes 1310752 | tf_op jit(solution)/shard_map/all_to_all | solution.py:265
  55.8 11.9 %all-to-all-start.3 = ((bf16[4,128,512]{2,1,0:T(8,128)(2,1)}), bf16[4,128,512]{2,1,0:T(8,128)(2,1)S(1)}, u32[]{:S(2)}, u32[]{:S(2)}) async-start(bf16[4,128,512]{2,1,0:T(8,128)(2,1)} %get-tuple-element.21), calls=%async_computation.3 | async-start | bytes 1048576 | tf_op jit(solution)/shard_map/all_to_all | solution.py:265
  67.8 6.0 %collective-permute-start.4 = (bf16[32,128]{1,0:T(8,128)(2,1)S(1)}, bf16[32,128]{1,0:T(8,128)(2,1)S(1)}, u32[]{:S(2)}, u32[]{:S(2)}) collective-permute-start(bf16[32,128]{1,0:T(8,128)(2,1)S(1)} %pad_maximum_fusion.rest_0_), channel_id=1, source_target_pairs={{0,3},{1,0},{2,1},{3,2},{4,7},{5,4},{6,5},{7,6},{8,11},{9,8},{10,9... | collective-permute-start | bytes 24584 | tf_op jit(solution)/shard_map/ppermute | solution.py:257
  73.8 4.3 %collective-permute-start.3 = (bf16[32,128]{1,0:T(8,128)(2,1)S(1)}, bf16[32,128]{1,0:T(8,128)(2,1)S(1)}, u32[]{:S(2)}, u32[]{:S(2)}) collective-permute-start(bf16[32,128]{1,0:T(8,128)(2,1)S(1)} %pad_maximum_fusion.rest_0_), channel_id=1, source_target_pairs={{0,2},{1,3},{2,0},{3,1},{4,6},{5,7},{6,4},{7,5},{8,10},{9,11},{10,... | collective-permute-start | bytes 24584 | tf_op jit(solution)/shard_map/ppermute | solution.py:257
  78.1 4.3 %collective-permute-start.2 = (bf16[32,128]{1,0:T(8,128)(2,1)S(1)}, bf16[32,128]{1,0:T(8,128)(2,1)S(1)}, u32[]{:S(2)}, u32[]{:S(2)}) collective-permute-start(bf16[32,128]{1,0:T(8,128)(2,1)S(1)} %pad_maximum_fusion.rest_0_), channel_id=1, source_target_pairs={{0,1},{1,2},{2,3},{3,0},{4,5},{5,6},{6,7},{7,4},{8,9},{9,10},{10,1... | collective-permute-start | bytes 24584 | tf_op jit(solution)/shard_map/ppermute | solution.py:257
  82.4 0.9 collective-permute-done.3.rest_2_
  83.3 2.5 %collective-permute-done.2.rest_1_ = bf16[32,128]{1,0:T(8,128)(2,1)S(1)} collective-permute-done((bf16[32,128]{1,0:T(8,128)(2,1)S(1)}, bf16[32,128]{1,0:T(8,128)(2,1)S(1)}, u32[]{:S(2)}, u32[]{:S(2)}) %collective-permute-start.2) | collective-permute-done | bytes 8224 | tf_op jit(solution)/shard_map/ppermute | solution.py:257
  85.8 0.4 shard_map.114.weights
  86.2 1.2 shard_map.117
  87.4 4.7 %collective-permute-start.5 = (bf16[512,256]{1,0:T(8,128)(2,1)}, bf16[512,256]{1,0:T(8,128)(2,1)S(1)}, u32[]{:S(2)}, u32[]{:S(2)}) collective-permute-start(bf16[512,256]{1,0:T(8,128)(2,1)} %get-tuple-element.19), channel_id=1, source_target_pairs={{0,4},{1,5},{2,6},{3,7},{4,8},{5,9},{6,10},{7,11},{8,12},{9,13},{1... | collective-permute-start | bytes 786440 | tf_op jit(solution)/shard_map/ppermute | solution.py:261
  92.1 1.9 %collective-permute-start.9 = (bf16[512,256]{1,0:T(8,128)(2,1)}, bf16[512,256]{1,0:T(8,128)(2,1)}, u32[]{:S(2)}, u32[]{:S(2)}) collective-permute-start(bf16[512,256]{1,0:T(8,128)(2,1)} %get-tuple-element.22), channel_id=1, source_target_pairs={{0,28},{1,29},{2,30},{3,31},{4,0},{5,1},{6,2},{7,3},{8,4},{9,5},{1... | collective-permute-start | bytes 786440 | tf_op jit(solution)/shard_map/ppermute | solution.py:261
  94.0 4.9 %all-to-all-start.1 = ((bf16[4,128,768]{2,1,0:T(8,128)(2,1)}), bf16[4,128,768]{2,1,0:T(8,128)(2,1)S(1)}, u32[]{:S(2)}, u32[]{:S(2)}) async-start(bf16[4,128,768]{2,1,0:T(8,128)(2,1)} %get-tuple-element.17), calls=%async_computation.1 | async-start | bytes 1572864 | tf_op jit(solution)/shard_map/all_to_all | solution.py:265
  99.1 0.7 copy-done.1
  99.8 0.9 copy-done.2
  100.7 0.4 shard_map.118
  101.2 5.5 %collective-permute-start.6 = (bf16[1024,256]{1,0:T(8,128)(2,1)S(1)}, bf16[1024,256]{1,0:T(8,128)(2,1)S(1)}, u32[]{:S(2)}, u32[]{:S(2)}) collective-permute-start(bf16[1024,256]{1,0:T(8,128)(2,1)S(1)} %shard_map.118), channel_id=1, source_target_pairs={{0,4},{1,5},{2,6},{3,7},{4,8},{5,9},{6,10},{7,11},{8,12},{9,13},{1... | collective-permute-start | bytes 1572872 | tf_op jit(solution)/shard_map/ppermute | solution.py:261
  106.7 1.4 shard_map.121
  108.1 1.9 %collective-permute-start.10 = (bf16[1024,256]{1,0:T(8,128)(2,1)S(1)}, bf16[1024,256]{1,0:T(8,128)(2,1)S(1)}, u32[]{:S(2)}, u32[]{:S(2)}) collective-permute-start(bf16[1024,256]{1,0:T(8,128)(2,1)S(1)} %shard_map.121), channel_id=1, source_target_pairs={{0,28},{1,29},{2,30},{3,31},{4,0},{5,1},{6,2},{7,3},{8,4},{9,5},{1... | collective-permute-start | bytes 1572872 | tf_op jit(solution)/shard_map/ppermute | solution.py:261
  110.0 7.3 %collective-permute-done.6.received = bf16[1024,256]{1,0:T(8,128)(2,1)S(1)} collective-permute-done((bf16[1024,256]{1,0:T(8,128)(2,1)S(1)}, bf16[1024,256]{1,0:T(8,128)(2,1)S(1)}, u32[]{:S(2)}, u32[]{:S(2)}) %collective-permute-start.6) | collective-permute-done | bytes 524320 | tf_op jit(solution)/shard_map/ppermute | solution.py:261
  117.3 0.4 shard_map.119
  117.8 5.6 %collective-permute-start.7 = (bf16[1024,256]{1,0:T(8,128)(2,1)S(1)}, bf16[1024,256]{1,0:T(8,128)(2,1)}, u32[]{:S(2)}, u32[]{:S(2)}) collective-permute-start(bf16[1024,256]{1,0:T(8,128)(2,1)S(1)} %shard_map.119), channel_id=1, source_target_pairs={{0,4},{1,5},{2,6},{3,7},{4,8},{5,9},{6,10},{7,11},{8,12},{9,13},{1... | collective-permute-start | bytes 1572872 | tf_op jit(solution)/shard_map/ppermute | solution.py:261
  123.4 1.0 collective-permute-done.10.received
  124.4 0.4 shard_map.122
  124.8 1.9 %collective-permute-start.11 = (bf16[1024,256]{1,0:T(8,128)(2,1)S(1)}, bf16[1024,256]{1,0:T(8,128)(2,1)}, u32[]{:S(2)}, u32[]{:S(2)}) collective-permute-start(bf16[1024,256]{1,0:T(8,128)(2,1)S(1)} %shard_map.122), channel_id=1, source_target_pairs={{0,28},{1,29},{2,30},{3,31},{4,0},{5,1},{6,2},{7,3},{8,4},{9,5},{1... | collective-permute-start | bytes 1572872 | tf_op jit(solution)/shard_map/ppermute | solution.py:261
  126.7 7.6 %collective-permute-done.7.received = bf16[1024,256]{1,0:T(8,128)(2,1)} collective-permute-done((bf16[1024,256]{1,0:T(8,128)(2,1)S(1)}, bf16[1024,256]{1,0:T(8,128)(2,1)}, u32[]{:S(2)}, u32[]{:S(2)}) %collective-permute-start.7) | collective-permute-done | bytes 524320 | tf_op jit(solution)/shard_map/ppermute | solution.py:261
  134.4 1.5 shard_map.120
  135.9 5.8 %collective-permute-start.8 = (bf16[1024,256]{1,0:T(8,128)(2,1)S(1)}, bf16[1024,256]{1,0:T(8,128)(2,1)}, u32[]{:S(2)}, u32[]{:S(2)}) collective-permute-start(bf16[1024,256]{1,0:T(8,128)(2,1)S(1)} %shard_map.120), channel_id=1, source_target_pairs={{0,4},{1,5},{2,6},{3,7},{4,8},{5,9},{6,10},{7,11},{8,12},{9,13},{1... | collective-permute-start | bytes 1572872 | tf_op jit(solution)/shard_map/ppermute | solution.py:261
  141.8 1.5 shard_map.123
  143.2 1.9 %collective-permute-start.12 = (bf16[1024,256]{1,0:T(8,128)(2,1)S(1)}, bf16[1024,256]{1,0:T(8,128)(2,1)}, u32[]{:S(2)}, u32[]{:S(2)}) collective-permute-start(bf16[1024,256]{1,0:T(8,128)(2,1)S(1)} %shard_map.123), channel_id=1, source_target_pairs={{0,28},{1,29},{2,30},{3,31},{4,0},{5,1},{6,2},{7,3},{8,4},{9,5},{1... | collective-permute-start | bytes 1572872 | tf_op jit(solution)/shard_map/ppermute | solution.py:261
  145.3 0.7 broadcast_in_dim.21
  146.0 0.8 reshape.9.offsets
  146.8 0.9 copy-done.4
  147.7 0.9 copy-done.6
  148.6 0.8 copy-done.7
  149.4 0.4 shard_map.116
  149.8 5.8 %collective-permute-done.12.down = bf16[1024,256]{1,0:T(8,128)(2,1)} collective-permute-done((bf16[1024,256]{1,0:T(8,128)(2,1)S(1)}, bf16[1024,256]{1,0:T(8,128)(2,1)}, u32[]{:S(2)}, u32[]{:S(2)}) %collective-permute-start.12) | collective-permute-done | bytes 524320 | tf_op jit(solution)/shard_map/ppermute | solution.py:261
  155.6 5.2 %shard_map.124 = (bf16[1024,256]{1,0:T(8,128)(2,1)S(1)}, f32[64,256]{1,0:T(8,128)S(1)}, bf16[16,64,256]{2,1,0:T(8,128)(2,1)}) custom-call(f32[1024,256]{1,0:T(8,128)S(1)} %get-tuple-element.18.product, bf16[1024,256]{1,0:T(8,128)(2,1)} %collective-permute-done.8.up, bf16[1024,256]{1,0:T(8,128)(2,1)} %collective-permute-done.12.down, ...), custom_call_target="tpu_custom_call" | custom-call | flops 1610612736 | bytes 2097152 | tf_op jit(solution)/shard_map/pallas_call | solution.py:344
  160.8 4.4 %all-to-all-start.4 = ((bf16[16,64,256]{2,1,0:T(8,128)(2,1)}), bf16[16,64,256]{2,1,0:T(8,128)(2,1)S(1)}, u32[]{:S(2)}, u32[]{:S(2)}) async-start(bf16[16,64,256]{2,1,0:T(8,128)(2,1)} %get-tuple-element.31), calls=%async_computation.4 | async-start | bytes 1048576 | tf_op jit(solution)/shard_map/all_to_all | solution.py:356
  165.3 1.7 shard_map.125
  167.0 9.1 %all-to-all-done.4.parts = bf16[16,64,256]{2,1,0:T(8,128)(2,1)S(1)} async-done(((bf16[16,64,256]{2,1,0:T(8,128)(2,1)}), bf16[16,64,256]{2,1,0:T(8,128)(2,1)S(1)}, u32[]{:S(2)}, u32[]{:S(2)}) %all-to-all-start.4) | async-done | bytes 524320 | tf_op jit(solution)/shard_map/all_to_all | solution.py:356
  176.1 1.7 shard_map.126
  (34 shorter events, 0.6 us)
Async XLA Ops:
  3.6 24.8 %all-to-all-start.2 = ((bf16[4,128,512]{2,1,0:T(8,128)(2,1)}), bf16[4,128,512]{2,1,0:T(8,128)(2,1)S(1)}, u32[]{:S(2)}, u32[]{:S(2)}) async-start(bf16[4,128,512]{2,1,0:T(8,128)(2,1)} %get-tuple-element.20), calls=%async_computation.2 | async-start | bytes 1048576 | tf_op jit(solution)/shard_map/all_to_all | solution.py:265
  16.6 16.7 %copy-start.10 = (s32[1,1,128]{2,1,0:T(1,128)S(1)}, s32[1,1,128]{2,1,0:T(1,128)}, u32[]{:S(2)}) copy-start(s32[1,1,128]{2,1,0:T(1,128)} %param.12) | copy-start | bytes 1540
  28.4 27.4 %all-to-all-start = ((bf16[4,128,1280]{2,1,0:T(8,128)(2,1)}), bf16[4,128,1280]{2,1,0:T(8,128)(2,1)S(1)}, u32[]{:S(2)}, u32[]{:S(2)}) async-start(bf16[4,128,1280]{2,1,0:T(8,128)(2,1)} %shard_map.113), calls=%async_computation | async-start | bytes 2621440 | tf_op jit(solution)/shard_map/all_to_all | solution.py:265
  33.5 34.3 %collective-permute-start.1 = (bf16[16,128]{1,0:T(8,128)(2,1)S(1)}, bf16[16,128]{1,0:T(8,128)(2,1)S(1)}, u32[]{:S(2)}, u32[]{:S(2)}) collective-permute-start(bf16[16,128]{1,0:T(8,128)(2,1)S(1)} %broadcast_in_dim.19), channel_id=1, source_target_pairs={{0,28},{1,29},{2,30},{3,31},{4,0},{5,1},{6,2},{7,3},{8,4},{9,5},{1... | collective-permute-start | bytes 12296 | tf_op jit(solution)/shard_map/ppermute | solution.py:261
  35.8 31.9 %collective-permute-start = (bf16[16,128]{1,0:T(8,128)(2,1)S(1)}, bf16[16,128]{1,0:T(8,128)(2,1)S(1)}, u32[]{:S(2)}, u32[]{:S(2)}) collective-permute-start(bf16[16,128]{1,0:T(8,128)(2,1)S(1)} %broadcast_in_dim.19), channel_id=1, source_target_pairs={{0,4},{1,5},{2,6},{3,7},{4,8},{5,9},{6,10},{7,11},{8,12},{9,13},{1... | collective-permute-start | bytes 12296 | tf_op jit(solution)/shard_map/ppermute | solution.py:261
  55.8 38.2 %all-to-all-start.3 = ((bf16[4,128,512]{2,1,0:T(8,128)(2,1)}), bf16[4,128,512]{2,1,0:T(8,128)(2,1)S(1)}, u32[]{:S(2)}, u32[]{:S(2)}) async-start(bf16[4,128,512]{2,1,0:T(8,128)(2,1)} %get-tuple-element.21), calls=%async_computation.3 | async-start | bytes 1048576 | tf_op jit(solution)/shard_map/all_to_all | solution.py:265
  67.8 14.6 %collective-permute-start.4 = (bf16[32,128]{1,0:T(8,128)(2,1)S(1)}, bf16[32,128]{1,0:T(8,128)(2,1)S(1)}, u32[]{:S(2)}, u32[]{:S(2)}) collective-permute-start(bf16[32,128]{1,0:T(8,128)(2,1)S(1)} %pad_maximum_fusion.rest_0_), channel_id=1, source_target_pairs={{0,3},{1,0},{2,1},{3,2},{4,7},{5,4},{6,5},{7,6},{8,11},{9,8},{10,9... | collective-permute-start | bytes 24584 | tf_op jit(solution)/shard_map/ppermute | solution.py:257
  73.8 9.5 %collective-permute-start.3 = (bf16[32,128]{1,0:T(8,128)(2,1)S(1)}, bf16[32,128]{1,0:T(8,128)(2,1)S(1)}, u32[]{:S(2)}, u32[]{:S(2)}) collective-permute-start(bf16[32,128]{1,0:T(8,128)(2,1)S(1)} %pad_maximum_fusion.rest_0_), channel_id=1, source_target_pairs={{0,2},{1,3},{2,0},{3,1},{4,6},{5,7},{6,4},{7,5},{8,10},{9,11},{10,... | collective-permute-start | bytes 24584 | tf_op jit(solution)/shard_map/ppermute | solution.py:257
  78.1 7.7 %collective-permute-start.2 = (bf16[32,128]{1,0:T(8,128)(2,1)S(1)}, bf16[32,128]{1,0:T(8,128)(2,1)S(1)}, u32[]{:S(2)}, u32[]{:S(2)}) collective-permute-start(bf16[32,128]{1,0:T(8,128)(2,1)S(1)} %pad_maximum_fusion.rest_0_), channel_id=1, source_target_pairs={{0,1},{1,2},{2,3},{3,0},{4,5},{5,6},{6,7},{7,4},{8,9},{9,10},{10,1... | collective-permute-start | bytes 24584 | tf_op jit(solution)/shard_map/ppermute | solution.py:257
  87.4 11.7 %collective-permute-start.5 = (bf16[512,256]{1,0:T(8,128)(2,1)}, bf16[512,256]{1,0:T(8,128)(2,1)S(1)}, u32[]{:S(2)}, u32[]{:S(2)}) collective-permute-start(bf16[512,256]{1,0:T(8,128)(2,1)} %get-tuple-element.19), channel_id=1, source_target_pairs={{0,4},{1,5},{2,6},{3,7},{4,8},{5,9},{6,10},{7,11},{8,12},{9,13},{1... | collective-permute-start | bytes 786440 | tf_op jit(solution)/shard_map/ppermute | solution.py:261
  92.1 14.6 %collective-permute-start.9 = (bf16[512,256]{1,0:T(8,128)(2,1)}, bf16[512,256]{1,0:T(8,128)(2,1)}, u32[]{:S(2)}, u32[]{:S(2)}) collective-permute-start(bf16[512,256]{1,0:T(8,128)(2,1)} %get-tuple-element.22), channel_id=1, source_target_pairs={{0,28},{1,29},{2,30},{3,31},{4,0},{5,1},{6,2},{7,3},{8,4},{9,5},{1... | collective-permute-start | bytes 786440 | tf_op jit(solution)/shard_map/ppermute | solution.py:261
  94.0 32.7 %all-to-all-start.1 = ((bf16[4,128,768]{2,1,0:T(8,128)(2,1)}), bf16[4,128,768]{2,1,0:T(8,128)(2,1)S(1)}, u32[]{:S(2)}, u32[]{:S(2)}) async-start(bf16[4,128,768]{2,1,0:T(8,128)(2,1)} %get-tuple-element.17), calls=%async_computation.1 | async-start | bytes 1572864 | tf_op jit(solution)/shard_map/all_to_all | solution.py:265
  99.1 0.7 copy-start.1
  99.8 0.9 copy-start.2
  101.2 16.2 %collective-permute-start.6 = (bf16[1024,256]{1,0:T(8,128)(2,1)S(1)}, bf16[1024,256]{1,0:T(8,128)(2,1)S(1)}, u32[]{:S(2)}, u32[]{:S(2)}) collective-permute-start(bf16[1024,256]{1,0:T(8,128)(2,1)S(1)} %shard_map.118), channel_id=1, source_target_pairs={{0,4},{1,5},{2,6},{3,7},{4,8},{5,9},{6,10},{7,11},{8,12},{9,13},{1... | collective-permute-start | bytes 1572872 | tf_op jit(solution)/shard_map/ppermute | solution.py:261
  108.1 16.3 %collective-permute-start.10 = (bf16[1024,256]{1,0:T(8,128)(2,1)S(1)}, bf16[1024,256]{1,0:T(8,128)(2,1)S(1)}, u32[]{:S(2)}, u32[]{:S(2)}) collective-permute-start(bf16[1024,256]{1,0:T(8,128)(2,1)S(1)} %shard_map.121), channel_id=1, source_target_pairs={{0,28},{1,29},{2,30},{3,31},{4,0},{5,1},{6,2},{7,3},{8,4},{9,5},{1... | collective-permute-start | bytes 1572872 | tf_op jit(solution)/shard_map/ppermute | solution.py:261
  117.8 16.6 %collective-permute-start.7 = (bf16[1024,256]{1,0:T(8,128)(2,1)S(1)}, bf16[1024,256]{1,0:T(8,128)(2,1)}, u32[]{:S(2)}, u32[]{:S(2)}) collective-permute-start(bf16[1024,256]{1,0:T(8,128)(2,1)S(1)} %shard_map.119), channel_id=1, source_target_pairs={{0,4},{1,5},{2,6},{3,7},{4,8},{5,9},{6,10},{7,11},{8,12},{9,13},{1... | collective-permute-start | bytes 1572872 | tf_op jit(solution)/shard_map/ppermute | solution.py:261
  124.8 17.0 %collective-permute-start.11 = (bf16[1024,256]{1,0:T(8,128)(2,1)S(1)}, bf16[1024,256]{1,0:T(8,128)(2,1)}, u32[]{:S(2)}, u32[]{:S(2)}) collective-permute-start(bf16[1024,256]{1,0:T(8,128)(2,1)S(1)} %shard_map.122), channel_id=1, source_target_pairs={{0,28},{1,29},{2,30},{3,31},{4,0},{5,1},{6,2},{7,3},{8,4},{9,5},{1... | collective-permute-start | bytes 1572872 | tf_op jit(solution)/shard_map/ppermute | solution.py:261
  135.9 9.3 %copy-start.9 = (s32[1,16,4]{1,2,0:T(4,128)S(1)}, s32[1,16,4]{1,2,0:T(4,128)}, u32[]{:S(2)}) copy-start(s32[1,16,4]{1,2,0:T(4,128)} %param.13) | copy-start | bytes 772
  135.9 10.9 %copy-start = (bf16[1,1024,256]{2,1,0:T(8,128)(2,1)S(1)}, bf16[1,1024,256]{2,1,0:T(8,128)(2,1)}, u32[]{:S(2)}) copy-start(bf16[1,1024,256]{2,1,0:T(8,128)(2,1)} %param.14) | copy-start | bytes 1572868
  135.9 10.9 %copy-start.3 = (bf16[256,256]{1,0:T(8,128)(2,1)S(1)}, bf16[256,256]{1,0:T(8,128)(2,1)}, u32[]{:S(2)}) copy-start(bf16[256,256]{1,0:T(8,128)(2,1)} %constant.19.clone.rest_1_.low) | copy-start | bytes 393220
  135.9 13.9 %collective-permute-start.8 = (bf16[1024,256]{1,0:T(8,128)(2,1)S(1)}, bf16[1024,256]{1,0:T(8,128)(2,1)}, u32[]{:S(2)}, u32[]{:S(2)}) collective-permute-start(bf16[1024,256]{1,0:T(8,128)(2,1)S(1)} %shard_map.120), channel_id=1, source_target_pairs={{0,4},{1,5},{2,6},{3,7},{4,8},{5,9},{6,10},{7,11},{8,12},{9,13},{1... | collective-permute-start | bytes 1572872 | tf_op jit(solution)/shard_map/ppermute | solution.py:261
  143.2 12.4 %collective-permute-start.12 = (bf16[1024,256]{1,0:T(8,128)(2,1)S(1)}, bf16[1024,256]{1,0:T(8,128)(2,1)}, u32[]{:S(2)}, u32[]{:S(2)}) collective-permute-start(bf16[1024,256]{1,0:T(8,128)(2,1)S(1)} %shard_map.123), channel_id=1, source_target_pairs={{0,28},{1,29},{2,30},{3,31},{4,0},{5,1},{6,2},{7,3},{8,4},{9,5},{1... | collective-permute-start | bytes 1572872 | tf_op jit(solution)/shard_map/ppermute | solution.py:261
  146.8 0.9 copy-start.4
  147.7 0.9 copy-start.6
  148.6 0.8 copy-start.7
  155.6 9.6 %copy-start.5 = (bf16[256,256]{1,0:T(8,128)(2,1)S(1)}, bf16[256,256]{1,0:T(8,128)(2,1)}, u32[]{:S(2)}) copy-start(bf16[256,256]{1,0:T(8,128)(2,1)} %constant.18.clone.rest_0_.high) | copy-start | bytes 393220
  155.6 9.6 %copy-start.8 = (bf16[64,192]{1,0:T(8,128)(2,1)S(1)}, bf16[64,192]{1,0:T(8,128)(2,1)}, u32[]{:S(2)}) copy-start(bf16[64,192]{1,0:T(8,128)(2,1)} %constant.21.clone.back_table) | copy-start | bytes 73732
  160.8 15.3 %all-to-all-start.4 = ((bf16[16,64,256]{2,1,0:T(8,128)(2,1)}), bf16[16,64,256]{2,1,0:T(8,128)(2,1)S(1)}, u32[]{:S(2)}, u32[]{:S(2)}) async-start(bf16[16,64,256]{2,1,0:T(8,128)(2,1)} %get-tuple-element.31), calls=%async_computation.4 | async-start | bytes 1048576 | tf_op jit(solution)/shard_map/all_to_all | solution.py:356

commit v4 on v3

--- a/solution.py
+++ b/solution.py
@@ -21,6 +21,7 @@
 
 TILE = 256
 GRANT = 16 << 20
+NOTE_ROWS = 8
 FULL = 60 << 20
 
 
@@ -72,8 +73,9 @@
 
 def gathered(exchanged, start, size):
     deep = exchanged.shape[0]
+    tokens = exchanged.shape[1] // 128 * 128
     z = lax.axis_index("shard") % deep
-    return jnp.concatenate([exchanged[(z - k + deep) % deep, :, start : start + size] for k in range(deep)], axis=0)
+    return jnp.concatenate([exchanged[(z - k + deep) % deep, :tokens, start : start + size] for k in range(deep)], axis=0)
 
 
 def fetch(rows, deep, width, moves, sem):
@@ -89,15 +91,18 @@
     return copies
 
 
-def early_kernel(rows, grads, out, sem, given):
+def early_kernel(rows, grads, ids, out, sem, given):
     deep = out.shape[0]
-    panel = grads.shape[1]
+    tokens, panel = grads.shape
     width = out.shape[2] - panel
-    moves = [(4, z, out.at[z, :, pl.ds(panel, width)]) for z in range(deep)]
+    here = pl.ds(0, tokens)
+    moves = [(4, z, out.at[z, here, pl.ds(panel, width)]) for z in range(deep)]
     copies = fetch(rows, deep, width, moves, sem)
     for z in range(deep):
-        copies.append(pltpu.make_async_copy(grads, out.at[z, :, pl.ds(0, panel)], given.at[z]))
+        copies.append(pltpu.make_async_copy(grads, out.at[z, here, pl.ds(0, panel)], given.at[z]))
         copies[-1].start()
+    for z in range(deep):
+        out[z, tokens:, :tokens] = jnp.broadcast_to(ids[...], (NOTE_ROWS, tokens)).astype(jnp.bfloat16)
     for copy in copies:
         copy.wait()
 
@@ -114,19 +119,29 @@
         copy.wait()
 
 
-def scale_kernel(exchanged, *rest):
-    notes, out = rest[:-1], rest[-1]
-    deep, tokens = exchanged.shape[0], exchanged.shape[1]
+def marked(exchanged, k):
+    deep = exchanged.shape[0]
+    tokens = exchanged.shape[1] - NOTE_ROWS
+    z = lax.axis_index("shard") % deep
+    ids = exchanged[(z - k + deep) % deep, tokens:, :tokens].astype(jnp.float32)[:1]
+    documents = lax.broadcasted_iota(jnp.int32, (DOCS, tokens), 0).astype(jnp.float32)
+    return jnp.where(ids == documents, 1.0, 0.0)
+
+
+def count_kernel(exchanged, out):
+    total = sum(marked(exchanged, k) for k in range(exchanged.shape[0]))
+    out[...] = jnp.broadcast_to(jnp.sum(total, axis=1, keepdims=True), out.shape)
+
+
+def scale_kernel(exchanged, counts, before, after, out):
+    deep = exchanged.shape[0]
+    tokens = exchanged.shape[1] - NOTE_ROWS
     panel = out.shape[0]
     z = lax.axis_index("shard") % deep
-    marks = [note[...].astype(jnp.float32) for note in notes]
-    heads = marks[0][DOCS:]
-    for mark in marks[1:]:
-        heads = heads + mark[DOCS:]
-    share = 1.0 / jnp.maximum(jnp.sum(heads, axis=1, keepdims=True), 1.0)
+    share = 1.0 / jnp.maximum(counts[...] + before[...] + after[...], 1.0)
     for k in range(deep):
-        weight = jnp.sum(marks[k][:DOCS] * share, axis=0, keepdims=True)
-        block = exchanged[(z - k + deep) % deep, :, :panel].astype(jnp.float32)
+        weight = jnp.sum(marked(exchanged, k) * share, axis=0, keepdims=True)
+        block = exchanged[(z - k + deep) % deep, :tokens, :panel].astype(jnp.float32)
         out[:, k * tokens : (k + 1) * tokens] = (block.T * weight).astype(jnp.bfloat16)
 
 
@@ -159,17 +174,28 @@
         out[...] = table[...]
 
 
-def forward_kernel(product, up, down, momentum, offsets, high, low, ahead, ones, summed, decoded, sent, packed, held, sem):
+def forward_kernel(
+    product, up, down, momentum, offsets, high, low, ahead, ones, summed, decoded, sent, packed, held, parts, sem
+):
     table = (high[...], low[...])
     per = TILE // BLOCK
     rows = TILE // STRIDE
+    fetches = []
+    for i in range(product.shape[0] // TILE):
+        there = pl.ds(i * TILE, TILE)
+        pair = [pltpu.make_async_copy(x.at[there], parts.at[j, there], sem.at[1 + j, i]) for j, x in enumerate((up, down))]
+        fetches.append(pair)
+        for copy in pair:
+            copy.start()
     copies = []
     for i in range(product.shape[0] // TILE):
         here = slice(i * TILE, (i + 1) * TILE)
-        total = product[here] + up[here].astype(jnp.float32) + down[here].astype(jnp.float32)
+        for copy in fetches[i]:
+            copy.wait()
+        total = product[here] + parts[0, here].astype(jnp.float32) + parts[1, here].astype(jnp.float32)
         gradient = total.astype(jnp.bfloat16)
         held[here] = gradient
-        copies.append(pltpu.make_async_copy(held.at[pl.ds(i * TILE, TILE)], summed.at[pl.ds(i * TILE, TILE)], sem.at[i]))
+        copies.append(pltpu.make_async_copy(held.at[pl.ds(i * TILE, TILE)], summed.at[pl.ds(i * TILE, TILE)], sem.at[0, i]))
         copies[-1].start()
         value = BETA * momentum[here].astype(jnp.float32) + gradient.astype(jnp.float32)
         spectrum = right(left(ahead[...], value), table, 1)
@@ -252,10 +278,6 @@
     deep = shards // LINES
     groups = lax.axis_size("rep")
 
-    def along_line(x, k):
-        pairs = [(y * deep + z, y * deep + (z + k) % deep) for y in range(LINES) for z in range(deep)]
-        return lax.ppermute(x, "shard", pairs)
-
     def across(x, k):
         pairs = [(y * deep + z, (y + k) % LINES * deep + z) for y in range(LINES) for z in range(deep)]
         return lax.ppermute(x, "shard", pairs)
@@ -274,27 +296,13 @@
 
     early = call(
         early_kernel,
-        shaped(deep, tokens, panel + width),
+        shaped(deep, tokens + NOTE_ROWS, panel + width),
         work,
         (pltpu.SemaphoreType.DMA((deep,)), pltpu.SemaphoreType.DMA((deep,))),
-        [apart, apart],
+        [apart, apart, whole],
         FULL,
-    )(rows, grads)
+    )(rows, grads, doc_ids[0].astype(jnp.float32))
     early = exchange(early)
-
-    documents = lax.broadcasted_iota(jnp.int32, (DOCS, tokens), 0)
-    onehot = (doc_ids[0] == documents).astype(jnp.float32)
-    counts = jnp.broadcast_to(jnp.sum(onehot, axis=1, keepdims=True), (DOCS, tokens))
-    before = across(counts, 1)
-    after = across(counts, -1)
-    lane = lax.broadcasted_iota(jnp.int32, (DOCS, tokens), 1)
-    heads = jnp.where(lane == 0, counts, jnp.where(lane == 1, before, jnp.where(lane == 2, after, 0.0)))
-    extra = jnp.concatenate([onehot, heads], axis=0).astype(jnp.bfloat16)
-
-    notes = [extra]
-    for k in (2, 1, 3):
-        notes.append(along_line(extra, k))
-    notes = [notes[0], notes[2], notes[1], notes[3]]
 
     third, second, first = call(
         late_kernel,
@@ -308,7 +316,10 @@
     second = exchange(second)
     first = exchange(first)
 
-    weights = call(scale_kernel, shaped(panel, deep * tokens), work)(early, *notes)
+    counts = call(count_kernel, shaped(DOCS, 128, dtype=jnp.float32), work // 64)(early)
+    before = across(counts, 1)
+    after = across(counts, -1)
+    weights = call(scale_kernel, shaped(panel, deep * tokens), work)(early, counts, before, after)
     half = panel // 2
     up, down = call(far_kernel, [shaped(half, width)] * 2, work)(weights, early)
 
@@ -344,11 +355,13 @@
     summed, decoded, sent = pl.pallas_call(
         forward_kernel,
         out_shape=(shaped(panel, width), shaped(kept, width, dtype=jnp.float32), shaped(groups, kept, width)),
+        in_specs=[whole, apart, apart] + [whole] * 6,
         out_specs=(apart, whole, whole),
         scratch_shapes=(
             pltpu.VMEM((kept, width), jnp.float32),
             pltpu.VMEM((panel, width), jnp.bfloat16),
-            pltpu.SemaphoreType.DMA((panel // TILE,)),
+            pltpu.VMEM((2, panel, width), jnp.bfloat16),
+            pltpu.SemaphoreType.DMA((3, panel // TILE)),
         ),
         compiler_params=pltpu.CompilerParams(vmem_limit_bytes=GRANT),
         cost_estimate=pl.CostEstimate(flops=flops, bytes_accessed=2 << 20, transcendentals=0),

time: 179 us -> 173 us (0.966)
  the two profiles are of different devices: /device:TPU:24 before, /device:TPU:1 now
where the time goes in v4:
time: 173 us; the launch traced here: 172 us
  starting transfers between devices  74.9 us (43%)
  waiting for transfers between devices  38.8 us (22%)
  blocking collectives  29.3 us (17%)
  Pallas kernels  22.6 us (13%)
  local copies, waits for them, and re-layouts  4.65 us (3%)
    ppermute x10, starting transfers between devices, across(): return lax.ppermute(x, 'shard', pairs)  33.6 us
    all_to_all x1, blocking collectives, exchange(): return lax.all_to_all(x, 'shard', 0, 0, axis_index_groups=lines, tiled=True)  29.3 us
    ppermute x10, waiting for transfers between devices, across(): return lax.ppermute(x, 'shard', pairs)  22.9 us
    all_to_all x3, starting transfers between devices, exchange(): return lax.all_to_all(x, 'shard', 0, 0, axis_index_groups=lines, tiled=True)  21.5 us
    all_to_all x1, starting transfers between devices, step(): parts = lax.all_to_all(sent, 'rep', 0, 0, tiled=True)  19.8 us
    all_to_all x3, waiting for transfers between devices, exchange(): return lax.all_to_all(x, 'shard', 0, 0, axis_index_groups=lines, tiled=True)  8 us
    all_to_all x1, waiting for transfers between devices, step(): parts = lax.all_to_all(sent, 'rep', 0, 0, tiled=True)  7.87 us
    pallas_call x6, Pallas kernels, near(): call(kernel, shaped(panel, width), work)(weights, received, exchanged)  5.66 us
  transfers between devices with their start and end apart: 14, of which 7 were waited for; matrix products, arithmetic and copies ran while one was open for 0% of the time, Pallas kernels for 7%

profile of v4, /device:TPU:1, one launch (start us, length us, event | category | flops | bytes accessed | tf_op | source)
XLA Modules:
  0.0 171.8 jit_solution(1157197111536943198)
XLA Ops:
  0.6 3.0 %shard_map.116 = (bf16[4,128,512]{2,1,0:T(8,128)(2,1)}, bf16[4,128,512]{2,1,0:T(8,128)(2,1)}, bf16[4,128,768]{2,1,0:T(8,128)(2,1)}) custom-call(bf16[128,8192]{1,0:T(8,128)(2,1)} %bitcast.10), custom_call_target="tpu_custom_call" | custom-call | flops 268435456 | bytes 2097152 | tf_op jit(solution)/shard_map/pallas_call | solution.py:307
  3.6 10.8 %all-to-all-start.2 = ((bf16[4,128,512]{2,1,0:T(8,128)(2,1)}), bf16[4,128,512]{2,1,0:T(8,128)(2,1)S(1)}, u32[]{:S(2)}, u32[]{:S(2)}) async-start(bf16[4,128,512]{2,1,0:T(8,128)(2,1)} %get-tuple-element.20), calls=%async_computation.2 | async-start | bytes 1048576 | tf_op jit(solution)/shard_map/all_to_all | solution.py:287
  14.5 0.6 convert_bitcast_fusion.ids
  15.1 3.3 %shard_map.113 = bf16[4,136,1280]{2,1,0:T(8,128)(2,1)} custom-call(bf16[128,8192]{1,0:T(8,128)(2,1)} %bitcast.11, bf16[128,1024]{1,0:T(8,128)(2,1)} %bitcast.12, f32[1,128]{1,0:T(1,128)} %convert_bitcast_fusion.ids), custom_call_target="tpu_custom_call" | custom-call | flops 268435456 | bytes 2097152 | tf_op jit(solution)/shard_map/pallas_call | solution.py:297
  18.4 8.0 %all-to-all-done.2.exchanged = bf16[4,128,512]{2,1,0:T(8,128)(2,1)S(1)} async-done(((bf16[4,128,512]{2,1,0:T(8,128)(2,1)}), bf16[4,128,512]{2,1,0:T(8,128)(2,1)S(1)}, u32[]{:S(2)}, u32[]{:S(2)}) %all-to-all-start.2) | async-done | bytes 524320 | tf_op jit(solution)/shard_map/all_to_all | solution.py:287
  26.4 29.3 %all_to_all.25.exchanged = bf16[4,136,1280]{2,1,0:T(8,128)(2,1)S(1)} all-to-all(bf16[4,136,1280]{2,1,0:T(8,128)(2,1)} %shard_map.113), channel_id=1, replica_groups={{0,1,2,3},{4,5,6,7},{8,9,10,11},{12,13,14,15},{16,17,18,19},{20,21,22,2..., dimensions={0} | all-to-all | bytes 2785280 | tf_op jit(solution)/shard_map/all_to_all | solution.py:287
  55.7 4.0 %all-to-all-start.3 = ((bf16[4,128,512]{2,1,0:T(8,128)(2,1)}), bf16[4,128,512]{2,1,0:T(8,128)(2,1)S(1)}, u32[]{:S(2)}, u32[]{:S(2)}) async-start(bf16[4,128,512]{2,1,0:T(8,128)(2,1)} %get-tuple-element.21), calls=%async_computation.3 | async-start | bytes 1048576 | tf_op jit(solution)/shard_map/all_to_all | solution.py:287
  59.8 0.1 shard_map.114.counts
  59.9 5.1 %collective-permute-start.1 = (f32[16,128]{1,0:T(8,128)S(1)}, f32[16,128]{1,0:T(8,128)S(1)}, u32[]{:S(2)}, u32[]{:S(2)}) collective-permute-start(f32[16,128]{1,0:T(8,128)S(1)} %shard_map.114.counts), channel_id=1, source_target_pairs={{0,28},{1,29},{2,30},{3,31},{4,0},{5,1},{6,2},{7,3},{8,4},{9,5},{1... | collective-permute-start | bytes 24584 | tf_op jit(solution)/shard_map/ppermute | solution.py:283
  65.0 1.9 %collective-permute-start = (f32[16,128]{1,0:T(8,128)S(1)}, f32[16,128]{1,0:T(8,128)S(1)}, u32[]{:S(2)}, u32[]{:S(2)}) collective-permute-start(f32[16,128]{1,0:T(8,128)S(1)} %shard_map.114.counts), channel_id=1, source_target_pairs={{0,4},{1,5},{2,6},{3,7},{4,8},{5,9},{6,10},{7,11},{8,12},{9,13},{1... | collective-permute-start | bytes 24584 | tf_op jit(solution)/shard_map/ppermute | solution.py:283
  66.9 3.7 %collective-permute-done.before = f32[16,128]{1,0:T(8,128)S(1)} collective-permute-done((f32[16,128]{1,0:T(8,128)S(1)}, f32[16,128]{1,0:T(8,128)S(1)}, u32[]{:S(2)}, u32[]{:S(2)}) %collective-permute-start) | collective-permute-done | bytes 8224 | tf_op jit(solution)/shard_map/ppermute | solution.py:283
  70.6 0.4 shard_map.115.weights
  70.9 1.2 shard_map.118
  72.2 1.9 %collective-permute-start.2 = (bf16[512,256]{1,0:T(8,128)(2,1)}, bf16[512,256]{1,0:T(8,128)(2,1)S(1)}, u32[]{:S(2)}, u32[]{:S(2)}) collective-permute-start(bf16[512,256]{1,0:T(8,128)(2,1)} %get-tuple-element.19), channel_id=1, source_target_pairs={{0,4},{1,5},{2,6},{3,7},{4,8},{5,9},{6,10},{7,11},{8,12},{9,13},{1... | collective-permute-start | bytes 786440 | tf_op jit(solution)/shard_map/ppermute | solution.py:283
  74.1 4.6 %collective-permute-start.6 = (bf16[512,256]{1,0:T(8,128)(2,1)}, bf16[512,256]{1,0:T(8,128)(2,1)}, u32[]{:S(2)}, u32[]{:S(2)}) collective-permute-start(bf16[512,256]{1,0:T(8,128)(2,1)} %get-tuple-element.22), channel_id=1, source_target_pairs={{0,28},{1,29},{2,30},{3,31},{4,0},{5,1},{6,2},{7,3},{8,4},{9,5},{1... | collective-permute-start | bytes 786440 | tf_op jit(solution)/shard_map/ppermute | solution.py:283
  78.7 6.7 %all-to-all-start.1 = ((bf16[4,128,768]{2,1,0:T(8,128)(2,1)}), bf16[4,128,768]{2,1,0:T(8,128)(2,1)S(1)}, u32[]{:S(2)}, u32[]{:S(2)}) async-start(bf16[4,128,768]{2,1,0:T(8,128)(2,1)} %get-tuple-element.17), calls=%async_computation.1 | async-start | bytes 1572864 | tf_op jit(solution)/shard_map/all_to_all | solution.py:287
  85.3 0.7 copy-done.1
  86.0 0.9 copy-done.2
  87.0 0.4 shard_map.119
  87.4 1.9 %collective-permute-start.3 = (bf16[1024,256]{1,0:T(8,128)(2,1)S(1)}, bf16[1024,256]{1,0:T(8,128)(2,1)S(1)}, u32[]{:S(2)}, u32[]{:S(2)}) collective-permute-start(bf16[1024,256]{1,0:T(8,128)(2,1)S(1)} %shard_map.119), channel_id=1, source_target_pairs={{0,4},{1,5},{2,6},{3,7},{4,8},{5,9},{6,10},{7,11},{8,12},{9,13},{1... | collective-permute-start | bytes 1572872 | tf_op jit(solution)/shard_map/ppermute | solution.py:283
  89.4 1.4 shard_map.122
  90.8 4.6 %collective-permute-start.7 = (bf16[1024,256]{1,0:T(8,128)(2,1)S(1)}, bf16[1024,256]{1,0:T(8,128)(2,1)S(1)}, u32[]{:S(2)}, u32[]{:S(2)}) collective-permute-start(bf16[1024,256]{1,0:T(8,128)(2,1)S(1)} %shard_map.122), channel_id=1, source_target_pairs={{0,28},{1,29},{2,30},{3,31},{4,0},{5,1},{6,2},{7,3},{8,4},{9,5},{1... | collective-permute-start | bytes 1572872 | tf_op jit(solution)/shard_map/ppermute | solution.py:283
  95.3 3.9 %collective-permute-done.3.received = bf16[1024,256]{1,0:T(8,128)(2,1)S(1)} collective-permute-done((bf16[1024,256]{1,0:T(8,128)(2,1)S(1)}, bf16[1024,256]{1,0:T(8,128)(2,1)S(1)}, u32[]{:S(2)}, u32[]{:S(2)}) %collective-permute-start.3) | collective-permute-done | bytes 524320 | tf_op jit(solution)/shard_map/ppermute | solution.py:283
  99.2 0.4 shard_map.120
  99.7 1.9 %collective-permute-start.4 = (bf16[1024,256]{1,0:T(8,128)(2,1)S(1)}, bf16[1024,256]{1,0:T(8,128)(2,1)}, u32[]{:S(2)}, u32[]{:S(2)}) collective-permute-start(bf16[1024,256]{1,0:T(8,128)(2,1)S(1)} %shard_map.120), channel_id=1, source_target_pairs={{0,4},{1,5},{2,6},{3,7},{4,8},{5,9},{6,10},{7,11},{8,12},{9,13},{1... | collective-permute-start | bytes 1572872 | tf_op jit(solution)/shard_map/ppermute | solution.py:283
  101.6 0.5 shard_map.123
  102.1 5.1 %collective-permute-start.8 = (bf16[1024,256]{1,0:T(8,128)(2,1)S(1)}, bf16[1024,256]{1,0:T(8,128)(2,1)}, u32[]{:S(2)}, u32[]{:S(2)}) collective-permute-start(bf16[1024,256]{1,0:T(8,128)(2,1)S(1)} %shard_map.123), channel_id=1, source_target_pairs={{0,28},{1,29},{2,30},{3,31},{4,0},{5,1},{6,2},{7,3},{8,4},{9,5},{1... | collective-permute-start | bytes 1572872 | tf_op jit(solution)/shard_map/ppermute | solution.py:283
  107.2 7.8 %collective-permute-done.4.received = bf16[1024,256]{1,0:T(8,128)(2,1)} collective-permute-done((bf16[1024,256]{1,0:T(8,128)(2,1)S(1)}, bf16[1024,256]{1,0:T(8,128)(2,1)}, u32[]{:S(2)}, u32[]{:S(2)}) %collective-permute-start.4) | collective-permute-done | bytes 524320 | tf_op jit(solution)/shard_map/ppermute | solution.py:283
  115.0 1.5 shard_map.121
  116.5 0.0 copy-start.10
  116.5 0.0 copy-start.8
  116.5 2.1 %collective-permute-start.5 = (bf16[1024,256]{1,0:T(8,128)(2,1)S(1)}, bf16[1024,256]{1,0:T(8,128)(2,1)}, u32[]{:S(2)}, u32[]{:S(2)}) collective-permute-start(bf16[1024,256]{1,0:T(8,128)(2,1)S(1)} %shard_map.121), channel_id=1, source_target_pairs={{0,4},{1,5},{2,6},{3,7},{4,8},{5,9},{6,10},{7,11},{8,12},{9,13},{1... | collective-permute-start | bytes 1572872 | tf_op jit(solution)/shard_map/ppermute | solution.py:283
  118.6 1.5 shard_map.124
  120.1 4.6 %collective-permute-start.9 = (bf16[1024,256]{1,0:T(8,128)(2,1)S(1)}, bf16[1024,256]{1,0:T(8,128)(2,1)}, u32[]{:S(2)}, u32[]{:S(2)}) collective-permute-start(bf16[1024,256]{1,0:T(8,128)(2,1)S(1)} %shard_map.124), channel_id=1, source_target_pairs={{0,28},{1,29},{2,30},{3,31},{4,0},{5,1},{6,2},{7,3},{8,4},{9,5},{1... | collective-permute-start | bytes 1572872 | tf_op jit(solution)/shard_map/ppermute | solution.py:283
  124.6 0.1 copy.12
  124.7 0.1 broadcast_in_dim.9
  124.8 0.1 reshape.20.offsets
  124.9 0.9 copy-done.3
  125.8 0.9 copy-done.5
  126.7 0.9 copy-done.7
  127.6 0.4 shard_map.117
  128.1 4.3 %collective-permute-done.5.up = bf16[1024,256]{1,0:T(8,128)(2,1)} collective-permute-done((bf16[1024,256]{1,0:T(8,128)(2,1)S(1)}, bf16[1024,256]{1,0:T(8,128)(2,1)}, u32[]{:S(2)}, u32[]{:S(2)}) %collective-permute-start.5) | collective-permute-done | bytes 524320 | tf_op jit(solution)/shard_map/ppermute | solution.py:283
  132.4 3.2 %collective-permute-done.9.down = bf16[1024,256]{1,0:T(8,128)(2,1)} collective-permute-done((bf16[1024,256]{1,0:T(8,128)(2,1)S(1)}, bf16[1024,256]{1,0:T(8,128)(2,1)}, u32[]{:S(2)}, u32[]{:S(2)}) %collective-permute-start.9) | collective-permute-done | bytes 524320 | tf_op jit(solution)/shard_map/ppermute | solution.py:283
  135.6 5.0 %shard_map.125 = (bf16[1024,256]{1,0:T(8,128)(2,1)S(1)}, f32[64,256]{1,0:T(8,128)S(1)}, bf16[16,64,256]{2,1,0:T(8,128)(2,1)}) custom-call(f32[1024,256]{1,0:T(8,128)S(1)} %get-tuple-element.18.product, bf16[1024,256]{1,0:T(8,128)(2,1)} %collective-permute-done.5.up, bf16[1024,256]{1,0:T(8,128)(2,1)} %collective-permute-done.9.down, ...), custom_call_target="tpu_custom_call" | custom-call | flops 1610612736 | bytes 2097152 | tf_op jit(solution)/shard_map/pallas_call | solution.py:355
  140.7 19.8 %all-to-all-start.4 = ((bf16[16,64,256]{2,1,0:T(8,128)(2,1)}), bf16[16,64,256]{2,1,0:T(8,128)(2,1)S(1)}, u32[]{:S(2)}, u32[]{:S(2)}) async-start(bf16[16,64,256]{2,1,0:T(8,128)(2,1)} %get-tuple-element.31), calls=%async_computation.4 | async-start | bytes 1048576 | tf_op jit(solution)/shard_map/all_to_all | solution.py:369
  160.5 1.8 %shard_map.126 = bf16[1024,256]{1,0:T(8,128)(2,1)} custom-call(bf16[1024,256]{1,0:T(8,128)(2,1)S(1)} %bitcast.9, bf16[1024,256]{1,0:T(8,128)(2,1)S(1)} %get-tuple-element.29.summed, f32[64,256]{1,0:T(8,128)S(1)} %get-tuple-element.30.decoded, s32[16,256]{1,0:T(8,128)S(1)} %reshape.20.offsets, bf16[256,256]{1,0:T(8,128)(2,1)S(1)} %copy-done.6, ...), custom_call_target="tpu_custom_call" | custom-call | flops 1610612736 | bytes 2097152 | tf_op jit(solution)/shard_map/pallas_call | solution.py:370
  162.2 7.9 %all-to-all-done.4.parts = bf16[16,64,256]{2,1,0:T(8,128)(2,1)S(1)} async-done(((bf16[16,64,256]{2,1,0:T(8,128)(2,1)}), bf16[16,64,256]{2,1,0:T(8,128)(2,1)S(1)}, u32[]{:S(2)}, u32[]{:S(2)}) %all-to-all-start.4) | async-done | bytes 524320 | tf_op jit(solution)/shard_map/all_to_all | solution.py:369
  170.1 1.7 %shard_map.127 = bf16[1024,256]{1,0:T(8,128)(2,1)} custom-call(bf16[16,64,256]{2,1,0:T(8,128)(2,1)S(1)} %all-to-all-done.4.parts, s32[16,256]{1,0:T(8,128)S(1)} %reshape.20.offsets, bf16[256,256]{1,0:T(8,128)(2,1)S(1)} %copy-done.6, bf16[256,256]{1,0:T(8,128)(2,1)S(1)} %copy-done.4, bf16[64,192]{1,0:T(8,128)(2,1)S(1)} %copy-done.9), custom_call_target="tpu_custom_call" | custom-call | flops 1610612736 | bytes 2097152 | tf_op jit(solution)/shard_map/pallas_call | solution.py:371
  (24 shorter events, 0.1 us)
Async XLA Ops:
  0.6 13.9 %copy-start.11 = (s32[1,1,128]{2,1,0:T(1,128)S(1)}, s32[1,1,128]{2,1,0:T(1,128)}, u32[]{:S(2)}) copy-start(s32[1,1,128]{2,1,0:T(1,128)} %param.12) | copy-start | bytes 1540
  3.6 22.8 %all-to-all-start.2 = ((bf16[4,128,512]{2,1,0:T(8,128)(2,1)}), bf16[4,128,512]{2,1,0:T(8,128)(2,1)S(1)}, u32[]{:S(2)}, u32[]{:S(2)}) async-start(bf16[4,128,512]{2,1,0:T(8,128)(2,1)} %get-tuple-element.20), calls=%async_computation.2 | async-start | bytes 1048576 | tf_op jit(solution)/shard_map/all_to_all | solution.py:287
  55.7 22.9 %all-to-all-start.3 = ((bf16[4,128,512]{2,1,0:T(8,128)(2,1)}), bf16[4,128,512]{2,1,0:T(8,128)(2,1)S(1)}, u32[]{:S(2)}, u32[]{:S(2)}) async-start(bf16[4,128,512]{2,1,0:T(8,128)(2,1)} %get-tuple-element.21), calls=%async_computation.3 | async-start | bytes 1048576 | tf_op jit(solution)/shard_map/all_to_all | solution.py:287
  59.9 7.0 %collective-permute-start.1 = (f32[16,128]{1,0:T(8,128)S(1)}, f32[16,128]{1,0:T(8,128)S(1)}, u32[]{:S(2)}, u32[]{:S(2)}) collective-permute-start(f32[16,128]{1,0:T(8,128)S(1)} %shard_map.114.counts), channel_id=1, source_target_pairs={{0,28},{1,29},{2,30},{3,31},{4,0},{5,1},{6,2},{7,3},{8,4},{9,5},{1... | collective-permute-start | bytes 24584 | tf_op jit(solution)/shard_map/ppermute | solution.py:283
  65.0 5.6 %collective-permute-start = (f32[16,128]{1,0:T(8,128)S(1)}, f32[16,128]{1,0:T(8,128)S(1)}, u32[]{:S(2)}, u32[]{:S(2)}) collective-permute-start(f32[16,128]{1,0:T(8,128)S(1)} %shard_map.114.counts), channel_id=1, source_target_pairs={{0,4},{1,5},{2,6},{3,7},{4,8},{5,9},{6,10},{7,11},{8,12},{9,13},{1... | collective-permute-start | bytes 24584 | tf_op jit(solution)/shard_map/ppermute | solution.py:283
  72.2 13.2 %collective-permute-start.2 = (bf16[512,256]{1,0:T(8,128)(2,1)}, bf16[512,256]{1,0:T(8,128)(2,1)S(1)}, u32[]{:S(2)}, u32[]{:S(2)}) collective-permute-start(bf16[512,256]{1,0:T(8,128)(2,1)} %get-tuple-element.19), channel_id=1, source_target_pairs={{0,4},{1,5},{2,6},{3,7},{4,8},{5,9},{6,10},{7,11},{8,12},{9,13},{1... | collective-permute-start | bytes 786440 | tf_op jit(solution)/shard_map/ppermute | solution.py:283
  74.1 15.3 %collective-permute-start.6 = (bf16[512,256]{1,0:T(8,128)(2,1)}, bf16[512,256]{1,0:T(8,128)(2,1)}, u32[]{:S(2)}, u32[]{:S(2)}) collective-permute-start(bf16[512,256]{1,0:T(8,128)(2,1)} %get-tuple-element.22), channel_id=1, source_target_pairs={{0,28},{1,29},{2,30},{3,31},{4,0},{5,1},{6,2},{7,3},{8,4},{9,5},{1... | collective-permute-start | bytes 786440 | tf_op jit(solution)/shard_map/ppermute | solution.py:283
  78.7 28.5 %all-to-all-start.1 = ((bf16[4,128,768]{2,1,0:T(8,128)(2,1)}), bf16[4,128,768]{2,1,0:T(8,128)(2,1)S(1)}, u32[]{:S(2)}, u32[]{:S(2)}) async-start(bf16[4,128,768]{2,1,0:T(8,128)(2,1)} %get-tuple-element.17), calls=%async_computation.1 | async-start | bytes 1572864 | tf_op jit(solution)/shard_map/all_to_all | solution.py:287
  85.3 0.7 copy-start.1
  86.0 0.9 copy-start.2
  87.4 11.8 %collective-permute-start.3 = (bf16[1024,256]{1,0:T(8,128)(2,1)S(1)}, bf16[1024,256]{1,0:T(8,128)(2,1)S(1)}, u32[]{:S(2)}, u32[]{:S(2)}) collective-permute-start(bf16[1024,256]{1,0:T(8,128)(2,1)S(1)} %shard_map.119), channel_id=1, source_target_pairs={{0,4},{1,5},{2,6},{3,7},{4,8},{5,9},{6,10},{7,11},{8,12},{9,13},{1... | collective-permute-start | bytes 1572872 | tf_op jit(solution)/shard_map/ppermute | solution.py:283
  90.8 10.9 %collective-permute-start.7 = (bf16[1024,256]{1,0:T(8,128)(2,1)S(1)}, bf16[1024,256]{1,0:T(8,128)(2,1)S(1)}, u32[]{:S(2)}, u32[]{:S(2)}) collective-permute-start(bf16[1024,256]{1,0:T(8,128)(2,1)S(1)} %shard_map.122), channel_id=1, source_target_pairs={{0,28},{1,29},{2,30},{3,31},{4,0},{5,1},{6,2},{7,3},{8,4},{9,5},{1... | collective-permute-start | bytes 1572872 | tf_op jit(solution)/shard_map/ppermute | solution.py:283
  99.7 15.3 %collective-permute-start.4 = (bf16[1024,256]{1,0:T(8,128)(2,1)S(1)}, bf16[1024,256]{1,0:T(8,128)(2,1)}, u32[]{:S(2)}, u32[]{:S(2)}) collective-permute-start(bf16[1024,256]{1,0:T(8,128)(2,1)S(1)} %shard_map.120), channel_id=1, source_target_pairs={{0,4},{1,5},{2,6},{3,7},{4,8},{5,9},{6,10},{7,11},{8,12},{9,13},{1... | collective-permute-start | bytes 1572872 | tf_op jit(solution)/shard_map/ppermute | solution.py:283
  102.1 16.5 %collective-permute-start.8 = (bf16[1024,256]{1,0:T(8,128)(2,1)S(1)}, bf16[1024,256]{1,0:T(8,128)(2,1)}, u32[]{:S(2)}, u32[]{:S(2)}) collective-permute-start(bf16[1024,256]{1,0:T(8,128)(2,1)S(1)} %shard_map.123), channel_id=1, source_target_pairs={{0,28},{1,29},{2,30},{3,31},{4,0},{5,1},{6,2},{7,3},{8,4},{9,5},{1... | collective-permute-start | bytes 1572872 | tf_op jit(solution)/shard_map/ppermute | solution.py:283
  116.5 8.2 %copy-start.10 = (s32[1,16,4]{1,2,0:T(4,128)S(1)}, s32[1,16,4]{1,2,0:T(4,128)}, u32[]{:S(2)}) copy-start(s32[1,16,4]{1,2,0:T(4,128)} %param.13) | copy-start | bytes 772
  116.5 8.4 %copy-start = (bf16[1,1024,256]{2,1,0:T(8,128)(2,1)S(1)}, bf16[1,1024,256]{2,1,0:T(8,128)(2,1)}, u32[]{:S(2)}) copy-start(bf16[1,1024,256]{2,1,0:T(8,128)(2,1)} %param.14) | copy-start | bytes 1572868
  116.5 8.4 %copy-start.8 = (bf16[64,192]{1,0:T(8,128)(2,1)S(1)}, bf16[64,192]{1,0:T(8,128)(2,1)}, u32[]{:S(2)}) copy-start(bf16[64,192]{1,0:T(8,128)(2,1)} %constant.12.clone.rest_2_) | copy-start | bytes 73732
  116.5 15.9 %collective-permute-start.5 = (bf16[1024,256]{1,0:T(8,128)(2,1)S(1)}, bf16[1024,256]{1,0:T(8,128)(2,1)}, u32[]{:S(2)}, u32[]{:S(2)}) collective-permute-start(bf16[1024,256]{1,0:T(8,128)(2,1)S(1)} %shard_map.121), channel_id=1, source_target_pairs={{0,4},{1,5},{2,6},{3,7},{4,8},{5,9},{6,10},{7,11},{8,12},{9,13},{1... | collective-permute-start | bytes 1572872 | tf_op jit(solution)/shard_map/ppermute | solution.py:283
  120.1 15.6 %collective-permute-start.9 = (bf16[1024,256]{1,0:T(8,128)(2,1)S(1)}, bf16[1024,256]{1,0:T(8,128)(2,1)}, u32[]{:S(2)}, u32[]{:S(2)}) collective-permute-start(bf16[1024,256]{1,0:T(8,128)(2,1)S(1)} %shard_map.124), channel_id=1, source_target_pairs={{0,28},{1,29},{2,30},{3,31},{4,0},{5,1},{6,2},{7,3},{8,4},{9,5},{1... | collective-permute-start | bytes 1572872 | tf_op jit(solution)/shard_map/ppermute | solution.py:283
  124.9 0.9 copy-start.3
  125.8 0.9 copy-start.5
  126.7 0.9 copy-start.7
  135.6 24.8 %copy-start.4 = (bf16[256,256]{1,0:T(8,128)(2,1)S(1)}, bf16[256,256]{1,0:T(8,128)(2,1)}, u32[]{:S(2)}) copy-start(bf16[256,256]{1,0:T(8,128)(2,1)} %constant.11.clone.rest_1_.low) | copy-start | bytes 393220
  135.6 24.8 %copy-start.6 = (bf16[256,256]{1,0:T(8,128)(2,1)S(1)}, bf16[256,256]{1,0:T(8,128)(2,1)}, u32[]{:S(2)}) copy-start(bf16[256,256]{1,0:T(8,128)(2,1)} %constant.10.clone.rest_0_.high) | copy-start | bytes 393220
  135.6 24.8 %copy-start.9 = (bf16[64,192]{1,0:T(8,128)(2,1)S(1)}, bf16[64,192]{1,0:T(8,128)(2,1)}, u32[]{:S(2)}) copy-start(bf16[64,192]{1,0:T(8,128)(2,1)} %constant.13.clone.back_table) | copy-start | bytes 73732
  140.7 29.4 %all-to-all-start.4 = ((bf16[16,64,256]{2,1,0:T(8,128)(2,1)}), bf16[16,64,256]{2,1,0:T(8,128)(2,1)S(1)}, u32[]{:S(2)}, u32[]{:S(2)}) async-start(bf16[16,64,256]{2,1,0:T(8,128)(2,1)} %get-tuple-element.31), calls=%async_computation.4 | async-start | bytes 1048576 | tf_op jit(solution)/shard_map/all_to_all | solution.py:369

commit v5 on v3

--- a/solution.py
+++ b/solution.py
@@ -102,11 +102,16 @@
         copy.wait()
 
 
-def late_kernel(rows, third, second, first, sem):
-    deep = third.shape[0]
-    width = third.shape[2] // 2
+def late_kernel(rows, *rest):
+    third, (second, first, sem) = rest[:-3], rest[-3:]
+    deep = len(third)
+    width = second.shape[2] // 2
+    me = lax.axis_index("shard") % deep
     moves = []
-    for target, owners in ((third, (3, -3)), (second, (2, -2)), (first, (1, -1, 0))):
+    for k in range(deep):
+        for j, owner in enumerate((3, -3)):
+            moves.append((owner, (me + k) % deep, third[k].at[:, pl.ds(j * width, width)]))
+    for target, owners in ((second, (2, -2)), (first, (1, -1, 0))):
         for z in range(deep):
             for j, owner in enumerate(owners):
                 moves.append((owner, z, target.at[z, :, pl.ds(j * width, width)]))
@@ -138,16 +143,21 @@
     down[...] = dot(weights[half:], columns, dims).astype(jnp.bfloat16)
 
 
-def near_kernel(start, top, weights, received, exchanged, out):
+def far_near_kernel(start, top, weights, received, *rest):
+    parts, out = rest[:-1], rest[-1]
+    width = out.shape[1]
+    columns = jnp.concatenate([part[:, start : start + width] for part in parts], axis=0)
+    total = dot(weights[...], columns, ((1,), (0,)))
+    rows = received.shape[0]
+    here, other = (slice(0, rows), slice(rows, None)) if top else (slice(rows, None), slice(0, rows))
+    out[here] = (total[here] + received[...].astype(jnp.float32)).astype(jnp.bfloat16)
+    out[other] = total[other].astype(jnp.bfloat16)
+
+
+def near_kernel(start, weights, received, exchanged, out):
     width = out.shape[1]
     total = dot(weights[...], gathered(exchanged, start, width), ((1,), (0,)))
-    rows = received.shape[0]
-    if rows == out.shape[0]:
-        out[...] = (total + received[...].astype(jnp.float32)).astype(jnp.bfloat16)
-    else:
-        here, other = (slice(0, rows), slice(rows, None)) if top else (slice(rows, None), slice(0, rows))
-        out[here] = (total[here] + received[...].astype(jnp.float32)).astype(jnp.bfloat16)
-        out[other] = total[other].astype(jnp.bfloat16)
+    out[...] = (total + received[...].astype(jnp.float32)).astype(jnp.bfloat16)
 
 
 def base_kernel(weights, exchanged, momentum, offsets, *rest):
@@ -159,17 +169,28 @@
         out[...] = table[...]
 
 
-def forward_kernel(product, up, down, momentum, offsets, high, low, ahead, ones, summed, decoded, sent, packed, held, sem):
+def forward_kernel(
+    product, up, down, momentum, offsets, high, low, ahead, ones, summed, decoded, sent, packed, held, parts, sem
+):
     table = (high[...], low[...])
     per = TILE // BLOCK
     rows = TILE // STRIDE
+    fetches = []
+    for i in range(product.shape[0] // TILE):
+        there = pl.ds(i * TILE, TILE)
+        pair = [pltpu.make_async_copy(x.at[there], parts.at[j, there], sem.at[1 + j, i]) for j, x in enumerate((up, down))]
+        fetches.append(pair)
+        for copy in pair:
+            copy.start()
     copies = []
     for i in range(product.shape[0] // TILE):
         here = slice(i * TILE, (i + 1) * TILE)
-        total = product[here] + up[here].astype(jnp.float32) + down[here].astype(jnp.float32)
+        for copy in fetches[i]:
+            copy.wait()
+        total = product[here] + parts[0, here].astype(jnp.float32) + parts[1, here].astype(jnp.float32)
         gradient = total.astype(jnp.bfloat16)
         held[here] = gradient
-        copies.append(pltpu.make_async_copy(held.at[pl.ds(i * TILE, TILE)], summed.at[pl.ds(i * TILE, TILE)], sem.at[i]))
+        copies.append(pltpu.make_async_copy(held.at[pl.ds(i * TILE, TILE)], summed.at[pl.ds(i * TILE, TILE)], sem.at[0, i]))
         copies[-1].start()
         value = BETA * momentum[here].astype(jnp.float32) + gradient.astype(jnp.float32)
         spectrum = right(left(ahead[...], value), table, 1)
@@ -296,15 +317,16 @@
         notes.append(along_line(extra, k))
     notes = [notes[0], notes[2], notes[1], notes[3]]
 
-    third, second, first = call(
+    *third, second, first = call(
         late_kernel,
-        [shaped(deep, tokens, 2 * width)] * 2 + [shaped(deep, tokens, 3 * width)],
+        [shaped(tokens, 2 * width)] * deep + [shaped(deep, tokens, 2 * width), shaped(deep, tokens, 3 * width)],
         work,
         (pltpu.SemaphoreType.DMA((7 * deep,)),),
         [apart],
         FULL,
     )(rows)
-    third = exchange(third)
+    for k in (2, 1, 3):
+        third[k] = along_line(third[k], k)
     second = exchange(second)
     first = exchange(first)
 
@@ -317,15 +339,17 @@
         down = across(down, -1)
         return up, down
 
-    def near(start, top, received, exchanged):
-        kernel = functools.partial(near_kernel, start, top)
-        return call(kernel, shaped(panel, width), work)(weights, received, exchanged)
+    def near(kernel, received, *given):
+        return call(kernel, shaped(panel, width), work)(weights, received, *given)
 
     def both(up, down, exchanged):
-        return near(0, True, up, exchanged), near(width, False, down, exchanged)
+        first_half, second_half = functools.partial(near_kernel, 0), functools.partial(near_kernel, width)
+        return near(first_half, up, exchanged), near(second_half, down, exchanged)
 
     up, down = ring(up, down)
-    up, down = ring(*both(up, down, third))
+    up = near(functools.partial(far_near_kernel, 0, True), up, *third)
+    down = near(functools.partial(far_near_kernel, width, False), down, *third)
+    up, down = ring(up, down)
     up, down = ring(*both(up, down, second))
     up, down = ring(*both(up, down, first))
 
@@ -344,11 +368,13 @@
     summed, decoded, sent = pl.pallas_call(
         forward_kernel,
         out_shape=(shaped(panel, width), shaped(kept, width, dtype=jnp.float32), shaped(groups, kept, width)),
+        in_specs=[whole, apart, apart] + [whole] * 6,
         out_specs=(apart, whole, whole),
         scratch_shapes=(
             pltpu.VMEM((kept, width), jnp.float32),
             pltpu.VMEM((panel, width), jnp.bfloat16),
-            pltpu.SemaphoreType.DMA((panel // TILE,)),
+            pltpu.VMEM((2, panel, width), jnp.bfloat16),
+            pltpu.SemaphoreType.DMA((3, panel // TILE)),
         ),
         compiler_params=pltpu.CompilerParams(vmem_limit_bytes=GRANT),
         cost_estimate=pl.CostEstimate(flops=flops, bytes_accessed=2 << 20, transcendentals=0),

time: 179 us -> 180 us (level)
  the two profiles are of different devices: /device:TPU:24 before, /device:TPU:152 now
where the time goes in v5:
time: 180 us; the launch traced here: 179 us
  starting transfers between devices  87.7 us (49%)
  waiting for transfers between devices  64.9 us (36%)
  Pallas kernels  20.9 us (12%)
  local copies, waits for them, and re-layouts  4.3 us (2%)
    ppermute x10, starting transfers between devices, across(): return lax.ppermute(x, 'shard', pairs)  35.5 us
    ppermute x6, starting transfers between devices, along_line(): return lax.ppermute(x, 'shard', pairs)  24.5 us
    all_to_all x3, starting transfers between devices, exchange(): return lax.all_to_all(x, 'shard', 0, 0, axis_index_groups=lines, tiled=True)  23.3 us
    all_to_all x3, waiting for transfers between devices, exchange(): return lax.all_to_all(x, 'shard', 0, 0, axis_index_groups=lines, tiled=True)  19.4 us
    ppermute x6, waiting for transfers between devices, along_line(): return lax.ppermute(x, 'shard', pairs)  18.9 us
    ppermute x10, waiting for transfers between devices, across(): return lax.ppermute(x, 'shard', pairs)  17.6 us
    all_to_all x1, waiting for transfers between devices, step(): parts = lax.all_to_all(sent, 'rep', 0, 0, tiled=True)  9.06 us
    pallas_call x1, Pallas kernels, step(): pl.pallas_call(forward_kernel, out_shape=(shaped(panel, width), shaped(ke...  5.02 us
  transfers between devices with their start and end apart: 20, of which 8 were waited for; matrix products, arithmetic and copies ran while one was open for 1% of the time, Pallas kernels for 6%

profile of v5, /device:TPU:152, one launch (start us, length us, event | category | flops | bytes accessed | tf_op | source)
XLA Modules:
  0.0 179.0 jit_solution(9746300411650632318)
XLA Ops:
  0.6 2.6 %shard_map.113 = bf16[4,128,1280]{2,1,0:T(8,128)(2,1)} custom-call(bf16[128,8192]{1,0:T(8,128)(2,1)} %bitcast.9, bf16[128,1024]{1,0:T(8,128)(2,1)} %bitcast.11), custom_call_target="tpu_custom_call" | custom-call | flops 268435456 | bytes 2097152 | tf_op jit(solution)/shard_map/pallas_call | solution.py:296
  3.3 9.1 %all-to-all-start = ((bf16[4,128,1280]{2,1,0:T(8,128)(2,1)}), bf16[4,128,1280]{2,1,0:T(8,128)(2,1)S(1)}, u32[]{:S(2)}, u32[]{:S(2)}) async-start(bf16[4,128,1280]{2,1,0:T(8,128)(2,1)} %shard_map.113), calls=%async_computation | async-start | bytes 2621440 | tf_op jit(solution)/shard_map/all_to_all | solution.py:286
  12.3 0.1 convert_reduce_fusion
  12.5 2.4 %collective-permute-start.1 = (bf16[16,128]{1,0:T(8,128)(2,1)S(1)}, bf16[16,128]{1,0:T(8,128)(2,1)S(1)}, u32[]{:S(2)}, u32[]{:S(2)}) collective-permute-start(bf16[16,128]{1,0:T(8,128)(2,1)S(1)} %broadcast_in_dim.19), channel_id=1, source_target_pairs={{0,28},{1,29},{2,30},{3,31},{4,0},{5,1},{6,2},{7,3},{8,4},{9,5},{1... | collective-permute-start | bytes 12296 | tf_op jit(solution)/shard_map/ppermute | solution.py:282
  14.9 4.6 %collective-permute-start = (bf16[16,128]{1,0:T(8,128)(2,1)S(1)}, bf16[16,128]{1,0:T(8,128)(2,1)S(1)}, u32[]{:S(2)}, u32[]{:S(2)}) collective-permute-start(bf16[16,128]{1,0:T(8,128)(2,1)S(1)} %broadcast_in_dim.19), channel_id=1, source_target_pairs={{0,4},{1,5},{2,6},{3,7},{4,8},{5,9},{6,10},{7,11},{8,12},{9,13},{1... | collective-permute-start | bytes 12296 | tf_op jit(solution)/shard_map/ppermute | solution.py:282
  19.6 3.0 %shard_map.115 = (bf16[128,512]{1,0:T(8,128)(2,1)}, bf16[128,512]{1,0:T(8,128)(2,1)}, bf16[128,512]{1,0:T(8,128)(2,1)}, bf16[128,512]{1,0:T(8,128)(2,1)}, bf16[4...) custom-call(bf16[128,8192]{1,0:T(8,128)(2,1)} %bitcast.10), custom_call_target="tpu_custom_call" | custom-call | flops 268435456 | bytes 2097152 | tf_op jit(solution)/shard_map/pallas_call | solution.py:320
  22.6 19.4 %all-to-all-done.exchanged = bf16[4,128,1280]{2,1,0:T(8,128)(2,1)S(1)} async-done(((bf16[4,128,1280]{2,1,0:T(8,128)(2,1)}), bf16[4,128,1280]{2,1,0:T(8,128)(2,1)S(1)}, u32[]{:S(2)}, u32[]{:S(2)}) %all-to-all-start) | async-done | bytes 1310752 | tf_op jit(solution)/shard_map/all_to_all | solution.py:286
  42.0 6.5 %all-to-all-start.2 = ((bf16[4,128,512]{2,1,0:T(8,128)(2,1)}), bf16[4,128,512]{2,1,0:T(8,128)(2,1)S(1)}, u32[]{:S(2)}, u32[]{:S(2)}) async-start(bf16[4,128,512]{2,1,0:T(8,128)(2,1)} %get-tuple-element.27), calls=%async_computation.2 | async-start | bytes 1048576 | tf_op jit(solution)/shard_map/all_to_all | solution.py:286
  48.6 1.9 %collective-permute-start.4 = (bf16[32,128]{1,0:T(8,128)(2,1)S(1)}, bf16[32,128]{1,0:T(8,128)(2,1)S(1)}, u32[]{:S(2)}, u32[]{:S(2)}) collective-permute-start(bf16[32,128]{1,0:T(8,128)(2,1)S(1)} %pad_maximum_fusion.rest_0_), channel_id=1, source_target_pairs={{0,3},{1,0},{2,1},{3,2},{4,7},{5,4},{6,5},{7,6},{8,11},{9,8},{10,9... | collective-permute-start | bytes 24584 | tf_op jit(solution)/shard_map/ppermute | solution.py:278
  50.5 7.8 %collective-permute-start.3 = (bf16[32,128]{1,0:T(8,128)(2,1)S(1)}, bf16[32,128]{1,0:T(8,128)(2,1)S(1)}, u32[]{:S(2)}, u32[]{:S(2)}) collective-permute-start(bf16[32,128]{1,0:T(8,128)(2,1)S(1)} %pad_maximum_fusion.rest_0_), channel_id=1, source_target_pairs={{0,2},{1,3},{2,0},{3,1},{4,6},{5,7},{6,4},{7,5},{8,10},{9,11},{10,... | collective-permute-start | bytes 24584 | tf_op jit(solution)/shard_map/ppermute | solution.py:278
  58.4 3.7 %collective-permute-start.2 = (bf16[32,128]{1,0:T(8,128)(2,1)S(1)}, bf16[32,128]{1,0:T(8,128)(2,1)S(1)}, u32[]{:S(2)}, u32[]{:S(2)}) collective-permute-start(bf16[32,128]{1,0:T(8,128)(2,1)S(1)} %pad_maximum_fusion.rest_0_), channel_id=1, source_target_pairs={{0,1},{1,2},{2,3},{3,0},{4,5},{5,6},{6,7},{7,4},{8,9},{9,10},{10,1... | collective-permute-start | bytes 24584 | tf_op jit(solution)/shard_map/ppermute | solution.py:278
  62.1 2.0 %collective-permute-done.4.rest_3_ = bf16[32,128]{1,0:T(8,128)(2,1)S(1)} collective-permute-done((bf16[32,128]{1,0:T(8,128)(2,1)S(1)}, bf16[32,128]{1,0:T(8,128)(2,1)S(1)}, u32[]{:S(2)}, u32[]{:S(2)}) %collective-permute-start.4) | collective-permute-done | bytes 8224 | tf_op jit(solution)/shard_map/ppermute | solution.py:278
  64.0 0.8 collective-permute-done.2.rest_1_
  64.8 0.4 shard_map.114.weights
  65.2 1.2 shard_map.117
  66.4 4.8 %collective-permute-start.5 = (bf16[512,256]{1,0:T(8,128)(2,1)}, bf16[512,256]{1,0:T(8,128)(2,1)S(1)}, u32[]{:S(2)}, u32[]{:S(2)}) collective-permute-start(bf16[512,256]{1,0:T(8,128)(2,1)} %get-tuple-element.22), channel_id=1, source_target_pairs={{0,4},{1,5},{2,6},{3,7},{4,8},{5,9},{6,10},{7,11},{8,12},{9,13},{1... | collective-permute-start | bytes 786440 | tf_op jit(solution)/shard_map/ppermute | solution.py:282
  71.3 1.9 %collective-permute-start.12 = (bf16[512,256]{1,0:T(8,128)(2,1)}, bf16[512,256]{1,0:T(8,128)(2,1)S(1)}, u32[]{:S(2)}, u32[]{:S(2)}) collective-permute-start(bf16[512,256]{1,0:T(8,128)(2,1)} %get-tuple-element.28), channel_id=1, source_target_pairs={{0,28},{1,29},{2,30},{3,31},{4,0},{5,1},{6,2},{7,3},{8,4},{9,5},{1... | collective-permute-start | bytes 786440 | tf_op jit(solution)/shard_map/ppermute | solution.py:282
  73.2 4.9 %collective-permute-start.6 = (bf16[128,512]{1,0:T(8,128)(2,1)}, bf16[128,512]{1,0:T(8,128)(2,1)S(1)}, u32[]{:S(2)}, u32[]{:S(2)}) collective-permute-start(bf16[128,512]{1,0:T(8,128)(2,1)} %get-tuple-element.24), channel_id=1, source_target_pairs={{0,1},{1,2},{2,3},{3,0},{4,5},{5,6},{6,7},{7,4},{8,9},{9,10},{10,1... | collective-permute-start | bytes 393224 | tf_op jit(solution)/shard_map/ppermute | solution.py:278
  78.1 4.3 %collective-permute-start.7 = (bf16[128,512]{1,0:T(8,128)(2,1)}, bf16[128,512]{1,0:T(8,128)(2,1)S(1)}, u32[]{:S(2)}, u32[]{:S(2)}) collective-permute-start(bf16[128,512]{1,0:T(8,128)(2,1)} %get-tuple-element.25), channel_id=1, source_target_pairs={{0,2},{1,3},{2,0},{3,1},{4,6},{5,7},{6,4},{7,5},{8,10},{9,11},{10,... | collective-permute-start | bytes 393224 | tf_op jit(solution)/shard_map/ppermute | solution.py:278
  82.4 1.9 %collective-permute-start.8 = (bf16[128,512]{1,0:T(8,128)(2,1)S(1)}, bf16[128,512]{1,0:T(8,128)(2,1)S(1)}, u32[]{:S(2)}, u32[]{:S(2)}) collective-permute-start(bf16[128,512]{1,0:T(8,128)(2,1)S(1)} %copy-done.10), channel_id=1, source_target_pairs={{0,3},{1,0},{2,1},{3,2},{4,7},{5,4},{6,5},{7,6},{8,11},{9,8},{10,9... | collective-permute-start | bytes 393224 | tf_op jit(solution)/shard_map/ppermute | solution.py:278
  84.3 7.8 %all-to-all-start.1 = ((bf16[4,128,768]{2,1,0:T(8,128)(2,1)}), bf16[4,128,768]{2,1,0:T(8,128)(2,1)S(1)}, u32[]{:S(2)}, u32[]{:S(2)}) async-start(bf16[4,128,768]{2,1,0:T(8,128)(2,1)} %get-tuple-element.20), calls=%async_computation.1 | async-start | bytes 1572864 | tf_op jit(solution)/shard_map/all_to_all | solution.py:286
  92.1 16.1 %collective-permute-done.8.rest_3_ = bf16[128,512]{1,0:T(8,128)(2,1)S(1)} collective-permute-done((bf16[128,512]{1,0:T(8,128)(2,1)S(1)}, bf16[128,512]{1,0:T(8,128)(2,1)S(1)}, u32[]{:S(2)}, u32[]{:S(2)}) %collective-permute-start.8) | collective-permute-done | bytes 131104 | tf_op jit(solution)/shard_map/ppermute | solution.py:278
  108.2 0.4 shard_map.118
  108.6 4.6 %collective-permute-start.9 = (bf16[1024,256]{1,0:T(8,128)(2,1)S(1)}, bf16[1024,256]{1,0:T(8,128)(2,1)S(1)}, u32[]{:S(2)}, u32[]{:S(2)}) collective-permute-start(bf16[1024,256]{1,0:T(8,128)(2,1)S(1)} %shard_map.118), channel_id=1, source_target_pairs={{0,4},{1,5},{2,6},{3,7},{4,8},{5,9},{6,10},{7,11},{8,12},{9,13},{1... | collective-permute-start | bytes 1572872 | tf_op jit(solution)/shard_map/ppermute | solution.py:282
  113.3 0.4 shard_map.121
  113.8 1.9 %collective-permute-start.13 = (bf16[1024,256]{1,0:T(8,128)(2,1)S(1)}, bf16[1024,256]{1,0:T(8,128)(2,1)S(1)}, u32[]{:S(2)}, u32[]{:S(2)}) collective-permute-start(bf16[1024,256]{1,0:T(8,128)(2,1)S(1)} %shard_map.121), channel_id=1, source_target_pairs={{0,28},{1,29},{2,30},{3,31},{4,0},{5,1},{6,2},{7,3},{8,4},{9,5},{1... | collective-permute-start | bytes 1572872 | tf_op jit(solution)/shard_map/ppermute | solution.py:282
  115.7 7.5 %collective-permute-done.9.received = bf16[1024,256]{1,0:T(8,128)(2,1)S(1)} collective-permute-done((bf16[1024,256]{1,0:T(8,128)(2,1)S(1)}, bf16[1024,256]{1,0:T(8,128)(2,1)S(1)}, u32[]{:S(2)}, u32[]{:S(2)}) %collective-permute-start.9) | collective-permute-done | bytes 524320 | tf_op jit(solution)/shard_map/ppermute | solution.py:282
  123.2 0.4 shard_map.119
  123.6 5.4 %collective-permute-start.10 = (bf16[1024,256]{1,0:T(8,128)(2,1)S(1)}, bf16[1024,256]{1,0:T(8,128)(2,1)}, u32[]{:S(2)}, u32[]{:S(2)}) collective-permute-start(bf16[1024,256]{1,0:T(8,128)(2,1)S(1)} %shard_map.119), channel_id=1, source_target_pairs={{0,4},{1,5},{2,6},{3,7},{4,8},{5,9},{6,10},{7,11},{8,12},{9,13},{1... | collective-permute-start | bytes 1572872 | tf_op jit(solution)/shard_map/ppermute | solution.py:282
  129.1 0.5 shard_map.122
  129.5 1.9 %collective-permute-start.14 = (bf16[1024,256]{1,0:T(8,128)(2,1)S(1)}, bf16[1024,256]{1,0:T(8,128)(2,1)}, u32[]{:S(2)}, u32[]{:S(2)}) collective-permute-start(bf16[1024,256]{1,0:T(8,128)(2,1)S(1)} %shard_map.122), channel_id=1, source_target_pairs={{0,28},{1,29},{2,30},{3,31},{4,0},{5,1},{6,2},{7,3},{8,4},{9,5},{1... | collective-permute-start | bytes 1572872 | tf_op jit(solution)/shard_map/ppermute | solution.py:282
  131.5 4.3 %collective-permute-done.10.received = bf16[1024,256]{1,0:T(8,128)(2,1)} collective-permute-done((bf16[1024,256]{1,0:T(8,128)(2,1)S(1)}, bf16[1024,256]{1,0:T(8,128)(2,1)}, u32[]{:S(2)}, u32[]{:S(2)}) %collective-permute-start.10) | collective-permute-done | bytes 524320 | tf_op jit(solution)/shard_map/ppermute | solution.py:282
  135.7 1.5 shard_map.120
  137.2 5.8 %collective-permute-start.11 = (bf16[1024,256]{1,0:T(8,128)(2,1)S(1)}, bf16[1024,256]{1,0:T(8,128)(2,1)}, u32[]{:S(2)}, u32[]{:S(2)}) collective-permute-start(bf16[1024,256]{1,0:T(8,128)(2,1)S(1)} %shard_map.120), channel_id=1, source_target_pairs={{0,4},{1,5},{2,6},{3,7},{4,8},{5,9},{6,10},{7,11},{8,12},{9,13},{1... | collective-permute-start | bytes 1572872 | tf_op jit(solution)/shard_map/ppermute | solution.py:282
  143.1 1.5 shard_map.123
  144.6 1.9 %collective-permute-start.15 = (bf16[1024,256]{1,0:T(8,128)(2,1)S(1)}, bf16[1024,256]{1,0:T(8,128)(2,1)}, u32[]{:S(2)}, u32[]{:S(2)}) collective-permute-start(bf16[1024,256]{1,0:T(8,128)(2,1)S(1)} %shard_map.123), channel_id=1, source_target_pairs={{0,28},{1,29},{2,30},{3,31},{4,0},{5,1},{6,2},{7,3},{8,4},{9,5},{1... | collective-permute-start | bytes 1572872 | tf_op jit(solution)/shard_map/ppermute | solution.py:282
  146.6 0.7 broadcast_in_dim.21
  147.3 0.8 reshape.9.offsets
  148.2 0.9 copy-done.3
  149.1 0.9 copy-done.5
  150.0 0.8 copy-done.6
  150.7 0.4 shard_map.116
  151.2 5.8 %collective-permute-done.15.down = bf16[1024,256]{1,0:T(8,128)(2,1)} collective-permute-done((bf16[1024,256]{1,0:T(8,128)(2,1)S(1)}, bf16[1024,256]{1,0:T(8,128)(2,1)}, u32[]{:S(2)}, u32[]{:S(2)}) %collective-permute-start.15) | collective-permute-done | bytes 524320 | tf_op jit(solution)/shard_map/ppermute | solution.py:282
  157.0 5.0 %shard_map.124 = (bf16[1024,256]{1,0:T(8,128)(2,1)S(1)}, f32[64,256]{1,0:T(8,128)S(1)}, bf16[16,64,256]{2,1,0:T(8,128)(2,1)}) custom-call(f32[1024,256]{1,0:T(8,128)S(1)} %get-tuple-element.21.product, bf16[1024,256]{1,0:T(8,128)(2,1)} %collective-permute-done.11.up, bf16[1024,256]{1,0:T(8,128)(2,1)} %collective-permute-done.15.down, ...), custom_call_target="tpu_custom_call" | custom-call | flops 1610612736 | bytes 2097152 | tf_op jit(solution)/shard_map/pallas_call | solution.py:368
  162.0 4.4 %all-to-all-start.3 = ((bf16[16,64,256]{2,1,0:T(8,128)(2,1)}), bf16[16,64,256]{2,1,0:T(8,128)(2,1)S(1)}, u32[]{:S(2)}, u32[]{:S(2)}) async-start(bf16[16,64,256]{2,1,0:T(8,128)(2,1)} %get-tuple-element.37), calls=%async_computation.3 | async-start | bytes 1048576 | tf_op jit(solution)/shard_map/all_to_all | solution.py:382
  166.5 1.7 shard_map.125
  168.2 9.1 %all-to-all-done.3.parts = bf16[16,64,256]{2,1,0:T(8,128)(2,1)S(1)} async-done(((bf16[16,64,256]{2,1,0:T(8,128)(2,1)}), bf16[16,64,256]{2,1,0:T(8,128)(2,1)S(1)}, u32[]{:S(2)}, u32[]{:S(2)}) %all-to-all-start.3) | async-done | bytes 524320 | tf_op jit(solution)/shard_map/all_to_all | solution.py:382
  177.3 1.7 shard_map.126
  (38 shorter events, 0.3 us)
Async XLA Ops:
  3.3 9.1 %copy-start.9 = (s32[1,1,128]{2,1,0:T(1,128)S(1)}, s32[1,1,128]{2,1,0:T(1,128)}, u32[]{:S(2)}) copy-start(s32[1,1,128]{2,1,0:T(1,128)} %param.12) | copy-start | bytes 1540
  3.3 38.7 %all-to-all-start = ((bf16[4,128,1280]{2,1,0:T(8,128)(2,1)}), bf16[4,128,1280]{2,1,0:T(8,128)(2,1)S(1)}, u32[]{:S(2)}, u32[]{:S(2)}) async-start(bf16[4,128,1280]{2,1,0:T(8,128)(2,1)} %shard_map.113), calls=%async_computation | async-start | bytes 2621440 | tf_op jit(solution)/shard_map/all_to_all | solution.py:286
  12.5 36.0 %collective-permute-start.1 = (bf16[16,128]{1,0:T(8,128)(2,1)S(1)}, bf16[16,128]{1,0:T(8,128)(2,1)S(1)}, u32[]{:S(2)}, u32[]{:S(2)}) collective-permute-start(bf16[16,128]{1,0:T(8,128)(2,1)S(1)} %broadcast_in_dim.19), channel_id=1, source_target_pairs={{0,28},{1,29},{2,30},{3,31},{4,0},{5,1},{6,2},{7,3},{8,4},{9,5},{1... | collective-permute-start | bytes 12296 | tf_op jit(solution)/shard_map/ppermute | solution.py:282
  14.9 33.6 %collective-permute-start = (bf16[16,128]{1,0:T(8,128)(2,1)S(1)}, bf16[16,128]{1,0:T(8,128)(2,1)S(1)}, u32[]{:S(2)}, u32[]{:S(2)}) collective-permute-start(bf16[16,128]{1,0:T(8,128)(2,1)S(1)} %broadcast_in_dim.19), channel_id=1, source_target_pairs={{0,4},{1,5},{2,6},{3,7},{4,8},{5,9},{6,10},{7,11},{8,12},{9,13},{1... | collective-permute-start | bytes 12296 | tf_op jit(solution)/shard_map/ppermute | solution.py:282
  42.0 42.3 %all-to-all-start.2 = ((bf16[4,128,512]{2,1,0:T(8,128)(2,1)}), bf16[4,128,512]{2,1,0:T(8,128)(2,1)S(1)}, u32[]{:S(2)}, u32[]{:S(2)}) async-start(bf16[4,128,512]{2,1,0:T(8,128)(2,1)} %get-tuple-element.27), calls=%async_computation.2 | async-start | bytes 1048576 | tf_op jit(solution)/shard_map/all_to_all | solution.py:286
  48.6 15.4 %collective-permute-start.4 = (bf16[32,128]{1,0:T(8,128)(2,1)S(1)}, bf16[32,128]{1,0:T(8,128)(2,1)S(1)}, u32[]{:S(2)}, u32[]{:S(2)}) collective-permute-start(bf16[32,128]{1,0:T(8,128)(2,1)S(1)} %pad_maximum_fusion.rest_0_), channel_id=1, source_target_pairs={{0,3},{1,0},{2,1},{3,2},{4,7},{5,4},{6,5},{7,6},{8,11},{9,8},{10,9... | collective-permute-start | bytes 24584 | tf_op jit(solution)/shard_map/ppermute | solution.py:278
  50.5 13.5 %collective-permute-start.3 = (bf16[32,128]{1,0:T(8,128)(2,1)S(1)}, bf16[32,128]{1,0:T(8,128)(2,1)S(1)}, u32[]{:S(2)}, u32[]{:S(2)}) collective-permute-start(bf16[32,128]{1,0:T(8,128)(2,1)S(1)} %pad_maximum_fusion.rest_0_), channel_id=1, source_target_pairs={{0,2},{1,3},{2,0},{3,1},{4,6},{5,7},{6,4},{7,5},{8,10},{9,11},{10,... | collective-permute-start | bytes 24584 | tf_op jit(solution)/shard_map/ppermute | solution.py:278
  58.4 6.4 %collective-permute-start.2 = (bf16[32,128]{1,0:T(8,128)(2,1)S(1)}, bf16[32,128]{1,0:T(8,128)(2,1)S(1)}, u32[]{:S(2)}, u32[]{:S(2)}) collective-permute-start(bf16[32,128]{1,0:T(8,128)(2,1)S(1)} %pad_maximum_fusion.rest_0_), channel_id=1, source_target_pairs={{0,1},{1,2},{2,3},{3,0},{4,5},{5,6},{6,7},{7,4},{8,9},{9,10},{10,1... | collective-permute-start | bytes 24584 | tf_op jit(solution)/shard_map/ppermute | solution.py:278
  65.2 17.2 %copy-start.10 = (bf16[128,512]{1,0:T(8,128)(2,1)S(1)}, bf16[128,512]{1,0:T(8,128)(2,1)}, u32[]{:S(2)}) copy-start(bf16[128,512]{1,0:T(8,128)(2,1)} %get-tuple-element.26) | copy-start | bytes 393220
  66.4 41.8 %copy-start = (bf16[128,512]{1,0:T(8,128)(2,1)S(1)}, bf16[128,512]{1,0:T(8,128)(2,1)}, u32[]{:S(2)}) copy-start(bf16[128,512]{1,0:T(8,128)(2,1)} %get-tuple-element.23.rest_0_) | copy-start | bytes 393220
  66.4 41.8 %collective-permute-start.5 = (bf16[512,256]{1,0:T(8,128)(2,1)}, bf16[512,256]{1,0:T(8,128)(2,1)S(1)}, u32[]{:S(2)}, u32[]{:S(2)}) collective-permute-start(bf16[512,256]{1,0:T(8,128)(2,1)} %get-tuple-element.22), channel_id=1, source_target_pairs={{0,4},{1,5},{2,6},{3,7},{4,8},{5,9},{6,10},{7,11},{8,12},{9,13},{1... | collective-permute-start | bytes 786440 | tf_op jit(solution)/shard_map/ppermute | solution.py:282
  71.3 42.0 %collective-permute-start.12 = (bf16[512,256]{1,0:T(8,128)(2,1)}, bf16[512,256]{1,0:T(8,128)(2,1)S(1)}, u32[]{:S(2)}, u32[]{:S(2)}) collective-permute-start(bf16[512,256]{1,0:T(8,128)(2,1)} %get-tuple-element.28), channel_id=1, source_target_pairs={{0,28},{1,29},{2,30},{3,31},{4,0},{5,1},{6,2},{7,3},{8,4},{9,5},{1... | collective-permute-start | bytes 786440 | tf_op jit(solution)/shard_map/ppermute | solution.py:282
  73.2 18.9 %collective-permute-start.6 = (bf16[128,512]{1,0:T(8,128)(2,1)}, bf16[128,512]{1,0:T(8,128)(2,1)S(1)}, u32[]{:S(2)}, u32[]{:S(2)}) collective-permute-start(bf16[128,512]{1,0:T(8,128)(2,1)} %get-tuple-element.24), channel_id=1, source_target_pairs={{0,1},{1,2},{2,3},{3,0},{4,5},{5,6},{6,7},{7,4},{8,9},{9,10},{10,1... | collective-permute-start | bytes 393224 | tf_op jit(solution)/shard_map/ppermute | solution.py:278
  78.1 14.0 %collective-permute-start.7 = (bf16[128,512]{1,0:T(8,128)(2,1)}, bf16[128,512]{1,0:T(8,128)(2,1)S(1)}, u32[]{:S(2)}, u32[]{:S(2)}) collective-permute-start(bf16[128,512]{1,0:T(8,128)(2,1)} %get-tuple-element.25), channel_id=1, source_target_pairs={{0,2},{1,3},{2,0},{3,1},{4,6},{5,7},{6,4},{7,5},{8,10},{9,11},{10,... | collective-permute-start | bytes 393224 | tf_op jit(solution)/shard_map/ppermute | solution.py:278
  82.4 25.8 %collective-permute-start.8 = (bf16[128,512]{1,0:T(8,128)(2,1)S(1)}, bf16[128,512]{1,0:T(8,128)(2,1)S(1)}, u32[]{:S(2)}, u32[]{:S(2)}) collective-permute-start(bf16[128,512]{1,0:T(8,128)(2,1)S(1)} %copy-done.10), channel_id=1, source_target_pairs={{0,3},{1,0},{2,1},{3,2},{4,7},{5,4},{6,5},{7,6},{8,11},{9,8},{10,9... | collective-permute-start | bytes 393224 | tf_op jit(solution)/shard_map/ppermute | solution.py:278
  84.3 47.1 %all-to-all-start.1 = ((bf16[4,128,768]{2,1,0:T(8,128)(2,1)}), bf16[4,128,768]{2,1,0:T(8,128)(2,1)S(1)}, u32[]{:S(2)}, u32[]{:S(2)}) async-start(bf16[4,128,768]{2,1,0:T(8,128)(2,1)} %get-tuple-element.20), calls=%async_computation.1 | async-start | bytes 1572864 | tf_op jit(solution)/shard_map/all_to_all | solution.py:286
  108.6 14.5 %collective-permute-start.9 = (bf16[1024,256]{1,0:T(8,128)(2,1)S(1)}, bf16[1024,256]{1,0:T(8,128)(2,1)S(1)}, u32[]{:S(2)}, u32[]{:S(2)}) collective-permute-start(bf16[1024,256]{1,0:T(8,128)(2,1)S(1)} %shard_map.118), channel_id=1, source_target_pairs={{0,4},{1,5},{2,6},{3,7},{4,8},{5,9},{6,10},{7,11},{8,12},{9,13},{1... | collective-permute-start | bytes 1572872 | tf_op jit(solution)/shard_map/ppermute | solution.py:282
  113.8 15.3 %collective-permute-start.13 = (bf16[1024,256]{1,0:T(8,128)(2,1)S(1)}, bf16[1024,256]{1,0:T(8,128)(2,1)S(1)}, u32[]{:S(2)}, u32[]{:S(2)}) collective-permute-start(bf16[1024,256]{1,0:T(8,128)(2,1)S(1)} %shard_map.121), channel_id=1, source_target_pairs={{0,28},{1,29},{2,30},{3,31},{4,0},{5,1},{6,2},{7,3},{8,4},{9,5},{1... | collective-permute-start | bytes 1572872 | tf_op jit(solution)/shard_map/ppermute | solution.py:282
  123.6 12.1 %collective-permute-start.10 = (bf16[1024,256]{1,0:T(8,128)(2,1)S(1)}, bf16[1024,256]{1,0:T(8,128)(2,1)}, u32[]{:S(2)}, u32[]{:S(2)}) collective-permute-start(bf16[1024,256]{1,0:T(8,128)(2,1)S(1)} %shard_map.119), channel_id=1, source_target_pairs={{0,4},{1,5},{2,6},{3,7},{4,8},{5,9},{6,10},{7,11},{8,12},{9,13},{1... | collective-permute-start | bytes 1572872 | tf_op jit(solution)/shard_map/ppermute | solution.py:282
  129.5 13.6 %collective-permute-start.14 = (bf16[1024,256]{1,0:T(8,128)(2,1)S(1)}, bf16[1024,256]{1,0:T(8,128)(2,1)}, u32[]{:S(2)}, u32[]{:S(2)}) collective-permute-start(bf16[1024,256]{1,0:T(8,128)(2,1)S(1)} %shard_map.122), channel_id=1, source_target_pairs={{0,28},{1,29},{2,30},{3,31},{4,0},{5,1},{6,2},{7,3},{8,4},{9,5},{1... | collective-permute-start | bytes 1572872 | tf_op jit(solution)/shard_map/ppermute | solution.py:282
  137.2 9.3 %copy-start.8 = (s32[1,16,4]{1,2,0:T(4,128)S(1)}, s32[1,16,4]{1,2,0:T(4,128)}, u32[]{:S(2)}) copy-start(s32[1,16,4]{1,2,0:T(4,128)} %param.13) | copy-start | bytes 772
  137.2 10.9 %copy-start.1 = (bf16[1,1024,256]{2,1,0:T(8,128)(2,1)S(1)}, bf16[1,1024,256]{2,1,0:T(8,128)(2,1)}, u32[]{:S(2)}) copy-start(bf16[1,1024,256]{2,1,0:T(8,128)(2,1)} %param.14) | copy-start | bytes 1572868
  137.2 10.9 %copy-start.2 = (bf16[256,256]{1,0:T(8,128)(2,1)S(1)}, bf16[256,256]{1,0:T(8,128)(2,1)}, u32[]{:S(2)}) copy-start(bf16[256,256]{1,0:T(8,128)(2,1)} %constant.19.clone.rest_1_.low) | copy-start | bytes 393220
  137.2 13.9 %collective-permute-start.11 = (bf16[1024,256]{1,0:T(8,128)(2,1)S(1)}, bf16[1024,256]{1,0:T(8,128)(2,1)}, u32[]{:S(2)}, u32[]{:S(2)}) collective-permute-start(bf16[1024,256]{1,0:T(8,128)(2,1)S(1)} %shard_map.120), channel_id=1, source_target_pairs={{0,4},{1,5},{2,6},{3,7},{4,8},{5,9},{6,10},{7,11},{8,12},{9,13},{1... | collective-permute-start | bytes 1572872 | tf_op jit(solution)/shard_map/ppermute | solution.py:282
  144.6 12.4 %collective-permute-start.15 = (bf16[1024,256]{1,0:T(8,128)(2,1)S(1)}, bf16[1024,256]{1,0:T(8,128)(2,1)}, u32[]{:S(2)}, u32[]{:S(2)}) collective-permute-start(bf16[1024,256]{1,0:T(8,128)(2,1)S(1)} %shard_map.123), channel_id=1, source_target_pairs={{0,28},{1,29},{2,30},{3,31},{4,0},{5,1},{6,2},{7,3},{8,4},{9,5},{1... | collective-permute-start | bytes 1572872 | tf_op jit(solution)/shard_map/ppermute | solution.py:282
  148.2 0.9 copy-start.3
  149.1 0.9 copy-start.5
  150.0 0.8 copy-start.6
  157.0 9.5 %copy-start.4 = (bf16[256,256]{1,0:T(8,128)(2,1)S(1)}, bf16[256,256]{1,0:T(8,128)(2,1)}, u32[]{:S(2)}) copy-start(bf16[256,256]{1,0:T(8,128)(2,1)} %constant.18.clone.rest_0_.high) | copy-start | bytes 393220
  157.0 9.5 %copy-start.7 = (bf16[64,192]{1,0:T(8,128)(2,1)S(1)}, bf16[64,192]{1,0:T(8,128)(2,1)}, u32[]{:S(2)}) copy-start(bf16[64,192]{1,0:T(8,128)(2,1)} %constant.21.clone.back_table) | copy-start | bytes 73732
  162.0 15.3 %all-to-all-start.3 = ((bf16[16,64,256]{2,1,0:T(8,128)(2,1)}), bf16[16,64,256]{2,1,0:T(8,128)(2,1)S(1)}, u32[]{:S(2)}, u32[]{:S(2)}) async-start(bf16[16,64,256]{2,1,0:T(8,128)(2,1)} %get-tuple-element.37), calls=%async_computation.3 | async-start | bytes 1048576 | tf_op jit(solution)/shard_map/all_to_all | solution.py:382

commit v6 on v5

--- a/solution.py
+++ b/solution.py
@@ -89,33 +89,29 @@
     return copies
 
 
-def early_kernel(rows, grads, out, sem, given):
-    deep = out.shape[0]
+def gather_kernel(rows, grads, *rest):
+    *outs, sem, given = rest
+    deep = outs[0].shape[0]
+    early, second, first = outs[:3]
+    third, own = outs[3 : 3 + deep], outs[3 + deep :]
     panel = grads.shape[1]
-    width = out.shape[2] - panel
-    moves = [(4, z, out.at[z, :, pl.ds(panel, width)]) for z in range(deep)]
-    copies = fetch(rows, deep, width, moves, sem)
-    for z in range(deep):
-        copies.append(pltpu.make_async_copy(grads, out.at[z, :, pl.ds(0, panel)], given.at[z]))
-        copies[-1].start()
-    for copy in copies:
-        copy.wait()
-
-
-def late_kernel(rows, *rest):
-    third, (second, first, sem) = rest[:-3], rest[-3:]
-    deep = len(third)
-    width = second.shape[2] // 2
+    width = early.shape[2] - panel
     me = lax.axis_index("shard") % deep
-    moves = []
+    moves = [(4, z, early.at[z, :, pl.ds(panel, width)]) for z in range(deep)]
     for k in range(deep):
+        z = (me + k) % deep
         for j, owner in enumerate((3, -3)):
-            moves.append((owner, (me + k) % deep, third[k].at[:, pl.ds(j * width, width)]))
-    for target, owners in ((second, (2, -2)), (first, (1, -1, 0))):
+            moves.append((owner, z, third[k].at[:, pl.ds(j * width, width)]))
+        moves.append((0, z, own[k]))
+    for target, owners in ((second, (2, -2)), (first, (1, -1))):
         for z in range(deep):
             for j, owner in enumerate(owners):
                 moves.append((owner, z, target.at[z, :, pl.ds(j * width, width)]))
-    for copy in fetch(rows, deep, width, moves, sem):
+    copies = fetch(rows, deep, width, moves, sem)
+    for z in range(deep):
+        copies.append(pltpu.make_async_copy(grads, early.at[z, :, pl.ds(0, panel)], given.at[z]))
+        copies[-1].start()
+    for copy in copies:
         copy.wait()
 
 
@@ -160,9 +156,12 @@
     out[...] = (total + received[...].astype(jnp.float32)).astype(jnp.bfloat16)
 
 
-def base_kernel(weights, exchanged, momentum, offsets, *rest):
-    tables, (product, kept, offsets_out, *tables_out) = rest[: len(rest) // 2 - 1], rest[len(rest) // 2 - 1 :]
-    product[...] = dot(weights[...], gathered(exchanged, 2 * product.shape[1], product.shape[1]), ((1,), (0,)))
+def base_kernel(count, *rest):
+    parts, (weights, momentum, offsets, *rest) = rest[:count], rest[count:]
+    half = len(rest) // 2 - 1
+    tables, (product, kept, offsets_out, *tables_out) = rest[:half], rest[half:]
+    columns = jnp.concatenate([part[...] for part in parts], axis=0)
+    product[...] = dot(weights[...], columns, ((1,), (0,)))
     kept[...] = momentum[...]
     offsets_out[...] = offsets[...]
     for table, out in zip(tables, tables_out):
@@ -293,14 +292,18 @@
     apart = pl.BlockSpec(memory_space=pltpu.HBM)
     work = 2 * panel * deep * tokens * width
 
-    early = call(
-        early_kernel,
-        shaped(deep, tokens, panel + width),
+    early, second, first, *others = call(
+        gather_kernel,
+        [shaped(deep, tokens, panel + width)]
+        + [shaped(deep, tokens, 2 * width)] * 2
+        + [shaped(tokens, 2 * width)] * deep
+        + [shaped(tokens, width)] * deep,
         work,
-        (pltpu.SemaphoreType.DMA((deep,)), pltpu.SemaphoreType.DMA((deep,))),
+        (pltpu.SemaphoreType.DMA((8 * deep,)), pltpu.SemaphoreType.DMA((deep,))),
         [apart, apart],
         FULL,
     )(rows, grads)
+    third, own = others[:deep], others[deep:]
     early = exchange(early)
 
     documents = lax.broadcasted_iota(jnp.int32, (DOCS, tokens), 0)
@@ -317,16 +320,10 @@
         notes.append(along_line(extra, k))
     notes = [notes[0], notes[2], notes[1], notes[3]]
 
-    *third, second, first = call(
-        late_kernel,
-        [shaped(tokens, 2 * width)] * deep + [shaped(deep, tokens, 2 * width), shaped(deep, tokens, 3 * width)],
-        work,
-        (pltpu.SemaphoreType.DMA((7 * deep,)),),
-        [apart],
-        FULL,
-    )(rows)
     for k in (2, 1, 3):
         third[k] = along_line(third[k], k)
+    for k in (2, 1, 3):
+        own[k] = along_line(own[k], k)
     second = exchange(second)
     first = exchange(first)
 
@@ -360,11 +357,11 @@
     flops = 6 * 2 * 2 * panel * TILE * TILE
     tables = (high, low, ahead, ones)
     product, momentum_near, wide_near, *tables_near = call(
-        base_kernel,
+        functools.partial(base_kernel, deep),
         [shaped(panel, width, dtype=jnp.float32), shaped(panel, width), shaped(*wide.shape, dtype=jnp.int32)]
         + [shaped(*table.shape) for table in tables],
         work,
-    )(weights, first, momentum[0], wide, *tables)
+    )(*own, weights, momentum[0], wide, *tables)
     summed, decoded, sent = pl.pallas_call(
         forward_kernel,
         out_shape=(shaped(panel, width), shaped(kept, width, dtype=jnp.float32), shaped(groups, kept, width)),

time: 180 us -> 182 us (1.011)
  the two profiles are of different devices: /device:TPU:152 before, /device:TPU:1 now
where the time goes in v6:
time: 182 us; the launch traced here: 181 us
  starting transfers between devices  115 us (63%)
  waiting for transfers between devices  41.8 us (23%)
  Pallas kernels  19.6 us (11%)
  local copies, waits for them, and re-layouts  3.8 us (2%)
    ppermute x9, starting transfers between devices, along_line(): return lax.ppermute(x, 'shard', pairs)  42.8 us
    ppermute x10, starting transfers between devices, across(): return lax.ppermute(x, 'shard', pairs)  33.7 us
    all_to_all x3, starting transfers between devices, exchange(): return lax.all_to_all(x, 'shard', 0, 0, axis_index_groups=lines, tiled=True)  28.7 us
    all_to_all x3, waiting for transfers between devices, exchange(): return lax.all_to_all(x, 'shard', 0, 0, axis_index_groups=lines, tiled=True)  16 us
    ppermute x9, waiting for transfers between devices, along_line(): return lax.ppermute(x, 'shard', pairs)  13.3 us
    all_to_all x1, starting transfers between devices, step(): parts = lax.all_to_all(sent, 'rep', 0, 0, tiled=True)  9.5 us
    all_to_all x1, waiting for transfers between devices, step(): parts = lax.all_to_all(sent, 'rep', 0, 0, tiled=True)  7.89 us
    pallas_call x6, Pallas kernels, near(): return call(kernel, shaped(panel, width), work)(weights, received, *given)  5.88 us
  transfers between devices with their start and end apart: 23, of which 10 were waited for; matrix products, arithmetic and copies ran while one was open for 0% of the time, Pallas kernels for 5%

profile of v6, /device:TPU:1, one launch (start us, length us, event | category | flops | bytes accessed | tf_op | source)
XLA Modules:
  0.0 181.2 jit_solution(13999499428454216469)
XLA Ops:
  0.6 4.0 %shard_map.113 = (bf16[4,128,1280]{2,1,0:T(8,128)(2,1)}, bf16[4,128,512]{2,1,0:T(8,128)(2,1)}, bf16[4,128,512]{2,1,0:T(8,128)(2,1)}, bf16[128,512]{1,0:T(8,128)(...) custom-call(bf16[128,8192]{1,0:T(8,128)(2,1)} %bitcast.9, ...), custom_call_target="tpu_custom_call" | custom-call | flops 268435456 | bytes 2097152 | tf_op jit(solution)/shard_map/pallas_call | solution.py:295
  4.6 10.8 %all-to-all-start = ((bf16[4,128,1280]{2,1,0:T(8,128)(2,1)}), bf16[4,128,1280]{2,1,0:T(8,128)(2,1)S(1)}, u32[]{:S(2)}, u32[]{:S(2)}) async-start(bf16[4,128,1280]{2,1,0:T(8,128)(2,1)} %get-tuple-element.29), calls=%async_computation | async-start | bytes 2621440 | tf_op jit(solution)/shard_map/all_to_all | solution.py:285
  15.7 3.2 %collective-permute-start.3 = (bf16[16,128]{1,0:T(8,128)(2,1)S(1)}, bf16[16,128]{1,0:T(8,128)(2,1)S(1)}, u32[]{:S(2)}, u32[]{:S(2)}) collective-permute-start(bf16[16,128]{1,0:T(8,128)(2,1)S(1)} %broadcast_in_dim.19), channel_id=1, source_target_pairs={{0,4},{1,5},{2,6},{3,7},{4,8},{5,9},{6,10},{7,11},{8,12},{9,13},{1... | collective-permute-start | bytes 12296 | tf_op jit(solution)/shard_map/ppermute | solution.py:281
  18.9 3.8 %collective-permute-start.4 = (bf16[16,128]{1,0:T(8,128)(2,1)S(1)}, bf16[16,128]{1,0:T(8,128)(2,1)S(1)}, u32[]{:S(2)}, u32[]{:S(2)}) collective-permute-start(bf16[16,128]{1,0:T(8,128)(2,1)S(1)} %broadcast_in_dim.19), channel_id=1, source_target_pairs={{0,28},{1,29},{2,30},{3,31},{4,0},{5,1},{6,2},{7,3},{8,4},{9,5},{1... | collective-permute-start | bytes 12296 | tf_op jit(solution)/shard_map/ppermute | solution.py:281
  22.7 15.1 %all-to-all-done.exchanged = bf16[4,128,1280]{2,1,0:T(8,128)(2,1)S(1)} async-done(((bf16[4,128,1280]{2,1,0:T(8,128)(2,1)}), bf16[4,128,1280]{2,1,0:T(8,128)(2,1)S(1)}, u32[]{:S(2)}, u32[]{:S(2)}) %all-to-all-start) | async-done | bytes 1310752 | tf_op jit(solution)/shard_map/all_to_all | solution.py:285
  37.8 12.1 %all-to-all-start.1 = ((bf16[4,128,512]{2,1,0:T(8,128)(2,1)}), bf16[4,128,512]{2,1,0:T(8,128)(2,1)S(1)}, u32[]{:S(2)}, u32[]{:S(2)}) async-start(bf16[4,128,512]{2,1,0:T(8,128)(2,1)} %get-tuple-element.36), calls=%async_computation.1 | async-start | bytes 1048576 | tf_op jit(solution)/shard_map/all_to_all | solution.py:285
  50.0 4.3 %collective-permute-start.5 = (bf16[32,128]{1,0:T(8,128)(2,1)S(1)}, bf16[32,128]{1,0:T(8,128)(2,1)S(1)}, u32[]{:S(2)}, u32[]{:S(2)}) collective-permute-start(bf16[32,128]{1,0:T(8,128)(2,1)S(1)} %pad_maximum_fusion.rest_0_), channel_id=1, source_target_pairs={{0,1},{1,2},{2,3},{3,0},{4,5},{5,6},{6,7},{7,4},{8,9},{9,10},{10,1... | collective-permute-start | bytes 24584 | tf_op jit(solution)/shard_map/ppermute | solution.py:277
  54.3 5.2 %collective-permute-start.6 = (bf16[32,128]{1,0:T(8,128)(2,1)S(1)}, bf16[32,128]{1,0:T(8,128)(2,1)S(1)}, u32[]{:S(2)}, u32[]{:S(2)}) collective-permute-start(bf16[32,128]{1,0:T(8,128)(2,1)S(1)} %pad_maximum_fusion.rest_0_), channel_id=1, source_target_pairs={{0,2},{1,3},{2,0},{3,1},{4,6},{5,7},{6,4},{7,5},{8,10},{9,11},{10,... | collective-permute-start | bytes 24584 | tf_op jit(solution)/shard_map/ppermute | solution.py:277
  59.5 5.2 %collective-permute-start.7 = (bf16[32,128]{1,0:T(8,128)(2,1)S(1)}, bf16[32,128]{1,0:T(8,128)(2,1)S(1)}, u32[]{:S(2)}, u32[]{:S(2)}) collective-permute-start(bf16[32,128]{1,0:T(8,128)(2,1)S(1)} %pad_maximum_fusion.rest_0_), channel_id=1, source_target_pairs={{0,3},{1,0},{2,1},{3,2},{4,7},{5,4},{6,5},{7,6},{8,11},{9,8},{10,9... | collective-permute-start | bytes 24584 | tf_op jit(solution)/shard_map/ppermute | solution.py:277
  64.7 1.2 collective-permute-done.7.rest_3_
  66.3 0.5 shard_map.116
  66.8 5.1 %collective-permute-start.15 = (bf16[512,256]{1,0:T(8,128)(2,1)S(1)}, bf16[512,256]{1,0:T(8,128)(2,1)S(1)}, u32[]{:S(2)}, u32[]{:S(2)}) collective-permute-start(bf16[512,256]{1,0:T(8,128)(2,1)S(1)} %get-tuple-element.38), channel_id=1, source_target_pairs={{0,28},{1,29},{2,30},{3,31},{4,0},{5,1},{6,2},{7,3},{8,4},{9,5},{1... | collective-permute-start | bytes 786440 | tf_op jit(solution)/shard_map/ppermute | solution.py:281
  71.9 1.9 %collective-permute-start.8 = (bf16[512,256]{1,0:T(8,128)(2,1)S(1)}, bf16[512,256]{1,0:T(8,128)(2,1)S(1)}, u32[]{:S(2)}, u32[]{:S(2)}) collective-permute-start(bf16[512,256]{1,0:T(8,128)(2,1)S(1)} %get-tuple-element.31), channel_id=1, source_target_pairs={{0,4},{1,5},{2,6},{3,7},{4,8},{5,9},{6,10},{7,11},{8,12},{9,13},{1... | collective-permute-start | bytes 786440 | tf_op jit(solution)/shard_map/ppermute | solution.py:281
  73.8 5.9 %collective-permute-start.10 = (bf16[128,512]{1,0:T(8,128)(2,1)S(1)}, bf16[128,512]{1,0:T(8,128)(2,1)S(1)}, u32[]{:S(2)}, u32[]{:S(2)}) collective-permute-start(bf16[128,512]{1,0:T(8,128)(2,1)S(1)} %copy-done.14), channel_id=1, source_target_pairs={{0,2},{1,3},{2,0},{3,1},{4,6},{5,7},{6,4},{7,5},{8,10},{9,11},{10,... | collective-permute-start | bytes 393224 | tf_op jit(solution)/shard_map/ppermute | solution.py:277
  79.7 5.1 %collective-permute-start.11 = (bf16[128,512]{1,0:T(8,128)(2,1)S(1)}, bf16[128,512]{1,0:T(8,128)(2,1)S(1)}, u32[]{:S(2)}, u32[]{:S(2)}) collective-permute-start(bf16[128,512]{1,0:T(8,128)(2,1)S(1)} %copy-done.13), channel_id=1, source_target_pairs={{0,3},{1,0},{2,1},{3,2},{4,7},{5,4},{6,5},{7,6},{8,11},{9,8},{10,9... | collective-permute-start | bytes 393224 | tf_op jit(solution)/shard_map/ppermute | solution.py:277
  84.9 1.9 %collective-permute-start.9 = (bf16[128,512]{1,0:T(8,128)(2,1)S(1)}, bf16[128,512]{1,0:T(8,128)(2,1)S(1)}, u32[]{:S(2)}, u32[]{:S(2)}) collective-permute-start(bf16[128,512]{1,0:T(8,128)(2,1)S(1)} %copy-done.12), channel_id=1, source_target_pairs={{0,1},{1,2},{2,3},{3,0},{4,5},{5,6},{6,7},{7,4},{8,9},{9,10},{10,1... | collective-permute-start | bytes 393224 | tf_op jit(solution)/shard_map/ppermute | solution.py:277
  86.8 7.0 %collective-permute-done.11.rest_3_ = bf16[128,512]{1,0:T(8,128)(2,1)S(1)} collective-permute-done((bf16[128,512]{1,0:T(8,128)(2,1)S(1)}, bf16[128,512]{1,0:T(8,128)(2,1)S(1)}, u32[]{:S(2)}, u32[]{:S(2)}) %collective-permute-start.11) | collective-permute-done | bytes 131104 | tf_op jit(solution)/shard_map/ppermute | solution.py:277
  93.8 0.7 collective-permute-done.9.rest_1_
  94.5 1.2 shard_map.120
  95.7 4.0 %collective-permute-start.16 = (bf16[1024,256]{1,0:T(8,128)(2,1)}, bf16[1024,256]{1,0:T(8,128)(2,1)S(1)}, u32[]{:S(2)}, u32[]{:S(2)}) collective-permute-start(bf16[1024,256]{1,0:T(8,128)(2,1)} %shard_map.120), channel_id=1, source_target_pairs={{0,28},{1,29},{2,30},{3,31},{4,0},{5,1},{6,2},{7,3},{8,4},{9,5},{1... | collective-permute-start | bytes 1572872 | tf_op jit(solution)/shard_map/ppermute | solution.py:281
  99.7 1.2 shard_map.117
  101.0 1.9 %collective-permute-start.12 = (bf16[1024,256]{1,0:T(8,128)(2,1)}, bf16[1024,256]{1,0:T(8,128)(2,1)S(1)}, u32[]{:S(2)}, u32[]{:S(2)}) collective-permute-start(bf16[1024,256]{1,0:T(8,128)(2,1)} %shard_map.117), channel_id=1, source_target_pairs={{0,4},{1,5},{2,6},{3,7},{4,8},{5,9},{6,10},{7,11},{8,12},{9,13},{1... | collective-permute-start | bytes 1572872 | tf_op jit(solution)/shard_map/ppermute | solution.py:281
  102.9 5.7 %all-to-all-start.2 = ((bf16[4,128,512]{2,1,0:T(8,128)(2,1)}), bf16[4,128,512]{2,1,0:T(8,128)(2,1)S(1)}, u32[]{:S(2)}, u32[]{:S(2)}) async-start(bf16[4,128,512]{2,1,0:T(8,128)(2,1)} %get-tuple-element.37), calls=%async_computation.2 | async-start | bytes 1048576 | tf_op jit(solution)/shard_map/all_to_all | solution.py:285
  108.6 0.7 collective-permute-done.16.received
  109.3 1.3 shard_map.121
  110.5 4.6 %collective-permute-start.17 = (bf16[1024,256]{1,0:T(8,128)(2,1)}, bf16[1024,256]{1,0:T(8,128)(2,1)S(1)}, u32[]{:S(2)}, u32[]{:S(2)}) collective-permute-start(bf16[1024,256]{1,0:T(8,128)(2,1)} %shard_map.121), channel_id=1, source_target_pairs={{0,28},{1,29},{2,30},{3,31},{4,0},{5,1},{6,2},{7,3},{8,4},{9,5},{1... | collective-permute-start | bytes 1572872 | tf_op jit(solution)/shard_map/ppermute | solution.py:281
  115.1 1.3 shard_map.118
  116.4 1.9 %collective-permute-start.13 = (bf16[1024,256]{1,0:T(8,128)(2,1)}, bf16[1024,256]{1,0:T(8,128)(2,1)S(1)}, u32[]{:S(2)}, u32[]{:S(2)}) collective-permute-start(bf16[1024,256]{1,0:T(8,128)(2,1)} %shard_map.118), channel_id=1, source_target_pairs={{0,4},{1,5},{2,6},{3,7},{4,8},{5,9},{6,10},{7,11},{8,12},{9,13},{1... | collective-permute-start | bytes 1572872 | tf_op jit(solution)/shard_map/ppermute | solution.py:281
  118.3 0.9 all-to-all-done.2.exchanged
  119.3 3.5 %collective-permute-done.17.received = bf16[1024,256]{1,0:T(8,128)(2,1)S(1)} collective-permute-done((bf16[1024,256]{1,0:T(8,128)(2,1)}, bf16[1024,256]{1,0:T(8,128)(2,1)S(1)}, u32[]{:S(2)}, u32[]{:S(2)}) %collective-permute-start.17) | collective-permute-done | bytes 524320 | tf_op jit(solution)/shard_map/ppermute | solution.py:281
  122.8 0.4 shard_map.122
  123.2 5.4 %collective-permute-start.18 = (bf16[1024,256]{1,0:T(8,128)(2,1)S(1)}, bf16[1024,256]{1,0:T(8,128)(2,1)}, u32[]{:S(2)}, u32[]{:S(2)}) collective-permute-start(bf16[1024,256]{1,0:T(8,128)(2,1)S(1)} %shard_map.122), channel_id=1, source_target_pairs={{0,28},{1,29},{2,30},{3,31},{4,0},{5,1},{6,2},{7,3},{8,4},{9,5},{1... | collective-permute-start | bytes 1572872 | tf_op jit(solution)/shard_map/ppermute | solution.py:281
  128.9 0.8 copy-done.1
  129.7 1.0 copy-done.2
  130.8 0.4 shard_map.119
  131.2 1.9 %collective-permute-start.14 = (bf16[1024,256]{1,0:T(8,128)(2,1)S(1)}, bf16[1024,256]{1,0:T(8,128)(2,1)}, u32[]{:S(2)}, u32[]{:S(2)}) collective-permute-start(bf16[1024,256]{1,0:T(8,128)(2,1)S(1)} %shard_map.119), channel_id=1, source_target_pairs={{0,4},{1,5},{2,6},{3,7},{4,8},{5,9},{6,10},{7,11},{8,12},{9,13},{1... | collective-permute-start | bytes 1572872 | tf_op jit(solution)/shard_map/ppermute | solution.py:281
  133.2 2.3 %collective-permute-start = (bf16[128,256]{1,0:T(8,128)(2,1)}, bf16[128,256]{1,0:T(8,128)(2,1)S(1)}, u32[]{:S(2)}, u32[]{:S(2)}) collective-permute-start(bf16[128,256]{1,0:T(8,128)(2,1)} %get-tuple-element.26), channel_id=1, source_target_pairs={{0,1},{1,2},{2,3},{3,0},{4,5},{5,6},{6,7},{7,4},{8,9},{9,10},{10,1... | collective-permute-start | bytes 196616 | tf_op jit(solution)/shard_map/ppermute | solution.py:277
  135.5 11.0 %collective-permute-start.1 = (bf16[128,256]{1,0:T(8,128)(2,1)}, bf16[128,256]{1,0:T(8,128)(2,1)S(1)}, u32[]{:S(2)}, u32[]{:S(2)}) collective-permute-start(bf16[128,256]{1,0:T(8,128)(2,1)} %get-tuple-element.27), channel_id=1, source_target_pairs={{0,2},{1,3},{2,0},{3,1},{4,6},{5,7},{6,4},{7,5},{8,10},{9,11},{10,... | collective-permute-start | bytes 196616 | tf_op jit(solution)/shard_map/ppermute | solution.py:277
  146.5 1.9 %collective-permute-start.2 = (bf16[128,256]{1,0:T(8,128)(2,1)}, bf16[128,256]{1,0:T(8,128)(2,1)S(1)}, u32[]{:S(2)}, u32[]{:S(2)}) collective-permute-start(bf16[128,256]{1,0:T(8,128)(2,1)} %get-tuple-element.28), channel_id=1, source_target_pairs={{0,3},{1,0},{2,1},{3,2},{4,7},{5,4},{6,5},{7,6},{8,11},{9,8},{10,9... | collective-permute-start | bytes 196616 | tf_op jit(solution)/shard_map/ppermute | solution.py:277
  148.7 4.5 %collective-permute-done.2.rest_3_ = bf16[128,256]{1,0:T(8,128)(2,1)S(1)} collective-permute-done((bf16[128,256]{1,0:T(8,128)(2,1)}, bf16[128,256]{1,0:T(8,128)(2,1)S(1)}, u32[]{:S(2)}, u32[]{:S(2)}) %collective-permute-start.2) | collective-permute-done | bytes 65568 | tf_op jit(solution)/shard_map/ppermute | solution.py:277
  153.2 0.8 copy-done.7
  154.0 0.8 copy-done.8
  154.8 0.4 shard_map.115
  155.3 5.0 %shard_map.123 = (bf16[1024,256]{1,0:T(8,128)(2,1)S(1)}, f32[64,256]{1,0:T(8,128)S(1)}, bf16[16,64,256]{2,1,0:T(8,128)(2,1)}) custom-call(f32[1024,256]{1,0:T(8,128)S(1)} %get-tuple-element.30.product, bf16[1024,256]{1,0:T(8,128)(2,1)} %collective-permute-done.14.up, bf16[1024,256]{1,0:T(8,128)(2,1)} %collective-permute-done.18.down, ...), custom_call_target="tpu_custom_call" | custom-call | flops 1610612736 | bytes 2097152 | tf_op jit(solution)/shard_map/pallas_call | solution.py:365
  160.3 9.5 %all-to-all-start.3 = ((bf16[16,64,256]{2,1,0:T(8,128)(2,1)}), bf16[16,64,256]{2,1,0:T(8,128)(2,1)S(1)}, u32[]{:S(2)}, u32[]{:S(2)}) async-start(bf16[16,64,256]{2,1,0:T(8,128)(2,1)} %get-tuple-element.47), calls=%async_computation.3 | async-start | bytes 1048576 | tf_op jit(solution)/shard_map/all_to_all | solution.py:379
  169.8 1.8 shard_map.124
  171.5 7.9 %all-to-all-done.3.parts = bf16[16,64,256]{2,1,0:T(8,128)(2,1)S(1)} async-done(((bf16[16,64,256]{2,1,0:T(8,128)(2,1)}), bf16[16,64,256]{2,1,0:T(8,128)(2,1)S(1)}, u32[]{:S(2)}, u32[]{:S(2)}) %all-to-all-start.3) | async-done | bytes 524320 | tf_op jit(solution)/shard_map/all_to_all | solution.py:379
  179.4 1.7 shard_map.125
  (51 shorter events, 1.4 us)
Async XLA Ops:
  4.6 10.9 %copy-start.11 = (s32[1,1,128]{2,1,0:T(1,128)S(1)}, s32[1,1,128]{2,1,0:T(1,128)}, u32[]{:S(2)}) copy-start(s32[1,1,128]{2,1,0:T(1,128)} %param.12) | copy-start | bytes 1540
  4.6 33.2 %all-to-all-start = ((bf16[4,128,1280]{2,1,0:T(8,128)(2,1)}), bf16[4,128,1280]{2,1,0:T(8,128)(2,1)S(1)}, u32[]{:S(2)}, u32[]{:S(2)}) async-start(bf16[4,128,1280]{2,1,0:T(8,128)(2,1)} %get-tuple-element.29), calls=%async_computation | async-start | bytes 2621440 | tf_op jit(solution)/shard_map/all_to_all | solution.py:285
  15.7 34.3 %collective-permute-start.3 = (bf16[16,128]{1,0:T(8,128)(2,1)S(1)}, bf16[16,128]{1,0:T(8,128)(2,1)S(1)}, u32[]{:S(2)}, u32[]{:S(2)}) collective-permute-start(bf16[16,128]{1,0:T(8,128)(2,1)S(1)} %broadcast_in_dim.19), channel_id=1, source_target_pairs={{0,4},{1,5},{2,6},{3,7},{4,8},{5,9},{6,10},{7,11},{8,12},{9,13},{1... | collective-permute-start | bytes 12296 | tf_op jit(solution)/shard_map/ppermute | solution.py:281
  18.9 31.1 %collective-permute-start.4 = (bf16[16,128]{1,0:T(8,128)(2,1)S(1)}, bf16[16,128]{1,0:T(8,128)(2,1)S(1)}, u32[]{:S(2)}, u32[]{:S(2)}) collective-permute-start(bf16[16,128]{1,0:T(8,128)(2,1)S(1)} %broadcast_in_dim.19), channel_id=1, source_target_pairs={{0,28},{1,29},{2,30},{3,31},{4,0},{5,1},{6,2},{7,3},{8,4},{9,5},{1... | collective-permute-start | bytes 12296 | tf_op jit(solution)/shard_map/ppermute | solution.py:281
  37.8 65.1 %all-to-all-start.1 = ((bf16[4,128,512]{2,1,0:T(8,128)(2,1)}), bf16[4,128,512]{2,1,0:T(8,128)(2,1)S(1)}, u32[]{:S(2)}, u32[]{:S(2)}) async-start(bf16[4,128,512]{2,1,0:T(8,128)(2,1)} %get-tuple-element.36), calls=%async_computation.1 | async-start | bytes 1048576 | tf_op jit(solution)/shard_map/all_to_all | solution.py:285
  50.0 14.7 %collective-permute-start.5 = (bf16[32,128]{1,0:T(8,128)(2,1)S(1)}, bf16[32,128]{1,0:T(8,128)(2,1)S(1)}, u32[]{:S(2)}, u32[]{:S(2)}) collective-permute-start(bf16[32,128]{1,0:T(8,128)(2,1)S(1)} %pad_maximum_fusion.rest_0_), channel_id=1, source_target_pairs={{0,1},{1,2},{2,3},{3,0},{4,5},{5,6},{6,7},{7,4},{8,9},{9,10},{10,1... | collective-permute-start | bytes 24584 | tf_op jit(solution)/shard_map/ppermute | solution.py:277
  54.3 10.4 %collective-permute-start.6 = (bf16[32,128]{1,0:T(8,128)(2,1)S(1)}, bf16[32,128]{1,0:T(8,128)(2,1)S(1)}, u32[]{:S(2)}, u32[]{:S(2)}) collective-permute-start(bf16[32,128]{1,0:T(8,128)(2,1)S(1)} %pad_maximum_fusion.rest_0_), channel_id=1, source_target_pairs={{0,2},{1,3},{2,0},{3,1},{4,6},{5,7},{6,4},{7,5},{8,10},{9,11},{10,... | collective-permute-start | bytes 24584 | tf_op jit(solution)/shard_map/ppermute | solution.py:277
  59.5 6.4 %collective-permute-start.7 = (bf16[32,128]{1,0:T(8,128)(2,1)S(1)}, bf16[32,128]{1,0:T(8,128)(2,1)S(1)}, u32[]{:S(2)}, u32[]{:S(2)}) collective-permute-start(bf16[32,128]{1,0:T(8,128)(2,1)S(1)} %pad_maximum_fusion.rest_0_), channel_id=1, source_target_pairs={{0,3},{1,0},{2,1},{3,2},{4,7},{5,4},{6,5},{7,6},{8,11},{9,8},{10,9... | collective-permute-start | bytes 24584 | tf_op jit(solution)/shard_map/ppermute | solution.py:277
  66.3 7.5 %copy-start.14 = (bf16[128,512]{1,0:T(8,128)(2,1)S(1)}, bf16[128,512]{1,0:T(8,128)(2,1)}, u32[]{:S(2)}) copy-start(bf16[128,512]{1,0:T(8,128)(2,1)} %get-tuple-element.34) | copy-start | bytes 393220
  66.3 13.5 %copy-start.13 = (bf16[128,512]{1,0:T(8,128)(2,1)S(1)}, bf16[128,512]{1,0:T(8,128)(2,1)}, u32[]{:S(2)}) copy-start(bf16[128,512]{1,0:T(8,128)(2,1)} %get-tuple-element.35) | copy-start | bytes 393220
  66.3 18.6 %copy-start.12 = (bf16[128,512]{1,0:T(8,128)(2,1)S(1)}, bf16[128,512]{1,0:T(8,128)(2,1)}, u32[]{:S(2)}) copy-start(bf16[128,512]{1,0:T(8,128)(2,1)} %get-tuple-element.33) | copy-start | bytes 393220
  66.3 28.2 %copy-start.3 = (bf16[128,512]{1,0:T(8,128)(2,1)S(1)}, bf16[128,512]{1,0:T(8,128)(2,1)}, u32[]{:S(2)}) copy-start(bf16[128,512]{1,0:T(8,128)(2,1)} %get-tuple-element.32.rest_0_) | copy-start | bytes 393220
  66.8 27.7 %collective-permute-start.15 = (bf16[512,256]{1,0:T(8,128)(2,1)S(1)}, bf16[512,256]{1,0:T(8,128)(2,1)S(1)}, u32[]{:S(2)}, u32[]{:S(2)}) collective-permute-start(bf16[512,256]{1,0:T(8,128)(2,1)S(1)} %get-tuple-element.38), channel_id=1, source_target_pairs={{0,28},{1,29},{2,30},{3,31},{4,0},{5,1},{6,2},{7,3},{8,4},{9,5},{1... | collective-permute-start | bytes 786440 | tf_op jit(solution)/shard_map/ppermute | solution.py:281
  71.9 27.8 %collective-permute-start.8 = (bf16[512,256]{1,0:T(8,128)(2,1)S(1)}, bf16[512,256]{1,0:T(8,128)(2,1)S(1)}, u32[]{:S(2)}, u32[]{:S(2)}) collective-permute-start(bf16[512,256]{1,0:T(8,128)(2,1)S(1)} %get-tuple-element.31), channel_id=1, source_target_pairs={{0,4},{1,5},{2,6},{3,7},{4,8},{5,9},{6,10},{7,11},{8,12},{9,13},{1... | collective-permute-start | bytes 786440 | tf_op jit(solution)/shard_map/ppermute | solution.py:281
  73.8 13.0 %collective-permute-start.10 = (bf16[128,512]{1,0:T(8,128)(2,1)S(1)}, bf16[128,512]{1,0:T(8,128)(2,1)S(1)}, u32[]{:S(2)}, u32[]{:S(2)}) collective-permute-start(bf16[128,512]{1,0:T(8,128)(2,1)S(1)} %copy-done.14), channel_id=1, source_target_pairs={{0,2},{1,3},{2,0},{3,1},{4,6},{5,7},{6,4},{7,5},{8,10},{9,11},{10,... | collective-permute-start | bytes 393224 | tf_op jit(solution)/shard_map/ppermute | solution.py:277
  79.7 14.0 %collective-permute-start.11 = (bf16[128,512]{1,0:T(8,128)(2,1)S(1)}, bf16[128,512]{1,0:T(8,128)(2,1)S(1)}, u32[]{:S(2)}, u32[]{:S(2)}) collective-permute-start(bf16[128,512]{1,0:T(8,128)(2,1)S(1)} %copy-done.13), channel_id=1, source_target_pairs={{0,3},{1,0},{2,1},{3,2},{4,7},{5,4},{6,5},{7,6},{8,11},{9,8},{10,9... | collective-permute-start | bytes 393224 | tf_op jit(solution)/shard_map/ppermute | solution.py:277
  84.9 9.6 %collective-permute-start.9 = (bf16[128,512]{1,0:T(8,128)(2,1)S(1)}, bf16[128,512]{1,0:T(8,128)(2,1)S(1)}, u32[]{:S(2)}, u32[]{:S(2)}) collective-permute-start(bf16[128,512]{1,0:T(8,128)(2,1)S(1)} %copy-done.12), channel_id=1, source_target_pairs={{0,1},{1,2},{2,3},{3,0},{4,5},{5,6},{6,7},{7,4},{8,9},{9,10},{10,1... | collective-permute-start | bytes 393224 | tf_op jit(solution)/shard_map/ppermute | solution.py:277
  95.7 13.5 %collective-permute-start.16 = (bf16[1024,256]{1,0:T(8,128)(2,1)}, bf16[1024,256]{1,0:T(8,128)(2,1)S(1)}, u32[]{:S(2)}, u32[]{:S(2)}) collective-permute-start(bf16[1024,256]{1,0:T(8,128)(2,1)} %shard_map.120), channel_id=1, source_target_pairs={{0,28},{1,29},{2,30},{3,31},{4,0},{5,1},{6,2},{7,3},{8,4},{9,5},{1... | collective-permute-start | bytes 1572872 | tf_op jit(solution)/shard_map/ppermute | solution.py:281
  101.0 14.2 %collective-permute-start.12 = (bf16[1024,256]{1,0:T(8,128)(2,1)}, bf16[1024,256]{1,0:T(8,128)(2,1)S(1)}, u32[]{:S(2)}, u32[]{:S(2)}) collective-permute-start(bf16[1024,256]{1,0:T(8,128)(2,1)} %shard_map.117), channel_id=1, source_target_pairs={{0,4},{1,5},{2,6},{3,7},{4,8},{5,9},{6,10},{7,11},{8,12},{9,13},{1... | collective-permute-start | bytes 1572872 | tf_op jit(solution)/shard_map/ppermute | solution.py:281
  102.9 16.4 %all-to-all-start.2 = ((bf16[4,128,512]{2,1,0:T(8,128)(2,1)}), bf16[4,128,512]{2,1,0:T(8,128)(2,1)S(1)}, u32[]{:S(2)}, u32[]{:S(2)}) async-start(bf16[4,128,512]{2,1,0:T(8,128)(2,1)} %get-tuple-element.37), calls=%async_computation.2 | async-start | bytes 1048576 | tf_op jit(solution)/shard_map/all_to_all | solution.py:285
  110.5 12.2 %collective-permute-start.17 = (bf16[1024,256]{1,0:T(8,128)(2,1)}, bf16[1024,256]{1,0:T(8,128)(2,1)S(1)}, u32[]{:S(2)}, u32[]{:S(2)}) collective-permute-start(bf16[1024,256]{1,0:T(8,128)(2,1)} %shard_map.121), channel_id=1, source_target_pairs={{0,28},{1,29},{2,30},{3,31},{4,0},{5,1},{6,2},{7,3},{8,4},{9,5},{1... | collective-permute-start | bytes 1572872 | tf_op jit(solution)/shard_map/ppermute | solution.py:281
  116.4 12.6 %collective-permute-start.13 = (bf16[1024,256]{1,0:T(8,128)(2,1)}, bf16[1024,256]{1,0:T(8,128)(2,1)S(1)}, u32[]{:S(2)}, u32[]{:S(2)}) collective-permute-start(bf16[1024,256]{1,0:T(8,128)(2,1)} %shard_map.118), channel_id=1, source_target_pairs={{0,4},{1,5},{2,6},{3,7},{4,8},{5,9},{6,10},{7,11},{8,12},{9,13},{1... | collective-permute-start | bytes 1572872 | tf_op jit(solution)/shard_map/ppermute | solution.py:281
  122.8 25.6 %copy-start.10 = (s32[1,16,4]{1,2,0:T(4,128)S(1)}, s32[1,16,4]{1,2,0:T(4,128)}, u32[]{:S(2)}) copy-start(s32[1,16,4]{1,2,0:T(4,128)} %param.13) | copy-start | bytes 772
  122.8 30.4 %copy-start.4 = (bf16[256,256]{1,0:T(8,128)(2,1)S(1)}, bf16[256,256]{1,0:T(8,128)(2,1)}, u32[]{:S(2)}) copy-start(bf16[256,256]{1,0:T(8,128)(2,1)} %constant.18.clone.rest_7_.high) | copy-start | bytes 393220
  122.8 30.4 %copy-start.5 = (bf16[256,256]{1,0:T(8,128)(2,1)S(1)}, bf16[256,256]{1,0:T(8,128)(2,1)}, u32[]{:S(2)}) copy-start(bf16[256,256]{1,0:T(8,128)(2,1)} %constant.19.clone.rest_8_.low) | copy-start | bytes 393220
  122.8 30.4 %copy-start.6 = (bf16[256,256]{1,0:T(8,128)(2,1)S(1)}, bf16[256,256]{1,0:T(8,128)(2,1)}, u32[]{:S(2)}) copy-start(bf16[256,256]{1,0:T(8,128)(2,1)} %constant.22.clone.rest_10_) | copy-start | bytes 393220
  123.2 30.0 %copy-start = (bf16[1,1024,256]{2,1,0:T(8,128)(2,1)S(1)}, bf16[1,1024,256]{2,1,0:T(8,128)(2,1)}, u32[]{:S(2)}) copy-start(bf16[1,1024,256]{2,1,0:T(8,128)(2,1)} %param.14) | copy-start | bytes 1572868
  123.2 32.0 %collective-permute-start.18 = (bf16[1024,256]{1,0:T(8,128)(2,1)S(1)}, bf16[1024,256]{1,0:T(8,128)(2,1)}, u32[]{:S(2)}, u32[]{:S(2)}) collective-permute-start(bf16[1024,256]{1,0:T(8,128)(2,1)S(1)} %shard_map.122), channel_id=1, source_target_pairs={{0,28},{1,29},{2,30},{3,31},{4,0},{5,1},{6,2},{7,3},{8,4},{9,5},{1... | collective-permute-start | bytes 1572872 | tf_op jit(solution)/shard_map/ppermute | solution.py:281
  128.9 0.8 copy-start.1
  129.7 1.0 copy-start.2
  131.2 24.0 %collective-permute-start.14 = (bf16[1024,256]{1,0:T(8,128)(2,1)S(1)}, bf16[1024,256]{1,0:T(8,128)(2,1)}, u32[]{:S(2)}, u32[]{:S(2)}) collective-permute-start(bf16[1024,256]{1,0:T(8,128)(2,1)S(1)} %shard_map.119), channel_id=1, source_target_pairs={{0,4},{1,5},{2,6},{3,7},{4,8},{5,9},{6,10},{7,11},{8,12},{9,13},{1... | collective-permute-start | bytes 1572872 | tf_op jit(solution)/shard_map/ppermute | solution.py:281
  133.2 15.5 %collective-permute-start = (bf16[128,256]{1,0:T(8,128)(2,1)}, bf16[128,256]{1,0:T(8,128)(2,1)S(1)}, u32[]{:S(2)}, u32[]{:S(2)}) collective-permute-start(bf16[128,256]{1,0:T(8,128)(2,1)} %get-tuple-element.26), channel_id=1, source_target_pairs={{0,1},{1,2},{2,3},{3,0},{4,5},{5,6},{6,7},{7,4},{8,9},{9,10},{10,1... | collective-permute-start | bytes 196616 | tf_op jit(solution)/shard_map/ppermute | solution.py:277
  135.5 13.2 %collective-permute-start.1 = (bf16[128,256]{1,0:T(8,128)(2,1)}, bf16[128,256]{1,0:T(8,128)(2,1)S(1)}, u32[]{:S(2)}, u32[]{:S(2)}) collective-permute-start(bf16[128,256]{1,0:T(8,128)(2,1)} %get-tuple-element.27), channel_id=1, source_target_pairs={{0,2},{1,3},{2,0},{3,1},{4,6},{5,7},{6,4},{7,5},{8,10},{9,11},{10,... | collective-permute-start | bytes 196616 | tf_op jit(solution)/shard_map/ppermute | solution.py:277
  146.5 6.7 %collective-permute-start.2 = (bf16[128,256]{1,0:T(8,128)(2,1)}, bf16[128,256]{1,0:T(8,128)(2,1)S(1)}, u32[]{:S(2)}, u32[]{:S(2)}) collective-permute-start(bf16[128,256]{1,0:T(8,128)(2,1)} %get-tuple-element.28), channel_id=1, source_target_pairs={{0,3},{1,0},{2,1},{3,2},{4,7},{5,4},{6,5},{7,6},{8,11},{9,8},{10,9... | collective-permute-start | bytes 196616 | tf_op jit(solution)/shard_map/ppermute | solution.py:277
  153.2 0.8 copy-start.7
  154.0 0.8 copy-start.8
  155.2 14.5 %copy-start.9 = (bf16[64,192]{1,0:T(8,128)(2,1)S(1)}, bf16[64,192]{1,0:T(8,128)(2,1)}, u32[]{:S(2)}) copy-start(bf16[64,192]{1,0:T(8,128)(2,1)} %constant.21.clone.back_table) | copy-start | bytes 73732
  160.3 19.2 %all-to-all-start.3 = ((bf16[16,64,256]{2,1,0:T(8,128)(2,1)}), bf16[16,64,256]{2,1,0:T(8,128)(2,1)S(1)}, u32[]{:S(2)}, u32[]{:S(2)}) async-start(bf16[16,64,256]{2,1,0:T(8,128)(2,1)} %get-tuple-element.47), calls=%async_computation.3 | async-start | bytes 1048576 | tf_op jit(solution)/shard_map/all_to_all | solution.py:379

commit v7 on v3

--- a/solution.py
+++ b/solution.py
@@ -150,26 +150,39 @@
         out[other] = total[other].astype(jnp.bfloat16)
 
 
-def base_kernel(weights, exchanged, momentum, offsets, *rest):
-    tables, (product, kept, offsets_out, *tables_out) = rest[: len(rest) // 2 - 1], rest[len(rest) // 2 - 1 :]
-    product[...] = dot(weights[...], gathered(exchanged, 2 * product.shape[1], product.shape[1]), ((1,), (0,)))
-    kept[...] = momentum[...]
-    offsets_out[...] = offsets[...]
-    for table, out in zip(tables, tables_out):
-        out[...] = table[...]
-
-
-def forward_kernel(product, up, down, momentum, offsets, high, low, ahead, ones, summed, decoded, sent, packed, held, sem):
+def own_kernel(weights, exchanged, product):
+    width = product.shape[1]
+    product[...] = dot(weights[...], gathered(exchanged, 2 * width, width), ((1,), (0,)))
+
+
+def keep_kernel(*refs):
+    half = len(refs) // 2
+    for given, out in zip(refs[:half], refs[half:]):
+        out[...] = given[...]
+
+
+def forward_kernel(
+    product, up, down, momentum, offsets, high, low, ahead, ones, summed, decoded, sent, packed, held, parts, sem
+):
     table = (high[...], low[...])
     per = TILE // BLOCK
     rows = TILE // STRIDE
+    fetches = []
+    for i in range(product.shape[0] // TILE):
+        there = pl.ds(i * TILE, TILE)
+        pair = [pltpu.make_async_copy(x.at[there], parts.at[j, there], sem.at[1 + j, i]) for j, x in enumerate((up, down))]
+        fetches.append(pair)
+        for copy in pair:
+            copy.start()
     copies = []
     for i in range(product.shape[0] // TILE):
         here = slice(i * TILE, (i + 1) * TILE)
-        total = product[here] + up[here].astype(jnp.float32) + down[here].astype(jnp.float32)
+        for copy in fetches[i]:
+            copy.wait()
+        total = product[here] + parts[0, here].astype(jnp.float32) + parts[1, here].astype(jnp.float32)
         gradient = total.astype(jnp.bfloat16)
         held[here] = gradient
-        copies.append(pltpu.make_async_copy(held.at[pl.ds(i * TILE, TILE)], summed.at[pl.ds(i * TILE, TILE)], sem.at[i]))
+        copies.append(pltpu.make_async_copy(held.at[pl.ds(i * TILE, TILE)], summed.at[pl.ds(i * TILE, TILE)], sem.at[0, i]))
         copies[-1].start()
         value = BETA * momentum[here].astype(jnp.float32) + gradient.astype(jnp.float32)
         spectrum = right(left(ahead[...], value), table, 1)
@@ -327,7 +340,9 @@
     up, down = ring(up, down)
     up, down = ring(*both(up, down, third))
     up, down = ring(*both(up, down, second))
-    up, down = ring(*both(up, down, first))
+    up = near(0, True, up, first)
+    down = near(width, False, down, first)
+    up, down = ring(up, down)
 
     high, low, ahead, back = dct_parts()
     ones = jnp.asarray(np.kron(np.eye(TILE // BLOCK), np.ones((BLOCK, BLOCK))), jnp.bfloat16)
@@ -335,20 +350,21 @@
     kept = panel // STRIDE
     flops = 6 * 2 * 2 * panel * TILE * TILE
     tables = (high, low, ahead, ones)
-    product, momentum_near, wide_near, *tables_near = call(
-        base_kernel,
-        [shaped(panel, width, dtype=jnp.float32), shaped(panel, width), shaped(*wide.shape, dtype=jnp.int32)]
-        + [shaped(*table.shape) for table in tables],
-        work,
-    )(weights, first, momentum[0], wide, *tables)
+    product = call(own_kernel, shaped(panel, width, dtype=jnp.float32), work)(weights, first)
+    near_by = (momentum[0], wide, *tables)
+    momentum_near, wide_near, *tables_near = call(
+        keep_kernel, [shaped(*x.shape, dtype=x.dtype) for x in near_by], work // 8
+    )(*near_by)
     summed, decoded, sent = pl.pallas_call(
         forward_kernel,
         out_shape=(shaped(panel, width), shaped(kept, width, dtype=jnp.float32), shaped(groups, kept, width)),
+        in_specs=[whole, apart, apart] + [whole] * 6,
         out_specs=(apart, whole, whole),
         scratch_shapes=(
             pltpu.VMEM((kept, width), jnp.float32),
             pltpu.VMEM((panel, width), jnp.bfloat16),
-            pltpu.SemaphoreType.DMA((panel // TILE,)),
+            pltpu.VMEM((2, panel, width), jnp.bfloat16),
+            pltpu.SemaphoreType.DMA((3, panel // TILE)),
         ),
         compiler_params=pltpu.CompilerParams(vmem_limit_bytes=GRANT),
         cost_estimate=pl.CostEstimate(flops=flops, bytes_accessed=2 << 20, transcendentals=0),

time: 179 us -> 180 us (level)
  the two profiles are of different devices: /device:TPU:24 before, /device:TPU:1 now
where the time goes in v7:
time: 180 us; the launch traced here: 179 us
  starting transfers between devices  95.9 us (53%)
  waiting for transfers between devices  54.2 us (30%)
  Pallas kernels  21.9 us (12%)
  local copies, waits for them, and re-layouts  5.95 us (3%)
    ppermute x10, starting transfers between devices, across(): return lax.ppermute(x, 'shard', pairs)  34.8 us
    all_to_all x4, starting transfers between devices, exchange(): return lax.all_to_all(x, 'shard', 0, 0, axis_index_groups=lines, tiled=True)  26.7 us
    ppermute x10, waiting for transfers between devices, across(): return lax.ppermute(x, 'shard', pairs)  23.7 us
    all_to_all x4, waiting for transfers between devices, exchange(): return lax.all_to_all(x, 'shard', 0, 0, axis_index_groups=lines, tiled=True)  21.9 us
    all_to_all x1, starting transfers between devices, step(): parts = lax.all_to_all(sent, 'rep', 0, 0, tiled=True)  19.7 us
    ppermute x3, starting transfers between devices, along_line(): return lax.ppermute(x, 'shard', pairs)  14.7 us
    all_to_all x1, waiting for transfers between devices, step(): parts = lax.all_to_all(sent, 'rep', 0, 0, tiled=True)  7.89 us
    pallas_call x6, Pallas kernels, near(): call(kernel, shaped(panel, width), work)(weights, received, exchanged)  5.64 us
  transfers between devices with their start and end apart: 18, of which 9 were waited for; matrix products, arithmetic and copies ran while one was open for 1% of the time, Pallas kernels for 7%

profile of v7, /device:TPU:1, one launch (start us, length us, event | category | flops | bytes accessed | tf_op | source)
XLA Modules:
  0.0 179.1 jit_solution(11300030481134067031)
XLA Ops:
  0.6 3.0 %shard_map.115 = (bf16[4,128,512]{2,1,0:T(8,128)(2,1)}, bf16[4,128,512]{2,1,0:T(8,128)(2,1)}, bf16[4,128,768]{2,1,0:T(8,128)(2,1)}) custom-call(bf16[128,8192]{1,0:T(8,128)(2,1)} %bitcast.9), custom_call_target="tpu_custom_call" | custom-call | flops 268435456 | bytes 2097152 | tf_op jit(solution)/shard_map/pallas_call | solution.py:312
  3.6 10.8 %all-to-all-start.2 = ((bf16[4,128,512]{2,1,0:T(8,128)(2,1)}), bf16[4,128,512]{2,1,0:T(8,128)(2,1)S(1)}, u32[]{:S(2)}, u32[]{:S(2)}) async-start(bf16[4,128,512]{2,1,0:T(8,128)(2,1)} %get-tuple-element.18), calls=%async_computation.2 | async-start | bytes 1048576 | tf_op jit(solution)/shard_map/all_to_all | solution.py:278
  14.5 2.6 %shard_map.113 = bf16[4,128,1280]{2,1,0:T(8,128)(2,1)} custom-call(bf16[128,8192]{1,0:T(8,128)(2,1)} %bitcast.10, bf16[128,1024]{1,0:T(8,128)(2,1)} %bitcast.11), custom_call_target="tpu_custom_call" | custom-call | flops 268435456 | bytes 2097152 | tf_op jit(solution)/shard_map/pallas_call | solution.py:288
  17.1 9.3 %all-to-all-done.2.exchanged = bf16[4,128,512]{2,1,0:T(8,128)(2,1)S(1)} async-done(((bf16[4,128,512]{2,1,0:T(8,128)(2,1)}), bf16[4,128,512]{2,1,0:T(8,128)(2,1)S(1)}, u32[]{:S(2)}, u32[]{:S(2)}) %all-to-all-start.2) | async-done | bytes 524320 | tf_op jit(solution)/shard_map/all_to_all | solution.py:278
  26.4 4.9 %all-to-all-start = ((bf16[4,128,1280]{2,1,0:T(8,128)(2,1)}), bf16[4,128,1280]{2,1,0:T(8,128)(2,1)S(1)}, u32[]{:S(2)}, u32[]{:S(2)}) async-start(bf16[4,128,1280]{2,1,0:T(8,128)(2,1)} %shard_map.113), calls=%async_computation | async-start | bytes 2621440 | tf_op jit(solution)/shard_map/all_to_all | solution.py:278
  31.5 3.2 %collective-permute-start = (bf16[16,128]{1,0:T(8,128)(2,1)S(1)}, bf16[16,128]{1,0:T(8,128)(2,1)S(1)}, u32[]{:S(2)}, u32[]{:S(2)}) collective-permute-start(bf16[16,128]{1,0:T(8,128)(2,1)S(1)} %broadcast_in_dim.19), channel_id=1, source_target_pairs={{0,4},{1,5},{2,6},{3,7},{4,8},{5,9},{6,10},{7,11},{8,12},{9,13},{1... | collective-permute-start | bytes 12296 | tf_op jit(solution)/shard_map/ppermute | solution.py:274
  34.7 3.8 %collective-permute-start.1 = (bf16[16,128]{1,0:T(8,128)(2,1)S(1)}, bf16[16,128]{1,0:T(8,128)(2,1)S(1)}, u32[]{:S(2)}, u32[]{:S(2)}) collective-permute-start(bf16[16,128]{1,0:T(8,128)(2,1)S(1)} %broadcast_in_dim.19), channel_id=1, source_target_pairs={{0,28},{1,29},{2,30},{3,31},{4,0},{5,1},{6,2},{7,3},{8,4},{9,5},{1... | collective-permute-start | bytes 12296 | tf_op jit(solution)/shard_map/ppermute | solution.py:274
  38.5 12.6 %all-to-all-done.exchanged = bf16[4,128,1280]{2,1,0:T(8,128)(2,1)S(1)} async-done(((bf16[4,128,1280]{2,1,0:T(8,128)(2,1)}), bf16[4,128,1280]{2,1,0:T(8,128)(2,1)S(1)}, u32[]{:S(2)}, u32[]{:S(2)}) %all-to-all-start) | async-done | bytes 1310752 | tf_op jit(solution)/shard_map/all_to_all | solution.py:278
  51.2 5.8 %all-to-all-start.3 = ((bf16[4,128,512]{2,1,0:T(8,128)(2,1)}), bf16[4,128,512]{2,1,0:T(8,128)(2,1)S(1)}, u32[]{:S(2)}, u32[]{:S(2)}) async-start(bf16[4,128,512]{2,1,0:T(8,128)(2,1)} %get-tuple-element.19), calls=%async_computation.3 | async-start | bytes 1048576 | tf_op jit(solution)/shard_map/all_to_all | solution.py:278
  57.1 4.3 %collective-permute-start.2 = (bf16[32,128]{1,0:T(8,128)(2,1)S(1)}, bf16[32,128]{1,0:T(8,128)(2,1)S(1)}, u32[]{:S(2)}, u32[]{:S(2)}) collective-permute-start(bf16[32,128]{1,0:T(8,128)(2,1)S(1)} %pad_maximum_fusion.rest_0_), channel_id=1, source_target_pairs={{0,1},{1,2},{2,3},{3,0},{4,5},{5,6},{6,7},{7,4},{8,9},{9,10},{10,1... | collective-permute-start | bytes 24584 | tf_op jit(solution)/shard_map/ppermute | solution.py:270
  61.4 5.2 %collective-permute-start.3 = (bf16[32,128]{1,0:T(8,128)(2,1)S(1)}, bf16[32,128]{1,0:T(8,128)(2,1)S(1)}, u32[]{:S(2)}, u32[]{:S(2)}) collective-permute-start(bf16[32,128]{1,0:T(8,128)(2,1)S(1)} %pad_maximum_fusion.rest_0_), channel_id=1, source_target_pairs={{0,2},{1,3},{2,0},{3,1},{4,6},{5,7},{6,4},{7,5},{8,10},{9,11},{10,... | collective-permute-start | bytes 24584 | tf_op jit(solution)/shard_map/ppermute | solution.py:270
  66.6 5.2 %collective-permute-start.4 = (bf16[32,128]{1,0:T(8,128)(2,1)S(1)}, bf16[32,128]{1,0:T(8,128)(2,1)S(1)}, u32[]{:S(2)}, u32[]{:S(2)}) collective-permute-start(bf16[32,128]{1,0:T(8,128)(2,1)S(1)} %pad_maximum_fusion.rest_0_), channel_id=1, source_target_pairs={{0,3},{1,0},{2,1},{3,2},{4,7},{5,4},{6,5},{7,6},{8,11},{9,8},{10,9... | collective-permute-start | bytes 24584 | tf_op jit(solution)/shard_map/ppermute | solution.py:270
  71.8 0.8 collective-permute-done.4.rest_3_
  72.6 0.4 shard_map.114.weights
  73.0 1.2 shard_map.117
  74.2 5.1 %collective-permute-start.9 = (bf16[512,256]{1,0:T(8,128)(2,1)}, bf16[512,256]{1,0:T(8,128)(2,1)S(1)}, u32[]{:S(2)}, u32[]{:S(2)}) collective-permute-start(bf16[512,256]{1,0:T(8,128)(2,1)} %get-tuple-element.20), channel_id=1, source_target_pairs={{0,28},{1,29},{2,30},{3,31},{4,0},{5,1},{6,2},{7,3},{8,4},{9,5},{1... | collective-permute-start | bytes 786440 | tf_op jit(solution)/shard_map/ppermute | solution.py:274
  79.3 1.9 %collective-permute-start.5 = (bf16[512,256]{1,0:T(8,128)(2,1)}, bf16[512,256]{1,0:T(8,128)(2,1)}, u32[]{:S(2)}, u32[]{:S(2)}) collective-permute-start(bf16[512,256]{1,0:T(8,128)(2,1)} %get-tuple-element.17), channel_id=1, source_target_pairs={{0,4},{1,5},{2,6},{3,7},{4,8},{5,9},{6,10},{7,11},{8,12},{9,13},{1... | collective-permute-start | bytes 786440 | tf_op jit(solution)/shard_map/ppermute | solution.py:274
  81.2 5.1 %all-to-all-start.1 = ((bf16[4,128,768]{2,1,0:T(8,128)(2,1)}), bf16[4,128,768]{2,1,0:T(8,128)(2,1)S(1)}, u32[]{:S(2)}, u32[]{:S(2)}) async-start(bf16[4,128,768]{2,1,0:T(8,128)(2,1)} %get-tuple-element.16), calls=%async_computation.1 | async-start | bytes 1572864 | tf_op jit(solution)/shard_map/all_to_all | solution.py:278
  86.3 0.7 copy-done.1
  87.0 0.9 copy-done.2
  88.0 0.4 shard_map.121
  88.4 4.6 %collective-permute-start.10 = (bf16[1024,256]{1,0:T(8,128)(2,1)S(1)}, bf16[1024,256]{1,0:T(8,128)(2,1)S(1)}, u32[]{:S(2)}, u32[]{:S(2)}) collective-permute-start(bf16[1024,256]{1,0:T(8,128)(2,1)S(1)} %shard_map.121), channel_id=1, source_target_pairs={{0,28},{1,29},{2,30},{3,31},{4,0},{5,1},{6,2},{7,3},{8,4},{9,5},{1... | collective-permute-start | bytes 1572872 | tf_op jit(solution)/shard_map/ppermute | solution.py:274
  93.0 1.4 shard_map.118
  94.4 1.9 %collective-permute-start.6 = (bf16[1024,256]{1,0:T(8,128)(2,1)S(1)}, bf16[1024,256]{1,0:T(8,128)(2,1)S(1)}, u32[]{:S(2)}, u32[]{:S(2)}) collective-permute-start(bf16[1024,256]{1,0:T(8,128)(2,1)S(1)} %shard_map.118), channel_id=1, source_target_pairs={{0,4},{1,5},{2,6},{3,7},{4,8},{5,9},{6,10},{7,11},{8,12},{9,13},{1... | collective-permute-start | bytes 1572872 | tf_op jit(solution)/shard_map/ppermute | solution.py:274
  96.3 5.6 %collective-permute-done.10.received = bf16[1024,256]{1,0:T(8,128)(2,1)S(1)} collective-permute-done((bf16[1024,256]{1,0:T(8,128)(2,1)S(1)}, bf16[1024,256]{1,0:T(8,128)(2,1)S(1)}, u32[]{:S(2)}, u32[]{:S(2)}) %collective-permute-start.10) | collective-permute-done | bytes 524320 | tf_op jit(solution)/shard_map/ppermute | solution.py:274
  101.9 0.4 shard_map.122
  102.4 5.0 %collective-permute-start.11 = (bf16[1024,256]{1,0:T(8,128)(2,1)S(1)}, bf16[1024,256]{1,0:T(8,128)(2,1)}, u32[]{:S(2)}, u32[]{:S(2)}) collective-permute-start(bf16[1024,256]{1,0:T(8,128)(2,1)S(1)} %shard_map.122), channel_id=1, source_target_pairs={{0,28},{1,29},{2,30},{3,31},{4,0},{5,1},{6,2},{7,3},{8,4},{9,5},{1... | collective-permute-start | bytes 1572872 | tf_op jit(solution)/shard_map/ppermute | solution.py:274
  107.4 1.0 collective-permute-done.6.received
  108.4 0.4 shard_map.119
  108.8 1.9 %collective-permute-start.7 = (bf16[1024,256]{1,0:T(8,128)(2,1)S(1)}, bf16[1024,256]{1,0:T(8,128)(2,1)}, u32[]{:S(2)}, u32[]{:S(2)}) collective-permute-start(bf16[1024,256]{1,0:T(8,128)(2,1)S(1)} %shard_map.119), channel_id=1, source_target_pairs={{0,4},{1,5},{2,6},{3,7},{4,8},{5,9},{6,10},{7,11},{8,12},{9,13},{1... | collective-permute-start | bytes 1572872 | tf_op jit(solution)/shard_map/ppermute | solution.py:274
  110.7 7.3 %collective-permute-done.11.received = bf16[1024,256]{1,0:T(8,128)(2,1)} collective-permute-done((bf16[1024,256]{1,0:T(8,128)(2,1)S(1)}, bf16[1024,256]{1,0:T(8,128)(2,1)}, u32[]{:S(2)}, u32[]{:S(2)}) %collective-permute-start.11) | collective-permute-done | bytes 524320 | tf_op jit(solution)/shard_map/ppermute | solution.py:274
  118.0 1.5 shard_map.123
  119.5 5.5 %collective-permute-start.12 = (bf16[1024,256]{1,0:T(8,128)(2,1)S(1)}, bf16[1024,256]{1,0:T(8,128)(2,1)}, u32[]{:S(2)}, u32[]{:S(2)}) collective-permute-start(bf16[1024,256]{1,0:T(8,128)(2,1)S(1)} %shard_map.123), channel_id=1, source_target_pairs={{0,28},{1,29},{2,30},{3,31},{4,0},{5,1},{6,2},{7,3},{8,4},{9,5},{1... | collective-permute-start | bytes 1572872 | tf_op jit(solution)/shard_map/ppermute | solution.py:274
  125.0 1.5 shard_map.120
  126.5 1.9 %collective-permute-start.8 = (bf16[1024,256]{1,0:T(8,128)(2,1)S(1)}, bf16[1024,256]{1,0:T(8,128)(2,1)}, u32[]{:S(2)}, u32[]{:S(2)}) collective-permute-start(bf16[1024,256]{1,0:T(8,128)(2,1)S(1)} %shard_map.120), channel_id=1, source_target_pairs={{0,4},{1,5},{2,6},{3,7},{4,8},{5,9},{6,10},{7,11},{8,12},{9,13},{1... | collective-permute-start | bytes 1572872 | tf_op jit(solution)/shard_map/ppermute | solution.py:274
  128.5 0.7 broadcast_in_dim.21
  129.2 0.8 reshape.9.refs_1_.offsets
  130.1 0.9 copy-done.4
  131.0 0.9 copy-done.6
  131.9 0.8 copy-done.7
  132.7 0.4 shard_map.116.product
  133.2 2.8 %collective-permute-done.12.down = bf16[1024,256]{1,0:T(8,128)(2,1)} collective-permute-done((bf16[1024,256]{1,0:T(8,128)(2,1)S(1)}, bf16[1024,256]{1,0:T(8,128)(2,1)}, u32[]{:S(2)}, u32[]{:S(2)}) %collective-permute-start.12) | collective-permute-done | bytes 524320 | tf_op jit(solution)/shard_map/ppermute | solution.py:274
  136.0 7.0 %collective-permute-done.8.up = bf16[1024,256]{1,0:T(8,128)(2,1)} collective-permute-done((bf16[1024,256]{1,0:T(8,128)(2,1)S(1)}, bf16[1024,256]{1,0:T(8,128)(2,1)}, u32[]{:S(2)}, u32[]{:S(2)}) %collective-permute-start.8) | collective-permute-done | bytes 524320 | tf_op jit(solution)/shard_map/ppermute | solution.py:274
  143.0 5.0 %shard_map.125 = (bf16[1024,256]{1,0:T(8,128)(2,1)S(1)}, f32[64,256]{1,0:T(8,128)S(1)}, bf16[16,64,256]{2,1,0:T(8,128)(2,1)}) custom-call(f32[1024,256]{1,0:T(8,128)S(1)} %shard_map.116.product, bf16[1024,256]{1,0:T(8,128)(2,1)} %collective-permute-done.8.up, bf16[1024,256]{1,0:T(8,128)(2,1)} %collective-permute-done.12.down, ...), custom_call_target="tpu_custom_call" | custom-call | flops 1610612736 | bytes 2097152 | tf_op jit(solution)/shard_map/pallas_call | solution.py:358
  148.0 19.7 %all-to-all-start.4 = ((bf16[16,64,256]{2,1,0:T(8,128)(2,1)}), bf16[16,64,256]{2,1,0:T(8,128)(2,1)S(1)}, u32[]{:S(2)}, u32[]{:S(2)}) async-start(bf16[16,64,256]{2,1,0:T(8,128)(2,1)} %get-tuple-element.29), calls=%async_computation.4 | async-start | bytes 1048576 | tf_op jit(solution)/shard_map/all_to_all | solution.py:372
  167.7 1.8 shard_map.126
  169.5 7.9 %all-to-all-done.4.parts = bf16[16,64,256]{2,1,0:T(8,128)(2,1)S(1)} async-done(((bf16[16,64,256]{2,1,0:T(8,128)(2,1)}), bf16[16,64,256]{2,1,0:T(8,128)(2,1)S(1)}, u32[]{:S(2)}, u32[]{:S(2)}) %all-to-all-start.4) | async-done | bytes 524320 | tf_op jit(solution)/shard_map/all_to_all | solution.py:372
  177.4 1.7 shard_map.127
  (35 shorter events, 0.5 us)
Async XLA Ops:
  3.6 22.8 %all-to-all-start.2 = ((bf16[4,128,512]{2,1,0:T(8,128)(2,1)}), bf16[4,128,512]{2,1,0:T(8,128)(2,1)S(1)}, u32[]{:S(2)}, u32[]{:S(2)}) async-start(bf16[4,128,512]{2,1,0:T(8,128)(2,1)} %get-tuple-element.18), calls=%async_computation.2 | async-start | bytes 1048576 | tf_op jit(solution)/shard_map/all_to_all | solution.py:278
  17.1 14.2 %copy-start.10 = (s32[1,1,128]{2,1,0:T(1,128)S(1)}, s32[1,1,128]{2,1,0:T(1,128)}, u32[]{:S(2)}) copy-start(s32[1,1,128]{2,1,0:T(1,128)} %param.12) | copy-start | bytes 1540
  26.4 24.8 %all-to-all-start = ((bf16[4,128,1280]{2,1,0:T(8,128)(2,1)}), bf16[4,128,1280]{2,1,0:T(8,128)(2,1)S(1)}, u32[]{:S(2)}, u32[]{:S(2)}) async-start(bf16[4,128,1280]{2,1,0:T(8,128)(2,1)} %shard_map.113), calls=%async_computation | async-start | bytes 2621440 | tf_op jit(solution)/shard_map/all_to_all | solution.py:278
  31.5 25.5 %collective-permute-start = (bf16[16,128]{1,0:T(8,128)(2,1)S(1)}, bf16[16,128]{1,0:T(8,128)(2,1)S(1)}, u32[]{:S(2)}, u32[]{:S(2)}) collective-permute-start(bf16[16,128]{1,0:T(8,128)(2,1)S(1)} %broadcast_in_dim.19), channel_id=1, source_target_pairs={{0,4},{1,5},{2,6},{3,7},{4,8},{5,9},{6,10},{7,11},{8,12},{9,13},{1... | collective-permute-start | bytes 12296 | tf_op jit(solution)/shard_map/ppermute | solution.py:274
  34.7 22.3 %collective-permute-start.1 = (bf16[16,128]{1,0:T(8,128)(2,1)S(1)}, bf16[16,128]{1,0:T(8,128)(2,1)S(1)}, u32[]{:S(2)}, u32[]{:S(2)}) collective-permute-start(bf16[16,128]{1,0:T(8,128)(2,1)S(1)} %broadcast_in_dim.19), channel_id=1, source_target_pairs={{0,28},{1,29},{2,30},{3,31},{4,0},{5,1},{6,2},{7,3},{8,4},{9,5},{1... | collective-permute-start | bytes 12296 | tf_op jit(solution)/shard_map/ppermute | solution.py:274
  51.2 30.0 %all-to-all-start.3 = ((bf16[4,128,512]{2,1,0:T(8,128)(2,1)}), bf16[4,128,512]{2,1,0:T(8,128)(2,1)S(1)}, u32[]{:S(2)}, u32[]{:S(2)}) async-start(bf16[4,128,512]{2,1,0:T(8,128)(2,1)} %get-tuple-element.19), calls=%async_computation.3 | async-start | bytes 1048576 | tf_op jit(solution)/shard_map/all_to_all | solution.py:278
  57.1 14.7 %collective-permute-start.2 = (bf16[32,128]{1,0:T(8,128)(2,1)S(1)}, bf16[32,128]{1,0:T(8,128)(2,1)S(1)}, u32[]{:S(2)}, u32[]{:S(2)}) collective-permute-start(bf16[32,128]{1,0:T(8,128)(2,1)S(1)} %pad_maximum_fusion.rest_0_), channel_id=1, source_target_pairs={{0,1},{1,2},{2,3},{3,0},{4,5},{5,6},{6,7},{7,4},{8,9},{9,10},{10,1... | collective-permute-start | bytes 24584 | tf_op jit(solution)/shard_map/ppermute | solution.py:270
  61.4 10.4 %collective-permute-start.3 = (bf16[32,128]{1,0:T(8,128)(2,1)S(1)}, bf16[32,128]{1,0:T(8,128)(2,1)S(1)}, u32[]{:S(2)}, u32[]{:S(2)}) collective-permute-start(bf16[32,128]{1,0:T(8,128)(2,1)S(1)} %pad_maximum_fusion.rest_0_), channel_id=1, source_target_pairs={{0,2},{1,3},{2,0},{3,1},{4,6},{5,7},{6,4},{7,5},{8,10},{9,11},{10,... | collective-permute-start | bytes 24584 | tf_op jit(solution)/shard_map/ppermute | solution.py:270
  66.6 6.0 %collective-permute-start.4 = (bf16[32,128]{1,0:T(8,128)(2,1)S(1)}, bf16[32,128]{1,0:T(8,128)(2,1)S(1)}, u32[]{:S(2)}, u32[]{:S(2)}) collective-permute-start(bf16[32,128]{1,0:T(8,128)(2,1)S(1)} %pad_maximum_fusion.rest_0_), channel_id=1, source_target_pairs={{0,3},{1,0},{2,1},{3,2},{4,7},{5,4},{6,5},{7,6},{8,11},{9,8},{10,9... | collective-permute-start | bytes 24584 | tf_op jit(solution)/shard_map/ppermute | solution.py:270
  74.2 12.1 %collective-permute-start.9 = (bf16[512,256]{1,0:T(8,128)(2,1)}, bf16[512,256]{1,0:T(8,128)(2,1)S(1)}, u32[]{:S(2)}, u32[]{:S(2)}) collective-permute-start(bf16[512,256]{1,0:T(8,128)(2,1)} %get-tuple-element.20), channel_id=1, source_target_pairs={{0,28},{1,29},{2,30},{3,31},{4,0},{5,1},{6,2},{7,3},{8,4},{9,5},{1... | collective-permute-start | bytes 786440 | tf_op jit(solution)/shard_map/ppermute | solution.py:274
  79.3 13.7 %collective-permute-start.5 = (bf16[512,256]{1,0:T(8,128)(2,1)}, bf16[512,256]{1,0:T(8,128)(2,1)}, u32[]{:S(2)}, u32[]{:S(2)}) collective-permute-start(bf16[512,256]{1,0:T(8,128)(2,1)} %get-tuple-element.17), channel_id=1, source_target_pairs={{0,4},{1,5},{2,6},{3,7},{4,8},{5,9},{6,10},{7,11},{8,12},{9,13},{1... | collective-permute-start | bytes 786440 | tf_op jit(solution)/shard_map/ppermute | solution.py:274
  81.2 29.5 %all-to-all-start.1 = ((bf16[4,128,768]{2,1,0:T(8,128)(2,1)}), bf16[4,128,768]{2,1,0:T(8,128)(2,1)S(1)}, u32[]{:S(2)}, u32[]{:S(2)}) async-start(bf16[4,128,768]{2,1,0:T(8,128)(2,1)} %get-tuple-element.16), calls=%async_computation.1 | async-start | bytes 1572864 | tf_op jit(solution)/shard_map/all_to_all | solution.py:278
  86.3 0.7 copy-start.1
  87.0 0.9 copy-start.2
  88.4 13.5 %collective-permute-start.10 = (bf16[1024,256]{1,0:T(8,128)(2,1)S(1)}, bf16[1024,256]{1,0:T(8,128)(2,1)S(1)}, u32[]{:S(2)}, u32[]{:S(2)}) collective-permute-start(bf16[1024,256]{1,0:T(8,128)(2,1)S(1)} %shard_map.121), channel_id=1, source_target_pairs={{0,28},{1,29},{2,30},{3,31},{4,0},{5,1},{6,2},{7,3},{8,4},{9,5},{1... | collective-permute-start | bytes 1572872 | tf_op jit(solution)/shard_map/ppermute | solution.py:274
  94.4 14.0 %collective-permute-start.6 = (bf16[1024,256]{1,0:T(8,128)(2,1)S(1)}, bf16[1024,256]{1,0:T(8,128)(2,1)S(1)}, u32[]{:S(2)}, u32[]{:S(2)}) collective-permute-start(bf16[1024,256]{1,0:T(8,128)(2,1)S(1)} %shard_map.118), channel_id=1, source_target_pairs={{0,4},{1,5},{2,6},{3,7},{4,8},{5,9},{6,10},{7,11},{8,12},{9,13},{1... | collective-permute-start | bytes 1572872 | tf_op jit(solution)/shard_map/ppermute | solution.py:274
  102.4 15.7 %collective-permute-start.11 = (bf16[1024,256]{1,0:T(8,128)(2,1)S(1)}, bf16[1024,256]{1,0:T(8,128)(2,1)}, u32[]{:S(2)}, u32[]{:S(2)}) collective-permute-start(bf16[1024,256]{1,0:T(8,128)(2,1)S(1)} %shard_map.122), channel_id=1, source_target_pairs={{0,28},{1,29},{2,30},{3,31},{4,0},{5,1},{6,2},{7,3},{8,4},{9,5},{1... | collective-permute-start | bytes 1572872 | tf_op jit(solution)/shard_map/ppermute | solution.py:274
  108.8 16.2 %collective-permute-start.7 = (bf16[1024,256]{1,0:T(8,128)(2,1)S(1)}, bf16[1024,256]{1,0:T(8,128)(2,1)}, u32[]{:S(2)}, u32[]{:S(2)}) collective-permute-start(bf16[1024,256]{1,0:T(8,128)(2,1)S(1)} %shard_map.119), channel_id=1, source_target_pairs={{0,4},{1,5},{2,6},{3,7},{4,8},{5,9},{6,10},{7,11},{8,12},{9,13},{1... | collective-permute-start | bytes 1572872 | tf_op jit(solution)/shard_map/ppermute | solution.py:274
  119.5 8.9 %copy-start.9 = (s32[1,16,4]{1,2,0:T(4,128)S(1)}, s32[1,16,4]{1,2,0:T(4,128)}, u32[]{:S(2)}) copy-start(s32[1,16,4]{1,2,0:T(4,128)} %param.13) | copy-start | bytes 772
  119.5 10.5 %copy-start = (bf16[1,1024,256]{2,1,0:T(8,128)(2,1)S(1)}, bf16[1,1024,256]{2,1,0:T(8,128)(2,1)}, u32[]{:S(2)}) copy-start(bf16[1,1024,256]{2,1,0:T(8,128)(2,1)} %param.14) | copy-start | bytes 1572868
  119.5 10.5 %copy-start.3 = (bf16[256,256]{1,0:T(8,128)(2,1)S(1)}, bf16[256,256]{1,0:T(8,128)(2,1)}, u32[]{:S(2)}) copy-start(bf16[256,256]{1,0:T(8,128)(2,1)} %constant.18.clone.refs_2_.high) | copy-start | bytes 393220
  119.5 16.4 %collective-permute-start.12 = (bf16[1024,256]{1,0:T(8,128)(2,1)S(1)}, bf16[1024,256]{1,0:T(8,128)(2,1)}, u32[]{:S(2)}, u32[]{:S(2)}) collective-permute-start(bf16[1024,256]{1,0:T(8,128)(2,1)S(1)} %shard_map.123), channel_id=1, source_target_pairs={{0,28},{1,29},{2,30},{3,31},{4,0},{5,1},{6,2},{7,3},{8,4},{9,5},{1... | collective-permute-start | bytes 1572872 | tf_op jit(solution)/shard_map/ppermute | solution.py:274
  126.5 16.5 %collective-permute-start.8 = (bf16[1024,256]{1,0:T(8,128)(2,1)S(1)}, bf16[1024,256]{1,0:T(8,128)(2,1)}, u32[]{:S(2)}, u32[]{:S(2)}) collective-permute-start(bf16[1024,256]{1,0:T(8,128)(2,1)S(1)} %shard_map.120), channel_id=1, source_target_pairs={{0,4},{1,5},{2,6},{3,7},{4,8},{5,9},{6,10},{7,11},{8,12},{9,13},{1... | collective-permute-start | bytes 1572872 | tf_op jit(solution)/shard_map/ppermute | solution.py:274
  130.1 0.9 copy-start.4
  131.0 0.9 copy-start.6
  131.9 0.8 copy-start.7
  143.0 24.7 %copy-start.5 = (bf16[256,256]{1,0:T(8,128)(2,1)S(1)}, bf16[256,256]{1,0:T(8,128)(2,1)}, u32[]{:S(2)}) copy-start(bf16[256,256]{1,0:T(8,128)(2,1)} %constant.19.clone.refs_3_.low) | copy-start | bytes 393220
  143.0 24.7 %copy-start.8 = (bf16[64,192]{1,0:T(8,128)(2,1)S(1)}, bf16[64,192]{1,0:T(8,128)(2,1)}, u32[]{:S(2)}) copy-start(bf16[64,192]{1,0:T(8,128)(2,1)} %constant.21.clone.back_table) | copy-start | bytes 73732
  148.0 29.4 %all-to-all-start.4 = ((bf16[16,64,256]{2,1,0:T(8,128)(2,1)}), bf16[16,64,256]{2,1,0:T(8,128)(2,1)S(1)}, u32[]{:S(2)}, u32[]{:S(2)}) async-start(bf16[16,64,256]{2,1,0:T(8,128)(2,1)} %get-tuple-element.29), calls=%async_computation.4 | async-start | bytes 1048576 | tf_op jit(solution)/shard_map/all_to_all | solution.py:372

commit v8 on v3

--- a/solution.py
+++ b/solution.py
@@ -159,17 +159,28 @@
         out[...] = table[...]
 
 
-def forward_kernel(product, up, down, momentum, offsets, high, low, ahead, ones, summed, decoded, sent, packed, held, sem):
+def forward_kernel(
+    product, up, down, momentum, offsets, high, low, ahead, ones, summed, decoded, sent, packed, held, parts, sem
+):
     table = (high[...], low[...])
     per = TILE // BLOCK
     rows = TILE // STRIDE
+    fetches = []
+    for i in range(product.shape[0] // TILE):
+        there = pl.ds(i * TILE, TILE)
+        pair = [pltpu.make_async_copy(x.at[there], parts.at[j, there], sem.at[1 + j, i]) for j, x in enumerate((up, down))]
+        fetches.append(pair)
+        for copy in pair:
+            copy.start()
     copies = []
     for i in range(product.shape[0] // TILE):
         here = slice(i * TILE, (i + 1) * TILE)
-        total = product[here] + up[here].astype(jnp.float32) + down[here].astype(jnp.float32)
+        for copy in fetches[i]:
+            copy.wait()
+        total = product[here] + parts[0, here].astype(jnp.float32) + parts[1, here].astype(jnp.float32)
         gradient = total.astype(jnp.bfloat16)
         held[here] = gradient
-        copies.append(pltpu.make_async_copy(held.at[pl.ds(i * TILE, TILE)], summed.at[pl.ds(i * TILE, TILE)], sem.at[i]))
+        copies.append(pltpu.make_async_copy(held.at[pl.ds(i * TILE, TILE)], summed.at[pl.ds(i * TILE, TILE)], sem.at[0, i]))
         copies[-1].start()
         value = BETA * momentum[here].astype(jnp.float32) + gradient.astype(jnp.float32)
         spectrum = right(left(ahead[...], value), table, 1)
@@ -344,11 +355,13 @@
     summed, decoded, sent = pl.pallas_call(
         forward_kernel,
         out_shape=(shaped(panel, width), shaped(kept, width, dtype=jnp.float32), shaped(groups, kept, width)),
+        in_specs=[whole, apart, apart] + [whole] * 6,
         out_specs=(apart, whole, whole),
         scratch_shapes=(
             pltpu.VMEM((kept, width), jnp.float32),
             pltpu.VMEM((panel, width), jnp.bfloat16),
-            pltpu.SemaphoreType.DMA((panel // TILE,)),
+            pltpu.VMEM((2, panel, width), jnp.bfloat16),
+            pltpu.SemaphoreType.DMA((3, panel // TILE)),
         ),
         compiler_params=pltpu.CompilerParams(vmem_limit_bytes=GRANT),
         cost_estimate=pl.CostEstimate(flops=flops, bytes_accessed=2 << 20, transcendentals=0),

time: 179 us -> 179 us (level)
  no operation moved by 1% of the time
where the time goes in v8:
time: 179 us; the launch traced here: 178 us
  starting transfers between devices  87.2 us (49%)
  waiting for transfers between devices  61.5 us (34%)
  Pallas kernels  21.8 us (12%)
  local copies, waits for them, and re-layouts  5.95 us (3%)
    ppermute x10, starting transfers between devices, across(): return lax.ppermute(x, 'shard', pairs)  36.3 us
    all_to_all x4, starting transfers between devices, exchange(): return lax.all_to_all(x, 'shard', 0, 0, axis_index_groups=lines, tiled=True)  31.9 us
    all_to_all x4, waiting for transfers between devices, exchange(): return lax.all_to_all(x, 'shard', 0, 0, axis_index_groups=lines, tiled=True)  27.1 us
    ppermute x10, waiting for transfers between devices, across(): return lax.ppermute(x, 'shard', pairs)  21.9 us
    ppermute x3, starting transfers between devices, along_line(): return lax.ppermute(x, 'shard', pairs)  14.6 us
    all_to_all x1, waiting for transfers between devices, step(): parts = lax.all_to_all(sent, 'rep', 0, 0, tiled=True)  9.06 us
    pallas_call x6, Pallas kernels, near(): call(kernel, shaped(panel, width), work)(weights, received, exchanged)  5.64 us
    pallas_call x1, Pallas kernels, step(): pl.pallas_call(forward_kernel, out_shape=(shaped(panel, width), shaped(ke...  5.02 us
  transfers between devices with their start and end apart: 18, of which 10 were waited for; matrix products, arithmetic and copies ran while one was open for 1% of the time, Pallas kernels for 7%

profile of v8, /device:TPU:24, one launch (start us, length us, event | category | flops | bytes accessed | tf_op | source)
XLA Modules:
  0.0 177.7 jit_solution(15434952932492500531)
XLA Ops:
  0.6 3.0 %shard_map.115 = (bf16[4,128,512]{2,1,0:T(8,128)(2,1)}, bf16[4,128,512]{2,1,0:T(8,128)(2,1)}, bf16[4,128,768]{2,1,0:T(8,128)(2,1)}) custom-call(bf16[128,8192]{1,0:T(8,128)(2,1)} %bitcast.9), custom_call_target="tpu_custom_call" | custom-call | flops 268435456 | bytes 2097152 | tf_op jit(solution)/shard_map/pallas_call | solution.py:310
  3.6 10.3 %all-to-all-start.2 = ((bf16[4,128,512]{2,1,0:T(8,128)(2,1)}), bf16[4,128,512]{2,1,0:T(8,128)(2,1)S(1)}, u32[]{:S(2)}, u32[]{:S(2)}) async-start(bf16[4,128,512]{2,1,0:T(8,128)(2,1)} %get-tuple-element.20), calls=%async_computation.2 | async-start | bytes 1048576 | tf_op jit(solution)/shard_map/all_to_all | solution.py:276
  13.9 2.6 %shard_map.113 = bf16[4,128,1280]{2,1,0:T(8,128)(2,1)} custom-call(bf16[128,8192]{1,0:T(8,128)(2,1)} %bitcast.10, bf16[128,1024]{1,0:T(8,128)(2,1)} %bitcast.11), custom_call_target="tpu_custom_call" | custom-call | flops 268435456 | bytes 2097152 | tf_op jit(solution)/shard_map/pallas_call | solution.py:286
  16.6 11.9 %all-to-all-done.2.exchanged = bf16[4,128,512]{2,1,0:T(8,128)(2,1)S(1)} async-done(((bf16[4,128,512]{2,1,0:T(8,128)(2,1)}), bf16[4,128,512]{2,1,0:T(8,128)(2,1)S(1)}, u32[]{:S(2)}, u32[]{:S(2)}) %all-to-all-start.2) | async-done | bytes 524320 | tf_op jit(solution)/shard_map/all_to_all | solution.py:276
  28.4 4.8 %all-to-all-start = ((bf16[4,128,1280]{2,1,0:T(8,128)(2,1)}), bf16[4,128,1280]{2,1,0:T(8,128)(2,1)S(1)}, u32[]{:S(2)}, u32[]{:S(2)}) async-start(bf16[4,128,1280]{2,1,0:T(8,128)(2,1)} %shard_map.113), calls=%async_computation | async-start | bytes 2621440 | tf_op jit(solution)/shard_map/all_to_all | solution.py:276
  33.5 2.4 %collective-permute-start.1 = (bf16[16,128]{1,0:T(8,128)(2,1)S(1)}, bf16[16,128]{1,0:T(8,128)(2,1)S(1)}, u32[]{:S(2)}, u32[]{:S(2)}) collective-permute-start(bf16[16,128]{1,0:T(8,128)(2,1)S(1)} %broadcast_in_dim.19), channel_id=1, source_target_pairs={{0,28},{1,29},{2,30},{3,31},{4,0},{5,1},{6,2},{7,3},{8,4},{9,5},{1... | collective-permute-start | bytes 12296 | tf_op jit(solution)/shard_map/ppermute | solution.py:272
  35.8 4.7 %collective-permute-start = (bf16[16,128]{1,0:T(8,128)(2,1)S(1)}, bf16[16,128]{1,0:T(8,128)(2,1)S(1)}, u32[]{:S(2)}, u32[]{:S(2)}) collective-permute-start(bf16[16,128]{1,0:T(8,128)(2,1)S(1)} %broadcast_in_dim.19), channel_id=1, source_target_pairs={{0,4},{1,5},{2,6},{3,7},{4,8},{5,9},{6,10},{7,11},{8,12},{9,13},{1... | collective-permute-start | bytes 12296 | tf_op jit(solution)/shard_map/ppermute | solution.py:272
  40.5 15.3 %all-to-all-done.exchanged = bf16[4,128,1280]{2,1,0:T(8,128)(2,1)S(1)} async-done(((bf16[4,128,1280]{2,1,0:T(8,128)(2,1)}), bf16[4,128,1280]{2,1,0:T(8,128)(2,1)S(1)}, u32[]{:S(2)}, u32[]{:S(2)}) %all-to-all-start) | async-done | bytes 1310752 | tf_op jit(solution)/shard_map/all_to_all | solution.py:276
  55.8 11.9 %all-to-all-start.3 = ((bf16[4,128,512]{2,1,0:T(8,128)(2,1)}), bf16[4,128,512]{2,1,0:T(8,128)(2,1)S(1)}, u32[]{:S(2)}, u32[]{:S(2)}) async-start(bf16[4,128,512]{2,1,0:T(8,128)(2,1)} %get-tuple-element.21), calls=%async_computation.3 | async-start | bytes 1048576 | tf_op jit(solution)/shard_map/all_to_all | solution.py:276
  67.8 6.0 %collective-permute-start.4 = (bf16[32,128]{1,0:T(8,128)(2,1)S(1)}, bf16[32,128]{1,0:T(8,128)(2,1)S(1)}, u32[]{:S(2)}, u32[]{:S(2)}) collective-permute-start(bf16[32,128]{1,0:T(8,128)(2,1)S(1)} %pad_maximum_fusion.rest_0_), channel_id=1, source_target_pairs={{0,3},{1,0},{2,1},{3,2},{4,7},{5,4},{6,5},{7,6},{8,11},{9,8},{10,9... | collective-permute-start | bytes 24584 | tf_op jit(solution)/shard_map/ppermute | solution.py:268
  73.8 4.3 %collective-permute-start.3 = (bf16[32,128]{1,0:T(8,128)(2,1)S(1)}, bf16[32,128]{1,0:T(8,128)(2,1)S(1)}, u32[]{:S(2)}, u32[]{:S(2)}) collective-permute-start(bf16[32,128]{1,0:T(8,128)(2,1)S(1)} %pad_maximum_fusion.rest_0_), channel_id=1, source_target_pairs={{0,2},{1,3},{2,0},{3,1},{4,6},{5,7},{6,4},{7,5},{8,10},{9,11},{10,... | collective-permute-start | bytes 24584 | tf_op jit(solution)/shard_map/ppermute | solution.py:268
  78.1 4.3 %collective-permute-start.2 = (bf16[32,128]{1,0:T(8,128)(2,1)S(1)}, bf16[32,128]{1,0:T(8,128)(2,1)S(1)}, u32[]{:S(2)}, u32[]{:S(2)}) collective-permute-start(bf16[32,128]{1,0:T(8,128)(2,1)S(1)} %pad_maximum_fusion.rest_0_), channel_id=1, source_target_pairs={{0,1},{1,2},{2,3},{3,0},{4,5},{5,6},{6,7},{7,4},{8,9},{9,10},{10,1... | collective-permute-start | bytes 24584 | tf_op jit(solution)/shard_map/ppermute | solution.py:268
  82.4 0.9 collective-permute-done.3.rest_2_
  83.3 2.5 %collective-permute-done.2.rest_1_ = bf16[32,128]{1,0:T(8,128)(2,1)S(1)} collective-permute-done((bf16[32,128]{1,0:T(8,128)(2,1)S(1)}, bf16[32,128]{1,0:T(8,128)(2,1)S(1)}, u32[]{:S(2)}, u32[]{:S(2)}) %collective-permute-start.2) | collective-permute-done | bytes 8224 | tf_op jit(solution)/shard_map/ppermute | solution.py:268
  85.8 0.4 shard_map.114.weights
  86.2 1.2 shard_map.117
  87.4 4.7 %collective-permute-start.5 = (bf16[512,256]{1,0:T(8,128)(2,1)}, bf16[512,256]{1,0:T(8,128)(2,1)S(1)}, u32[]{:S(2)}, u32[]{:S(2)}) collective-permute-start(bf16[512,256]{1,0:T(8,128)(2,1)} %get-tuple-element.19), channel_id=1, source_target_pairs={{0,4},{1,5},{2,6},{3,7},{4,8},{5,9},{6,10},{7,11},{8,12},{9,13},{1... | collective-permute-start | bytes 786440 | tf_op jit(solution)/shard_map/ppermute | solution.py:272
  92.1 1.9 %collective-permute-start.9 = (bf16[512,256]{1,0:T(8,128)(2,1)}, bf16[512,256]{1,0:T(8,128)(2,1)}, u32[]{:S(2)}, u32[]{:S(2)}) collective-permute-start(bf16[512,256]{1,0:T(8,128)(2,1)} %get-tuple-element.22), channel_id=1, source_target_pairs={{0,28},{1,29},{2,30},{3,31},{4,0},{5,1},{6,2},{7,3},{8,4},{9,5},{1... | collective-permute-start | bytes 786440 | tf_op jit(solution)/shard_map/ppermute | solution.py:272
  94.0 4.9 %all-to-all-start.1 = ((bf16[4,128,768]{2,1,0:T(8,128)(2,1)}), bf16[4,128,768]{2,1,0:T(8,128)(2,1)S(1)}, u32[]{:S(2)}, u32[]{:S(2)}) async-start(bf16[4,128,768]{2,1,0:T(8,128)(2,1)} %get-tuple-element.17), calls=%async_computation.1 | async-start | bytes 1572864 | tf_op jit(solution)/shard_map/all_to_all | solution.py:276
  99.1 0.7 copy-done.1
  99.8 0.9 copy-done.2
  100.7 0.4 shard_map.118
  101.2 5.5 %collective-permute-start.6 = (bf16[1024,256]{1,0:T(8,128)(2,1)S(1)}, bf16[1024,256]{1,0:T(8,128)(2,1)S(1)}, u32[]{:S(2)}, u32[]{:S(2)}) collective-permute-start(bf16[1024,256]{1,0:T(8,128)(2,1)S(1)} %shard_map.118), channel_id=1, source_target_pairs={{0,4},{1,5},{2,6},{3,7},{4,8},{5,9},{6,10},{7,11},{8,12},{9,13},{1... | collective-permute-start | bytes 1572872 | tf_op jit(solution)/shard_map/ppermute | solution.py:272
  106.7 1.4 shard_map.121
  108.1 1.9 %collective-permute-start.10 = (bf16[1024,256]{1,0:T(8,128)(2,1)S(1)}, bf16[1024,256]{1,0:T(8,128)(2,1)S(1)}, u32[]{:S(2)}, u32[]{:S(2)}) collective-permute-start(bf16[1024,256]{1,0:T(8,128)(2,1)S(1)} %shard_map.121), channel_id=1, source_target_pairs={{0,28},{1,29},{2,30},{3,31},{4,0},{5,1},{6,2},{7,3},{8,4},{9,5},{1... | collective-permute-start | bytes 1572872 | tf_op jit(solution)/shard_map/ppermute | solution.py:272
  110.0 7.3 %collective-permute-done.6.received = bf16[1024,256]{1,0:T(8,128)(2,1)S(1)} collective-permute-done((bf16[1024,256]{1,0:T(8,128)(2,1)S(1)}, bf16[1024,256]{1,0:T(8,128)(2,1)S(1)}, u32[]{:S(2)}, u32[]{:S(2)}) %collective-permute-start.6) | collective-permute-done | bytes 524320 | tf_op jit(solution)/shard_map/ppermute | solution.py:272
  117.3 0.4 shard_map.119
  117.8 5.6 %collective-permute-start.7 = (bf16[1024,256]{1,0:T(8,128)(2,1)S(1)}, bf16[1024,256]{1,0:T(8,128)(2,1)}, u32[]{:S(2)}, u32[]{:S(2)}) collective-permute-start(bf16[1024,256]{1,0:T(8,128)(2,1)S(1)} %shard_map.119), channel_id=1, source_target_pairs={{0,4},{1,5},{2,6},{3,7},{4,8},{5,9},{6,10},{7,11},{8,12},{9,13},{1... | collective-permute-start | bytes 1572872 | tf_op jit(solution)/shard_map/ppermute | solution.py:272
  123.4 1.0 collective-permute-done.10.received
  124.4 0.4 shard_map.122
  124.8 1.9 %collective-permute-start.11 = (bf16[1024,256]{1,0:T(8,128)(2,1)S(1)}, bf16[1024,256]{1,0:T(8,128)(2,1)}, u32[]{:S(2)}, u32[]{:S(2)}) collective-permute-start(bf16[1024,256]{1,0:T(8,128)(2,1)S(1)} %shard_map.122), channel_id=1, source_target_pairs={{0,28},{1,29},{2,30},{3,31},{4,0},{5,1},{6,2},{7,3},{8,4},{9,5},{1... | collective-permute-start | bytes 1572872 | tf_op jit(solution)/shard_map/ppermute | solution.py:272
  126.7 7.6 %collective-permute-done.7.received = bf16[1024,256]{1,0:T(8,128)(2,1)} collective-permute-done((bf16[1024,256]{1,0:T(8,128)(2,1)S(1)}, bf16[1024,256]{1,0:T(8,128)(2,1)}, u32[]{:S(2)}, u32[]{:S(2)}) %collective-permute-start.7) | collective-permute-done | bytes 524320 | tf_op jit(solution)/shard_map/ppermute | solution.py:272
  134.4 1.5 shard_map.120
  135.9 5.8 %collective-permute-start.8 = (bf16[1024,256]{1,0:T(8,128)(2,1)S(1)}, bf16[1024,256]{1,0:T(8,128)(2,1)}, u32[]{:S(2)}, u32[]{:S(2)}) collective-permute-start(bf16[1024,256]{1,0:T(8,128)(2,1)S(1)} %shard_map.120), channel_id=1, source_target_pairs={{0,4},{1,5},{2,6},{3,7},{4,8},{5,9},{6,10},{7,11},{8,12},{9,13},{1... | collective-permute-start | bytes 1572872 | tf_op jit(solution)/shard_map/ppermute | solution.py:272
  141.8 1.5 shard_map.123
  143.2 1.9 %collective-permute-start.12 = (bf16[1024,256]{1,0:T(8,128)(2,1)S(1)}, bf16[1024,256]{1,0:T(8,128)(2,1)}, u32[]{:S(2)}, u32[]{:S(2)}) collective-permute-start(bf16[1024,256]{1,0:T(8,128)(2,1)S(1)} %shard_map.123), channel_id=1, source_target_pairs={{0,28},{1,29},{2,30},{3,31},{4,0},{5,1},{6,2},{7,3},{8,4},{9,5},{1... | collective-permute-start | bytes 1572872 | tf_op jit(solution)/shard_map/ppermute | solution.py:272
  145.3 0.7 broadcast_in_dim.21
  146.0 0.8 reshape.9.offsets
  146.8 0.9 copy-done.4
  147.7 0.9 copy-done.6
  148.6 0.8 copy-done.7
  149.4 0.4 shard_map.116
  149.8 5.8 %collective-permute-done.12.down = bf16[1024,256]{1,0:T(8,128)(2,1)} collective-permute-done((bf16[1024,256]{1,0:T(8,128)(2,1)S(1)}, bf16[1024,256]{1,0:T(8,128)(2,1)}, u32[]{:S(2)}, u32[]{:S(2)}) %collective-permute-start.12) | collective-permute-done | bytes 524320 | tf_op jit(solution)/shard_map/ppermute | solution.py:272
  155.6 5.0 %shard_map.124 = (bf16[1024,256]{1,0:T(8,128)(2,1)S(1)}, f32[64,256]{1,0:T(8,128)S(1)}, bf16[16,64,256]{2,1,0:T(8,128)(2,1)}) custom-call(f32[1024,256]{1,0:T(8,128)S(1)} %get-tuple-element.18.product, bf16[1024,256]{1,0:T(8,128)(2,1)} %collective-permute-done.8.up, bf16[1024,256]{1,0:T(8,128)(2,1)} %collective-permute-done.12.down, ...), custom_call_target="tpu_custom_call" | custom-call | flops 1610612736 | bytes 2097152 | tf_op jit(solution)/shard_map/pallas_call | solution.py:355
  160.7 4.4 %all-to-all-start.4 = ((bf16[16,64,256]{2,1,0:T(8,128)(2,1)}), bf16[16,64,256]{2,1,0:T(8,128)(2,1)S(1)}, u32[]{:S(2)}, u32[]{:S(2)}) async-start(bf16[16,64,256]{2,1,0:T(8,128)(2,1)} %get-tuple-element.31), calls=%async_computation.4 | async-start | bytes 1048576 | tf_op jit(solution)/shard_map/all_to_all | solution.py:369
  165.1 1.7 shard_map.125
  166.9 9.1 %all-to-all-done.4.parts = bf16[16,64,256]{2,1,0:T(8,128)(2,1)S(1)} async-done(((bf16[16,64,256]{2,1,0:T(8,128)(2,1)}), bf16[16,64,256]{2,1,0:T(8,128)(2,1)S(1)}, u32[]{:S(2)}, u32[]{:S(2)}) %all-to-all-start.4) | async-done | bytes 524320 | tf_op jit(solution)/shard_map/all_to_all | solution.py:369
  175.9 1.7 shard_map.126
  (34 shorter events, 0.6 us)
Async XLA Ops:
  3.6 24.8 %all-to-all-start.2 = ((bf16[4,128,512]{2,1,0:T(8,128)(2,1)}), bf16[4,128,512]{2,1,0:T(8,128)(2,1)S(1)}, u32[]{:S(2)}, u32[]{:S(2)}) async-start(bf16[4,128,512]{2,1,0:T(8,128)(2,1)} %get-tuple-element.20), calls=%async_computation.2 | async-start | bytes 1048576 | tf_op jit(solution)/shard_map/all_to_all | solution.py:276
  16.6 16.7 %copy-start.10 = (s32[1,1,128]{2,1,0:T(1,128)S(1)}, s32[1,1,128]{2,1,0:T(1,128)}, u32[]{:S(2)}) copy-start(s32[1,1,128]{2,1,0:T(1,128)} %param.12) | copy-start | bytes 1540
  28.4 27.4 %all-to-all-start = ((bf16[4,128,1280]{2,1,0:T(8,128)(2,1)}), bf16[4,128,1280]{2,1,0:T(8,128)(2,1)S(1)}, u32[]{:S(2)}, u32[]{:S(2)}) async-start(bf16[4,128,1280]{2,1,0:T(8,128)(2,1)} %shard_map.113), calls=%async_computation | async-start | bytes 2621440 | tf_op jit(solution)/shard_map/all_to_all | solution.py:276
  33.5 34.3 %collective-permute-start.1 = (bf16[16,128]{1,0:T(8,128)(2,1)S(1)}, bf16[16,128]{1,0:T(8,128)(2,1)S(1)}, u32[]{:S(2)}, u32[]{:S(2)}) collective-permute-start(bf16[16,128]{1,0:T(8,128)(2,1)S(1)} %broadcast_in_dim.19), channel_id=1, source_target_pairs={{0,28},{1,29},{2,30},{3,31},{4,0},{5,1},{6,2},{7,3},{8,4},{9,5},{1... | collective-permute-start | bytes 12296 | tf_op jit(solution)/shard_map/ppermute | solution.py:272
  35.8 31.9 %collective-permute-start = (bf16[16,128]{1,0:T(8,128)(2,1)S(1)}, bf16[16,128]{1,0:T(8,128)(2,1)S(1)}, u32[]{:S(2)}, u32[]{:S(2)}) collective-permute-start(bf16[16,128]{1,0:T(8,128)(2,1)S(1)} %broadcast_in_dim.19), channel_id=1, source_target_pairs={{0,4},{1,5},{2,6},{3,7},{4,8},{5,9},{6,10},{7,11},{8,12},{9,13},{1... | collective-permute-start | bytes 12296 | tf_op jit(solution)/shard_map/ppermute | solution.py:272
  55.8 38.2 %all-to-all-start.3 = ((bf16[4,128,512]{2,1,0:T(8,128)(2,1)}), bf16[4,128,512]{2,1,0:T(8,128)(2,1)S(1)}, u32[]{:S(2)}, u32[]{:S(2)}) async-start(bf16[4,128,512]{2,1,0:T(8,128)(2,1)} %get-tuple-element.21), calls=%async_computation.3 | async-start | bytes 1048576 | tf_op jit(solution)/shard_map/all_to_all | solution.py:276
  67.8 14.6 %collective-permute-start.4 = (bf16[32,128]{1,0:T(8,128)(2,1)S(1)}, bf16[32,128]{1,0:T(8,128)(2,1)S(1)}, u32[]{:S(2)}, u32[]{:S(2)}) collective-permute-start(bf16[32,128]{1,0:T(8,128)(2,1)S(1)} %pad_maximum_fusion.rest_0_), channel_id=1, source_target_pairs={{0,3},{1,0},{2,1},{3,2},{4,7},{5,4},{6,5},{7,6},{8,11},{9,8},{10,9... | collective-permute-start | bytes 24584 | tf_op jit(solution)/shard_map/ppermute | solution.py:268
  73.8 9.5 %collective-permute-start.3 = (bf16[32,128]{1,0:T(8,128)(2,1)S(1)}, bf16[32,128]{1,0:T(8,128)(2,1)S(1)}, u32[]{:S(2)}, u32[]{:S(2)}) collective-permute-start(bf16[32,128]{1,0:T(8,128)(2,1)S(1)} %pad_maximum_fusion.rest_0_), channel_id=1, source_target_pairs={{0,2},{1,3},{2,0},{3,1},{4,6},{5,7},{6,4},{7,5},{8,10},{9,11},{10,... | collective-permute-start | bytes 24584 | tf_op jit(solution)/shard_map/ppermute | solution.py:268
  78.1 7.7 %collective-permute-start.2 = (bf16[32,128]{1,0:T(8,128)(2,1)S(1)}, bf16[32,128]{1,0:T(8,128)(2,1)S(1)}, u32[]{:S(2)}, u32[]{:S(2)}) collective-permute-start(bf16[32,128]{1,0:T(8,128)(2,1)S(1)} %pad_maximum_fusion.rest_0_), channel_id=1, source_target_pairs={{0,1},{1,2},{2,3},{3,0},{4,5},{5,6},{6,7},{7,4},{8,9},{9,10},{10,1... | collective-permute-start | bytes 24584 | tf_op jit(solution)/shard_map/ppermute | solution.py:268
  87.4 11.7 %collective-permute-start.5 = (bf16[512,256]{1,0:T(8,128)(2,1)}, bf16[512,256]{1,0:T(8,128)(2,1)S(1)}, u32[]{:S(2)}, u32[]{:S(2)}) collective-permute-start(bf16[512,256]{1,0:T(8,128)(2,1)} %get-tuple-element.19), channel_id=1, source_target_pairs={{0,4},{1,5},{2,6},{3,7},{4,8},{5,9},{6,10},{7,11},{8,12},{9,13},{1... | collective-permute-start | bytes 786440 | tf_op jit(solution)/shard_map/ppermute | solution.py:272
  92.1 14.6 %collective-permute-start.9 = (bf16[512,256]{1,0:T(8,128)(2,1)}, bf16[512,256]{1,0:T(8,128)(2,1)}, u32[]{:S(2)}, u32[]{:S(2)}) collective-permute-start(bf16[512,256]{1,0:T(8,128)(2,1)} %get-tuple-element.22), channel_id=1, source_target_pairs={{0,28},{1,29},{2,30},{3,31},{4,0},{5,1},{6,2},{7,3},{8,4},{9,5},{1... | collective-permute-start | bytes 786440 | tf_op jit(solution)/shard_map/ppermute | solution.py:272
  94.0 32.7 %all-to-all-start.1 = ((bf16[4,128,768]{2,1,0:T(8,128)(2,1)}), bf16[4,128,768]{2,1,0:T(8,128)(2,1)S(1)}, u32[]{:S(2)}, u32[]{:S(2)}) async-start(bf16[4,128,768]{2,1,0:T(8,128)(2,1)} %get-tuple-element.17), calls=%async_computation.1 | async-start | bytes 1572864 | tf_op jit(solution)/shard_map/all_to_all | solution.py:276
  99.1 0.7 copy-start.1
  99.8 0.9 copy-start.2
  101.2 16.2 %collective-permute-start.6 = (bf16[1024,256]{1,0:T(8,128)(2,1)S(1)}, bf16[1024,256]{1,0:T(8,128)(2,1)S(1)}, u32[]{:S(2)}, u32[]{:S(2)}) collective-permute-start(bf16[1024,256]{1,0:T(8,128)(2,1)S(1)} %shard_map.118), channel_id=1, source_target_pairs={{0,4},{1,5},{2,6},{3,7},{4,8},{5,9},{6,10},{7,11},{8,12},{9,13},{1... | collective-permute-start | bytes 1572872 | tf_op jit(solution)/shard_map/ppermute | solution.py:272
  108.1 16.3 %collective-permute-start.10 = (bf16[1024,256]{1,0:T(8,128)(2,1)S(1)}, bf16[1024,256]{1,0:T(8,128)(2,1)S(1)}, u32[]{:S(2)}, u32[]{:S(2)}) collective-permute-start(bf16[1024,256]{1,0:T(8,128)(2,1)S(1)} %shard_map.121), channel_id=1, source_target_pairs={{0,28},{1,29},{2,30},{3,31},{4,0},{5,1},{6,2},{7,3},{8,4},{9,5},{1... | collective-permute-start | bytes 1572872 | tf_op jit(solution)/shard_map/ppermute | solution.py:272
  117.8 16.6 %collective-permute-start.7 = (bf16[1024,256]{1,0:T(8,128)(2,1)S(1)}, bf16[1024,256]{1,0:T(8,128)(2,1)}, u32[]{:S(2)}, u32[]{:S(2)}) collective-permute-start(bf16[1024,256]{1,0:T(8,128)(2,1)S(1)} %shard_map.119), channel_id=1, source_target_pairs={{0,4},{1,5},{2,6},{3,7},{4,8},{5,9},{6,10},{7,11},{8,12},{9,13},{1... | collective-permute-start | bytes 1572872 | tf_op jit(solution)/shard_map/ppermute | solution.py:272
  124.8 17.0 %collective-permute-start.11 = (bf16[1024,256]{1,0:T(8,128)(2,1)S(1)}, bf16[1024,256]{1,0:T(8,128)(2,1)}, u32[]{:S(2)}, u32[]{:S(2)}) collective-permute-start(bf16[1024,256]{1,0:T(8,128)(2,1)S(1)} %shard_map.122), channel_id=1, source_target_pairs={{0,28},{1,29},{2,30},{3,31},{4,0},{5,1},{6,2},{7,3},{8,4},{9,5},{1... | collective-permute-start | bytes 1572872 | tf_op jit(solution)/shard_map/ppermute | solution.py:272
  135.9 9.3 %copy-start.9 = (s32[1,16,4]{1,2,0:T(4,128)S(1)}, s32[1,16,4]{1,2,0:T(4,128)}, u32[]{:S(2)}) copy-start(s32[1,16,4]{1,2,0:T(4,128)} %param.13) | copy-start | bytes 772
  135.9 10.9 %copy-start = (bf16[1,1024,256]{2,1,0:T(8,128)(2,1)S(1)}, bf16[1,1024,256]{2,1,0:T(8,128)(2,1)}, u32[]{:S(2)}) copy-start(bf16[1,1024,256]{2,1,0:T(8,128)(2,1)} %param.14) | copy-start | bytes 1572868
  135.9 10.9 %copy-start.3 = (bf16[256,256]{1,0:T(8,128)(2,1)S(1)}, bf16[256,256]{1,0:T(8,128)(2,1)}, u32[]{:S(2)}) copy-start(bf16[256,256]{1,0:T(8,128)(2,1)} %constant.19.clone.rest_1_.low) | copy-start | bytes 393220
  135.9 13.9 %collective-permute-start.8 = (bf16[1024,256]{1,0:T(8,128)(2,1)S(1)}, bf16[1024,256]{1,0:T(8,128)(2,1)}, u32[]{:S(2)}, u32[]{:S(2)}) collective-permute-start(bf16[1024,256]{1,0:T(8,128)(2,1)S(1)} %shard_map.120), channel_id=1, source_target_pairs={{0,4},{1,5},{2,6},{3,7},{4,8},{5,9},{6,10},{7,11},{8,12},{9,13},{1... | collective-permute-start | bytes 1572872 | tf_op jit(solution)/shard_map/ppermute | solution.py:272
  143.2 12.4 %collective-permute-start.12 = (bf16[1024,256]{1,0:T(8,128)(2,1)S(1)}, bf16[1024,256]{1,0:T(8,128)(2,1)}, u32[]{:S(2)}, u32[]{:S(2)}) collective-permute-start(bf16[1024,256]{1,0:T(8,128)(2,1)S(1)} %shard_map.123), channel_id=1, source_target_pairs={{0,28},{1,29},{2,30},{3,31},{4,0},{5,1},{6,2},{7,3},{8,4},{9,5},{1... | collective-permute-start | bytes 1572872 | tf_op jit(solution)/shard_map/ppermute | solution.py:272
  146.8 0.9 copy-start.4
  147.7 0.9 copy-start.6
  148.6 0.8 copy-start.7
  155.6 9.5 %copy-start.5 = (bf16[256,256]{1,0:T(8,128)(2,1)S(1)}, bf16[256,256]{1,0:T(8,128)(2,1)}, u32[]{:S(2)}) copy-start(bf16[256,256]{1,0:T(8,128)(2,1)} %constant.18.clone.rest_0_.high) | copy-start | bytes 393220
  155.6 9.5 %copy-start.8 = (bf16[64,192]{1,0:T(8,128)(2,1)S(1)}, bf16[64,192]{1,0:T(8,128)(2,1)}, u32[]{:S(2)}) copy-start(bf16[64,192]{1,0:T(8,128)(2,1)} %constant.21.clone.back_table) | copy-start | bytes 73732
  160.7 15.3 %all-to-all-start.4 = ((bf16[16,64,256]{2,1,0:T(8,128)(2,1)}), bf16[16,64,256]{2,1,0:T(8,128)(2,1)S(1)}, u32[]{:S(2)}, u32[]{:S(2)}) async-start(bf16[16,64,256]{2,1,0:T(8,128)(2,1)} %get-tuple-element.31), calls=%async_computation.4 | async-start | bytes 1048576 | tf_op jit(solution)/shard_map/all_to_all | solution.py:369
